TPU v7x, 32 devices: a whole 2x2x4 slice. The times are simulated.
32 devices in a mesh: dp: 8 (over z, x), head: 4 (over y, core).
Axes of the slice: x: 2, y: 2, z: 4, core: 2. Of those that a mesh axis runs over, the one named last changes fastest.
Arguments:
- inputs: bfloat16 [16384, 1024], P(('dp', 'head')), may hold values from -6 to 6
- lengths: int32 [8, 4], P('dp'), may hold values from 1 to 1024, 2048 in all within a row
- attn_gain: bfloat16 [1024], replicated, may hold values from 0.5 to 1.5
- attn_shift: bfloat16 [1024], replicated, may hold values from -3 to 3
- mlp_gain: bfloat16 [1024], replicated, may hold values from 0.5 to 1.5
- mlp_shift: bfloat16 [1024], replicated, may hold values from -3 to 3
- w_qkv: bfloat16 [1024, 3072], replicated, may hold values from -0.1875 to 0.1875
- b_qkv: bfloat16 [3072], replicated, may hold values from -3 to 3
- w_out: bfloat16 [1024, 1024], replicated, may hold values from -1.5 to 1.5
- b_out: bfloat16 [1024], replicated, may hold values from -3 to 3
- w_up: bfloat16 [1024, 4096], replicated, may hold values from -0.1875 to 0.1875
- b_up: bfloat16 [4096], replicated, may hold values from -3 to 3
- w_down: bfloat16 [4096, 1024], replicated, may hold values from -0.09375 to 0.09375
- b_down: bfloat16 [1024], replicated, may hold values from -3 to 3
- cotangent: bfloat16 [16384, 1024], P(('dp', 'head')), may hold values from -6 to 6
Outputs:
- output: bfloat16 [16384, 1024], P(('dp', 'head'))
- grad_inputs: float32 [16384, 1024], P(('dp', 'head'))
- grad_attn_gain: float32 [1024], replicated
- grad_attn_shift: float32 [1024], replicated
- grad_mlp_gain: float32 [1024], replicated
- grad_mlp_shift: float32 [1024], replicated
- grad_w_qkv: float32 [1024, 3072], P('dp', 'head')
- grad_b_qkv: float32 [3072], replicated
- grad_w_out: float32 [1024, 1024], P('dp', 'head')
- grad_b_out: float32 [1024], replicated
- grad_w_up: float32 [1024, 4096], P('dp', 'head')
- grad_b_up: float32 [4096], replicated
- grad_w_down: float32 [4096, 1024], P('dp', 'head')
- grad_b_down: float32 [1024], replicated
Inputs may be any that keep to these rules, and one draw needn't show every extreme that they name: Each row lists the lengths of the 4 sequences packed in order into one group of 2048 tokens; a row sums to 2048 and its longest sequence has 1024 tokens.
All inputs are finite; a program needn't handle non-finite values.
Results may differ from a plain program's by a relative error of at most 0.012.
Values may be sent and summed in bfloat16 or wider, within the bound.
A program may use at most 192 MiB of HBM per device.

v0:
```python
import jax
import jax.numpy as jnp
from jax import lax
from jax.sharding import PartitionSpec as P

HD = 64
ROT = 16


def layer_norm(value, gain, shift):
    center = value - jnp.mean(value, axis=-1, keepdims=True)
    scale_inv = lax.rsqrt(jnp.mean(center * center, axis=-1, keepdims=True) + 1e-05)
    normed = center * scale_inv
    return (normed * gain + shift, normed, scale_inv)


def norm_back(grad_norm, normed, scale_inv, gain):
    grad_hat = grad_norm * gain
    grad_value = scale_inv * (
        grad_hat
        - jnp.mean(grad_hat, axis=-1, keepdims=True)
        - normed * jnp.mean(grad_hat * normed, axis=-1, keepdims=True)
    )
    return (grad_value, jnp.sum(grad_norm * normed, axis=0), jnp.sum(grad_norm, axis=0))


def group_layout(seq_lens, total_len):
    seq_ends = jnp.cumsum(seq_lens, dtype=jnp.int32)
    starts = seq_ends - seq_lens
    index = jnp.arange(total_len, dtype=jnp.int32)
    segment = jnp.sum(
        (index[:, None] >= seq_ends[None, :]).astype(jnp.int32), axis=1, dtype=jnp.int32
    )
    chosen = segment[:, None] == jnp.arange(seq_lens.shape[0], dtype=jnp.int32)[None, :]
    offset = jnp.sum(jnp.where(chosen, starts[None, :], 0), axis=1, dtype=jnp.int32)
    return (segment, index - offset)


def rotate(value, position, sign):
    half_rot = ROT // 2
    freqs = 10000.0 ** (-(2.0 * jnp.arange(half_rot, dtype=jnp.float32)) / ROT)
    angles = position.astype(jnp.float32)[:, None] * freqs[None, :]
    cosine = jnp.cos(angles)[:, None, :]
    sine = jnp.sin(angles)[:, None, :]
    first = value[..., :half_rot]
    second = value[..., half_rot:ROT]
    return jnp.concatenate(
        [
            first * cosine - sign * second * sine,
            second * cosine + sign * first * sine,
            value[..., ROT:],
        ],
        axis=-1,
    )


def block_scores(queries, keys_rot, segment, start, block):
    query_blk = lax.dynamic_slice_in_dim(queries, start, block, 0)
    row_seg = lax.dynamic_slice_in_dim(segment, start, block, 0)
    row_index = start + jnp.arange(block, dtype=jnp.int32)
    key_index = jnp.arange(keys_rot.shape[0], dtype=jnp.int32)
    scores = jnp.einsum(
        "qhd,khd->hqk", query_blk, keys_rot, preferred_element_type=jnp.float32
    ) * HD ** (-0.5)
    allowed = (row_seg[:, None] == segment[None, :]) & (key_index[None, :] <= row_index[:, None])
    return (jnp.where(allowed[None], scores, -1e30), query_blk)


def body(
    inputs,
    lengths,
    attn_gain,
    attn_shift,
    mlp_gain,
    mlp_shift,
    w_qkv,
    b_qkv,
    w_out,
    b_out,
    w_up,
    b_up,
    w_down,
    b_down,
    cotangent,
):
    tok_rows = inputs.shape[0]
    width = inputs.shape[1]
    in_float = inputs.astype(jnp.float32)
    gain_attn = attn_gain.astype(jnp.float32)
    gain_mlp = mlp_gain.astype(jnp.float32)
    norm_attn, normed_attn, inv_attn = layer_norm(
        in_float, gain_attn, attn_shift.astype(jnp.float32)
    )
    norm_mlp, normed_mlp, inv_mlp = layer_norm(in_float, gain_mlp, mlp_shift.astype(jnp.float32))
    norm_attn = norm_attn.astype(jnp.bfloat16)
    norm_mlp = norm_mlp.astype(jnp.bfloat16)
    triple = (
        jnp.dot(norm_attn, w_qkv, preferred_element_type=jnp.float32) + b_qkv.astype(jnp.float32)
    ).astype(jnp.bfloat16)
    triple_heads = lax.all_to_all(
        triple.reshape(tok_rows, 3, width), "head", split_axis=2, concat_axis=0, tiled=True
    )
    group_rows = triple_heads.shape[0]
    local_width = triple_heads.shape[2]
    local_heads = local_width // HD
    segment, position = group_layout(lengths[0], group_rows)
    queries = rotate(
        triple_heads[:, 0].astype(jnp.float32).reshape(group_rows, local_heads, HD), position, 1.0
    ).astype(jnp.bfloat16)
    keys_rot = rotate(
        triple_heads[:, 1].astype(jnp.float32).reshape(group_rows, local_heads, HD), position, 1.0
    ).astype(jnp.bfloat16)
    values = triple_heads[:, 2].reshape(group_rows, local_heads, HD)
    block = min(512, group_rows)
    blocks = group_rows // block

    def forward_block(block_id):
        scores, unused = block_scores(queries, keys_rot, segment, block_id * block, block)
        peak = jnp.max(scores, axis=-1, keepdims=True)
        weights = jnp.exp(scores - peak)
        totals = jnp.sum(weights, axis=-1, keepdims=True)
        probs = (weights / totals).astype(jnp.bfloat16)
        out_blk = jnp.einsum("hqk,khd->qhd", probs, values, preferred_element_type=jnp.float32)
        return (out_blk.astype(jnp.bfloat16), (peak + jnp.log(totals))[..., 0])

    context_blocks, log_totals = lax.map(forward_block, jnp.arange(blocks, dtype=jnp.int32))
    context_heads = context_blocks.reshape(group_rows, local_width)
    context = lax.all_to_all(context_heads, "head", split_axis=0, concat_axis=1, tiled=True)
    attn_part = jnp.dot(context, w_out, preferred_element_type=jnp.float32) + b_out.astype(
        jnp.float32
    )
    pre_act = jnp.dot(norm_mlp, w_up, preferred_element_type=jnp.float32) + b_up.astype(jnp.float32)
    gelu_value, gelu_pull = jax.vjp(lambda value: jax.nn.gelu(value, approximate=False), pre_act)
    hidden = gelu_value.astype(jnp.bfloat16)
    mlp_part = jnp.dot(hidden, w_down, preferred_element_type=jnp.float32) + b_down.astype(
        jnp.float32
    )
    output = (in_float + attn_part + mlp_part).astype(jnp.bfloat16)
    grad_float = cotangent.astype(jnp.float32)
    grad_w_down = jnp.einsum("tf,td->fd", hidden, cotangent, preferred_element_type=jnp.float32)
    grad_hidden = jnp.einsum("td,fd->tf", cotangent, w_down, preferred_element_type=jnp.float32)
    grad_pre = gelu_pull(grad_hidden)[0].astype(jnp.bfloat16)
    grad_w_up = jnp.einsum("td,tf->df", norm_mlp, grad_pre, preferred_element_type=jnp.float32)
    grad_norm_mlp = jnp.einsum("tf,df->td", grad_pre, w_up, preferred_element_type=jnp.float32)
    grad_w_out = jnp.einsum("td,te->de", context, cotangent, preferred_element_type=jnp.float32)
    grad_context = jnp.einsum(
        "te,de->td", cotangent, w_out, preferred_element_type=jnp.float32
    ).astype(jnp.bfloat16)
    grad_ctx_heads = lax.all_to_all(grad_context, "head", split_axis=1, concat_axis=0, tiled=True)
    grad_ctx_heads = grad_ctx_heads.reshape(group_rows, local_heads, HD)
    scale = HD ** (-0.5)

    def backward_block(carry, block_id):
        grad_keys, grad_values = carry
        start = block_id * block
        scores, query_blk = block_scores(queries, keys_rot, segment, start, block)
        probs = jnp.exp(scores - log_totals[block_id][:, :, None])
        probs_low = probs.astype(jnp.bfloat16)
        grad_out_blk = lax.dynamic_slice_in_dim(grad_ctx_heads, start, block, 0)
        grad_values = grad_values + jnp.einsum(
            "hqk,qhd->khd", probs_low, grad_out_blk, preferred_element_type=jnp.float32
        )
        grad_probs = jnp.einsum(
            "qhd,khd->hqk", grad_out_blk, values, preferred_element_type=jnp.float32
        )
        inner = jnp.sum(probs * grad_probs, axis=-1, keepdims=True)
        grad_scores = (probs * (grad_probs - inner)).astype(jnp.bfloat16)
        grad_query = (
            jnp.einsum("hqk,khd->qhd", grad_scores, keys_rot, preferred_element_type=jnp.float32)
            * scale
        )
        grad_keys = (
            grad_keys
            + jnp.einsum("hqk,qhd->khd", grad_scores, query_blk, preferred_element_type=jnp.float32)
            * scale
        )
        return ((grad_keys, grad_values), grad_query)

    zeros_kv = jnp.zeros((group_rows, local_heads, HD), jnp.float32)
    (grad_keys, grad_values), grad_queries = lax.scan(
        backward_block, (zeros_kv, zeros_kv), jnp.arange(blocks, dtype=jnp.int32)
    )
    grad_queries = rotate(grad_queries.reshape(group_rows, local_heads, HD), position, -1.0)
    grad_keys = rotate(grad_keys, position, -1.0)
    grad_heads = (
        jnp.stack([grad_queries, grad_keys, grad_values], axis=1)
        .reshape(group_rows, 3, local_width)
        .astype(jnp.bfloat16)
    )
    grad_triple = lax.all_to_all(
        grad_heads, "head", split_axis=0, concat_axis=2, tiled=True
    ).reshape(tok_rows, 3 * width)
    grad_w_qkv = jnp.einsum("td,te->de", norm_attn, grad_triple, preferred_element_type=jnp.float32)
    grad_norm_attn = jnp.einsum("te,de->td", grad_triple, w_qkv, preferred_element_type=jnp.float32)
    grad_x_attn, grad_gain_attn, grad_shift_attn = norm_back(
        grad_norm_attn, normed_attn, inv_attn, gain_attn
    )
    grad_x_mlp, grad_gain_mlp, grad_shift_mlp = norm_back(
        grad_norm_mlp, normed_mlp, inv_mlp, gain_mlp
    )
    grad_inputs = grad_float + grad_x_attn + grad_x_mlp
    column_sum = jnp.sum(grad_float, axis=0)
    summed = lax.psum(
        (
            grad_gain_attn,
            grad_shift_attn,
            grad_gain_mlp,
            grad_shift_mlp,
            jnp.sum(grad_triple.astype(jnp.float32), axis=0),
            column_sum,
            jnp.sum(grad_pre.astype(jnp.float32), axis=0),
        ),
        ("dp", "head"),
    )
    matrices = (grad_w_qkv, grad_w_out, grad_w_up, grad_w_down)
    partial_rows = (
        lax.psum_scatter(matrices[0], "dp", scatter_dimension=0, tiled=True),
        lax.psum_scatter(matrices[1], "dp", scatter_dimension=0, tiled=True),
        lax.psum_scatter(matrices[2], "dp", scatter_dimension=0, tiled=True),
        lax.psum_scatter(matrices[3], "dp", scatter_dimension=0, tiled=True),
    )
    finals = (
        lax.psum_scatter(partial_rows[0], "head", scatter_dimension=1, tiled=True),
        lax.psum_scatter(partial_rows[1], "head", scatter_dimension=1, tiled=True),
        lax.psum_scatter(partial_rows[2], "head", scatter_dimension=1, tiled=True),
        lax.psum_scatter(partial_rows[3], "head", scatter_dimension=1, tiled=True),
    )
    return (
        output,
        grad_inputs,
        summed[0],
        summed[1],
        summed[2],
        summed[3],
        finals[0],
        summed[4],
        finals[1],
        summed[5],
        finals[2],
        summed[6],
        finals[3],
        summed[5],
    )


def solution(mesh):
    return jax.shard_map(
        body,
        mesh=mesh,
        in_specs=(
            P(("dp", "head"), None),
            P("dp", None),
            P(),
            P(),
            P(),
            P(),
            P(),
            P(),
            P(),
            P(),
            P(),
            P(),
            P(),
            P(),
            P(("dp", "head"), None),
        ),
        out_specs=(
            P(("dp", "head"), None),
            P(("dp", "head"), None),
            P(),
            P(),
            P(),
            P(),
            P("dp", "head"),
            P(),
            P("dp", "head"),
            P(),
            P("dp", "head"),
            P(),
            P("dp", "head"),
            P(),
        ),
        check_vma=False,
    )
```

profile of v0, /device:TPU:7, one launch (start us, length us, event | category | flops | bytes accessed | tf_op | source)
XLA Modules:
  0.0 1506.3 jit_solution(16333594497788970276)
XLA Ops:
  12.6 8.4 add_convert_fusion.1
  25.6 6.6 copy.84
  41.7 42.6 %all-to-all-done = bf16[512,3,1024]{0,1,2:T(4,128)(2,1)} async-done(((bf16[512,3,1024]{0,1,2:T(4,128)(2,1)}), bf16[512,3,1024]{0,1,2:T(4,128)(2,1)}, u32[]{:S(2)}, u32[]{:S(2)}) %all-to-all-start) | async-done | bytes 3145760 | tf_op jit(solution)/shard_map/all_to_all | solution.py:100
  84.3 6.3 all-to-all-start.2
  117.6 69.1 %while.27 = (s32[]{:T(128)}, bf16[4,512,4,64]{1,3,2,0:T(8,128)(2,1)}, f32[4,4,512]{2,1,0:T(4,128)S(1)}, s32[4]{0:T(128)S(1)}, s32[2048]{0:T(1024)S(1)}, /*index=...) while((s32[]{:T(128)}, ...), condition=%wide.region_8.9_spmd, body=%wide.region_5.0_spmd.sunk | while | flops 1127348736 | bytes 61426396 | solution.py:126
  196.4 7.3 all-to-all-done.1
  208.5 306.1 %while.28 = (s32[]{:T(128)}, f32[2048,4,64]{0,2,1:T(8,128)}, f32[2048,4,64]{0,2,1:T(8,128)}, f32[4,512,4,64]{1,0,3,2:T(4,128)}, s32[4]{0:T(128)S(1)}, /*index=5*...) while((s32[]{:T(128)}, f32[2048,4,64]{0,2,1:T(8,128)}, ...), condition=%wide.region_11.12_spmd.clone, body=%wide.region_9.11_spmd.clone.sunk | while | flops 2753165824 | bytes 187246960 | solution.py:180
  212.5 9.3 fusion.146
  223.7 14.8 multiply_reduce_fusion.4
  238.5 12.4 multiply_convert_fusion.3
  255.4 11.1 dynamic_update_slice.20
  266.5 6.6 fusion.148
  273.1 12.0 fusion.149
  288.6 9.0 fusion.146
  299.7 14.8 multiply_reduce_fusion.4
  314.4 12.1 multiply_convert_fusion.3
  331.1 11.1 dynamic_update_slice.20
  342.2 7.1 fusion.148
  349.2 12.4 fusion.149
  365.1 9.0 fusion.146
  376.1 14.8 multiply_reduce_fusion.4
  390.9 12.1 multiply_convert_fusion.3
  407.5 11.1 dynamic_update_slice.20
  418.6 7.1 fusion.148
  425.7 12.4 fusion.149
  441.5 9.0 fusion.146
  452.5 14.8 multiply_reduce_fusion.4
  467.3 12.1 multiply_convert_fusion.3
  484.0 11.1 dynamic_update_slice.20
  495.1 7.1 fusion.148
  502.1 12.4 fusion.149
  526.6 7.2 copy.93
  533.8 51.8 %all_to_all.68 = bf16[2048,3,256]{2,1,0:T(4,128)(2,1)S(1)} all-to-all(bf16[2048,3,256]{2,1,0:T(4,128)(2,1)} %copy.93), channel_id=1, replica_groups=mesh['dp'=8,'head'=4] {'head'}, dimensions={0} | all-to-all | bytes 6291456 | tf_op jit(solution)/shard_map/all_to_all | solution.py:190
  593.4 8.7 fusion.75
  602.9 7.2 fusion.73
  610.1 28.7 %convert_reduce_fusion = (f32[4096]{0:T(1024)S(1)}, bf16[512,4096]{1,0:T(8,128)(2,1)}, f32[512,4096]{1,0:T(8,128)}) fusion(f32[512,4096]{1,0:T(8,128)S(1)} %fusion.73, f32[4096]{0:T(1024)S(1)} %convert_element_type.119, bf16[512,1024]{1,0:T(8,128)(2,1)S(1)} %copy-done.10, bf16[4096,1024]{1,0:T(8,128)(2,1)} %param.31), kind=kOutput, calls=%fused_computation.49 | convolution fusion | flops 4452249600 | bytes 30441472 | tf_op jit(solution)/shard_map/td,fd->tf/dot_general | solution.py:141
  638.8 10.0 multiply_convert_fusion.1
  648.8 10.8 fusion.83
  659.7 10.5 fusion.71
  670.8 140.2 %reduce-scatter.9.cloned.1.call-done = f32[128,3072]{1,0:T(8,128)} async-done(((f32[1024,3072]{1,0:T(8,128)}), f32[128,3072]{1,0:T(8,128)}) %reduce-scatter.9.cloned.1.call-update) | async-done | bytes 1572880 | tf_op jit(solution)/shard_map/reduce_scatter | solution.py:217
  811.1 282.4 %reduce-scatter.21.cloned.1.call-done = f32[512,1024]{1,0:T(8,128)} async-done(((f32[4096,1024]{1,0:T(8,128)}), f32[512,1024]{1,0:T(8,128)}) %reduce-scatter.21.cloned.1.call-update) | async-done | bytes 2097168 | tf_op jit(solution)/shard_map/reduce_scatter | solution.py:220
  1093.5 10.5 fusion.81
  1104.0 271.7 %reduce-scatter.17.cloned.1.call-done = f32[128,4096]{1,0:T(8,128)} async-done(((f32[1024,4096]{1,0:T(8,128)}), f32[128,4096]{1,0:T(8,128)}) %reduce-scatter.17.cloned.1.call-update) | async-done | bytes 2097168 | tf_op jit(solution)/shard_map/reduce_scatter | solution.py:219
  1375.8 8.4 fusion.80
  1388.1 7.0 fusion.65
  1397.6 39.9 %all-reduce = (f32[1024]{0:T(1024)}, f32[1024]{0:T(1024)}, f32[1024]{0:T(1024)}, f32[1024]{0:T(1024)}, f32[3072]{0:T(1024)}, /*index=5*/f32[1024]{0:T(1024)S(1)}, f32[4096]{0:T(1024)}) all-reduce(f32[1024]{0:T(1024)S(1)} %get-tuple-element.189, f32[1024]{0:T(1024)S(1)} %get-tuple-element.194, ...), channel_id=1, replica_groups=mesh['dp'=8,'head'=4] {'dp','head'}, use_global_device_ids=true, to_apply=%region_17.18 | all-reduce | flops 12288 | bytes 98304 | tf_op jit(solution)/shard_map/psum | solution.py:203
  1437.4 26.7 %reduce-scatter.23.cloned.1.call-done = f32[512,256]{1,0:T(8,128)} async-done(((f32[512,1024]{1,0:T(8,128)}), f32[512,256]{1,0:T(8,128)}) %reduce-scatter.23.cloned.1.call-update) | async-done | bytes 524304 | tf_op jit(solution)/shard_map/reduce_scatter | solution.py:226
  1464.1 34.3 %reduce-scatter.19.cloned.1.call-done = f32[128,1024]{1,0:T(8,128)} async-done(((f32[128,4096]{1,0:T(8,128)}), f32[128,1024]{1,0:T(8,128)}) %reduce-scatter.19.cloned.1.call-update) | async-done | bytes 524304 | tf_op jit(solution)/shard_map/reduce_scatter | solution.py:225
  (232 shorter events, 185.0 us)
Async XLA Ops:
  7.2 30.9 %copy-start = (bf16[1024,1024]{1,0:T(8,128)(2,1)S(1)}, bf16[1024,1024]{1,0:T(8,128)(2,1)}, u32[]{:S(2)}) copy-start(bf16[1024,1024]{1,0:T(8,128)(2,1)} %param.27) | copy-start | bytes 6291460
  8.8 3.7 copy-start.16
  32.1 5.7 copy-start.31
  32.1 5.9 copy-start.9
  32.1 52.1 %all-to-all-start = ((bf16[512,3,1024]{0,1,2:T(4,128)(2,1)}), bf16[512,3,1024]{0,1,2:T(4,128)(2,1)}, u32[]{:S(2)}, u32[]{:S(2)}) async-start(bf16[512,3,1024]{0,1,2:T(4,128)(2,1)} %copy.84), calls=%async_computation | async-start | bytes 8388608 | tf_op jit(solution)/shard_map/all_to_all | solution.py:100
  41.7 72.1 %copy-start.12 = (f32[2048,8]{0,1:T(8,128)}, f32[2048,8]{0,1:T(8,128)S(1)}, u32[]{:S(2)}) copy-start(f32[2048,8]{0,1:T(8,128)S(1)} %get-tuple-element.272) | copy-start | bytes 196612
  84.3 102.5 %all-to-all-start.2 = ((bf16[512,4,256]{2,0,1:T(8,128)(2,1)}), bf16[512,4,256]{2,0,1:T(8,128)(2,1)}, u32[]{:S(2)}, u32[]{:S(2)}) async-start(bf16[512,4,256]{2,0,1:T(8,128)(2,1)} %bitcast.89), calls=%async_computation.2 | async-start | bytes 2097152 | tf_op jit(solution)/shard_map/all_to_all | solution.py:149
  124.6 4.4 copy-start.4
  141.9 4.4 copy-start.4
  159.2 4.4 copy-start.4
  176.4 4.4 copy-start.4
  186.8 16.9 %all-to-all-start.1 = ((bf16[4,512,256]{1,2,0:T(8,128)(2,1)}), bf16[4,512,256]{1,2,0:T(8,128)(2,1)}, u32[]{:S(2)}, u32[]{:S(2)}) async-start(bf16[4,512,256]{1,2,0:T(8,128)(2,1)} %bitcast.15), calls=%async_computation.1 | async-start | bytes 2097152 | tf_op jit(solution)/shard_map/all_to_all | solution.py:128
  191.0 479.2 %reduce-scatter.13.cloned.1.call-start = ((), (), s32[]{:S(2)}) async-start(), calls=%async_computation.14 | async-start | bytes 4718592 | tf_op jit(solution)/shard_map/reduce_scatter | solution.py:218
  208.4 602.6 %reduce-scatter.9.cloned.1.call-start = ((), (), s32[]{:S(2)}) async-start(), calls=%async_computation.12 | async-start | bytes 14155776 | tf_op jit(solution)/shard_map/reduce_scatter | solution.py:217
  223.7 14.8 copy-start.2
  250.9 3.2 copy-start.1
  266.5 6.6 copy-start.3
  299.6 14.8 copy-start.2
  342.2 7.1 copy-start.3
  376.1 14.8 copy-start.2
  402.9 3.2 copy-start.1
  418.6 7.1 copy-start.3
  452.5 14.8 copy-start.2
  479.4 3.2 copy-start.1
  495.1 7.1 copy-start.3
  518.3 4.8 copy-start.13
  518.3 4.8 copy-start.14
  588.6 4.8 copy-start.5
  588.6 4.8 copy-start.17
  588.6 4.8 copy-start.19
  588.6 4.8 copy-start.22
  588.6 4.8 copy-start.25
  602.2 491.3 %reduce-scatter.21.cloned.1.call-start = ((), (), s32[]{:S(2)}) async-start(), calls=%async_computation.18 | async-start | bytes 18874368 | tf_op jit(solution)/shard_map/reduce_scatter | solution.py:220
  602.9 7.2 copy-start.10
  610.1 28.7 %copy-start.6 = (f32[512,4096]{1,0:T(8,128)}, f32[512,4096]{1,0:T(8,128)S(1)}, u32[]{:S(2)}) copy-start(f32[512,4096]{1,0:T(8,128)S(1)} %fusion.73) | copy-start | bytes 25165828
  659.6 716.1 %reduce-scatter.17.cloned.1.call-start = ((), (), s32[]{:S(2)}) async-start(), calls=%async_computation.16 | async-start | bytes 18874368 | tf_op jit(solution)/shard_map/reduce_scatter | solution.py:219
  670.1 423.4 %copy-start.29 = (bf16[1024]{0:T(1024)(128)(2,1)S(1)}, bf16[1024]{0:T(1024)(128)(2,1)}, u32[]{:S(2)}) copy-start(bf16[1024]{0:T(1024)(128)(2,1)} %param.28) | copy-start | bytes 6148
  670.2 423.4 %copy-start.30 = (bf16[1024]{0:T(1024)(128)(2,1)S(1)}, bf16[1024]{0:T(1024)(128)(2,1)}, u32[]{:S(2)}) copy-start(bf16[1024]{0:T(1024)(128)(2,1)} %param.32) | copy-start | bytes 6148
  670.2 767.3 %reduce-scatter.15.cloned.1.call-start = ((), (), s32[]{:S(2)}) async-start(), calls=%async_computation.15 | async-start | bytes 655360 | tf_op jit(solution)/shard_map/reduce_scatter | solution.py:224
  670.8 766.7 %reduce-scatter.11.cloned.1.call-start = ((), (), s32[]{:S(2)}) async-start(), calls=%async_computation.13 | async-start | bytes 1966080 | tf_op jit(solution)/shard_map/reduce_scatter | solution.py:223
  811.0 653.1 %reduce-scatter.23.cloned.1.call-start = ((), (), s32[]{:S(2)}) async-start(), calls=%async_computation.19 | async-start | bytes 2621440 | tf_op jit(solution)/shard_map/reduce_scatter | solution.py:226
  1093.5 404.9 %reduce-scatter.19.cloned.1.call-start = ((), (), s32[]{:S(2)}) async-start(), calls=%async_computation.17 | async-start | bytes 2621440 | tf_op jit(solution)/shard_map/reduce_scatter | solution.py:225
  1384.2 3.8 copy-start.15
  1384.2 3.8 copy-start.7
  1384.2 3.8 copy-start.8
  1384.2 3.8 copy-start.20
  1388.1 7.1 copy-start.11
  1437.4 61.6 %copy-start.26 = (f32[1024]{0:T(1024)}, f32[1024]{0:T(1024)S(1)}, u32[]{:S(2)}) copy-start(f32[1024]{0:T(1024)S(1)} %get-tuple-element.511) | copy-start | bytes 12292
  (7 other events, 9.5 us)
Sparse Core Ops, SparseCore 0:
  208.6 89.2 reduce-scatter.12
  602.3 208.6 reduce-scatter.8
  814.8 278.5 reduce-scatter.20
  1097.1 278.6 reduce-scatter.16
  1378.7 19.9 reduce-scatter.14
  1401.6 28.1 reduce-scatter.10
  1432.9 31.1 reduce-scatter.22
  1467.2 31.1 reduce-scatter.18
where the time goes:
time: 1520 us; the launch traced here: 1510 us
  waiting for transfers between devices  806 us (53%)
  matrix products  334 us (22%)
  local copies, waits for them, and re-layouts  115 us (8%)
  other arithmetic  114 us (8%)
  blocking collectives  91.6 us (6%)
  starting transfers between devices  16.6 us (1%)
    reduce_scatter x1, waiting for transfers between devices, body(): lax.psum_scatter(matrices[3], 'dp', scatter_dimension=0, tiled=True)  282 us
    reduce_scatter x1, waiting for transfers between devices, body(): lax.psum_scatter(matrices[2], 'dp', scatter_dimension=0, tiled=True)  272 us
    reduce_scatter x1, waiting for transfers between devices, body(): lax.psum_scatter(matrices[0], 'dp', scatter_dimension=0, tiled=True)  140 us
    dot_general x4, matrix products, backward_block(): jnp.einsum('qhd,khd->hqk', grad_out_blk, values, preferred_element_type=j...  59.1 us
    dot_general x8, matrix products, block_scores(): jnp.einsum('qhd,khd->hqk', query_blk, keys_rot, preferred_element_type=jn...  54.1 us
    all_to_all x1, blocking collectives, body(): lax.all_to_all(grad_heads, 'head', split_axis=0, concat_axis=2, tiled=True)  51.8 us
    dynamic_update_slice x8, local copies, waits for them, and re-layouts, body(): lax.scan(backward_block, (zeros_kv, zeros_kv), jnp.arange(blocks, dtype=j...  49.7 us
    dot_general x4, matrix products, backward_block(): jnp.einsum('hqk,qhd->khd', probs_low, grad_out_blk, preferred_element_typ...  49.1 us
  transfers between devices with their start and end apart: 11, of which 7 were waited for; matrix products, arithmetic and copies ran while one was open for 35% of the time, Pallas kernels for 0%

commit v1 on v0

v1 whole, which is shorter than its diff:
```python
import functools

import jax
import jax.numpy as jnp
from jax import lax
from jax.experimental import pallas as pl
from jax.experimental.pallas import tpu as pltpu
from jax.sharding import PartitionSpec as P

HD = 64
ROT = 16
HALF = ROT // 2
NN = (((1,), (0,)), ((), ()))
NT = (((1,), (1,)), ((), ()))
TN = (((0,), (0,)), ((), ()))
BF = jnp.bfloat16
F32 = jnp.float32
VMEM_LIMIT = 62 * 1024 * 1024


def mm(a, b, dims=NN):
    return lax.dot_general(a, b, dims, preferred_element_type=F32)


def norm_parts(x):
    v = x.astype(F32)
    center = v - jnp.mean(v, axis=-1, keepdims=True)
    inv = lax.rsqrt(jnp.mean(center * center, axis=-1, keepdims=True) + 1e-5)
    return center * inv, inv


def mlp_kernel(prev, final, pos, *refs):
    x_ref, dy_ref, wu, wd, bu, gain, shift = refs[:7]
    refs = refs[7:]
    if prev:
        pwu, pwd, psmall, psmallf = refs[:4]
        refs = refs[4:]
    part_ref, g_ref, out_wu, out_wd, small, smallf = refs[:6]
    if final:
        dwu, dwd = refs[6:8]
    else:
        dwu, dwd = out_wu, out_wd
    step = pl.program_id(0)

    @pl.when(step == 0)
    def _():
        if prev:
            dwu[...] = pwu[...]
            dwd[...] = pwd[...]
            small[...] = psmall[...]
            smallf[...] = psmallf[...]
        else:
            dwu[...] = jnp.zeros_like(dwu)
            dwd[...] = jnp.zeros_like(dwd)
            small[...] = jnp.zeros_like(small)
            smallf[...] = jnp.zeros_like(smallf)

    normed, _unused = norm_parts(x_ref[...])
    scale = gain[...].astype(F32)
    nm = (normed * scale + shift[...].astype(F32)).astype(BF)
    dy = dy_ref[...]
    pre = mm(nm, wu[...]) + bu[...].astype(F32)
    cdf = 0.5 + 0.5 * lax.erf(pre * (0.5**0.5))
    hid = (pre * cdf).astype(BF)
    slope = cdf + pre * (jnp.exp(-0.5 * pre * pre) * 0.3989422804014327)
    gp = (mm(dy, wd[...], NT) * slope).astype(BF)
    part_ref[...] = mm(hid, wd[...]).astype(BF)
    r = mm(gp, wu[...], NT)
    g_ref[...] = (r * scale).astype(BF)
    smallf[0:1, :] += jnp.sum(gp.astype(F32), axis=0, keepdims=True)
    small[0:1, :] += jnp.sum(r * normed, axis=0, keepdims=True)
    small[1:2, :] += jnp.sum(r, axis=0, keepdims=True)
    small[2:3, :] += jnp.sum(dy.astype(F32), axis=0, keepdims=True)
    dwd[...] += mm(hid, dy, TN)
    dwu[...] += mm(nm, gp, TN)

    if final:

        @pl.when(step == pl.num_programs(0) - 1)
        def _():
            out_wu[...] = dwu[...].astype(BF)
            out_wd[...] = dwd[...].astype(BF)


def mlp(pos, x, dy, wu, wd, bu, gain, shift, n, prev=None, final=True, tt=512):
    tok, d = x.shape
    f = wu.shape[1] // n
    row = lambda i, p: (i, 0)
    zero = lambda i, p: (0, 0)
    one = pl.Buffered(1)
    const = lambda shape: pl.BlockSpec(shape, zero, pipeline_mode=one)
    accs = [const((d, f)), const((f, d)), const((8, d)), const((8, f))]
    kind = BF if final else F32
    grid_spec = pltpu.PrefetchScalarGridSpec(
        num_scalar_prefetch=1,
        grid=(tok // tt,),
        in_specs=[
            pl.BlockSpec((tt, d), row),
            pl.BlockSpec((tt, d), row),
            pl.BlockSpec((d, f), lambda i, p: (0, p[0]), pipeline_mode=one),
            pl.BlockSpec((f, d), lambda i, p: (p[0], 0), pipeline_mode=one),
            pl.BlockSpec((1, f), lambda i, p: (0, p[0])),
            const((1, d)),
            const((1, d)),
        ]
        + (accs if prev is not None else []),
        out_specs=[pl.BlockSpec((tt, d), row), pl.BlockSpec((tt, d), row)] + accs,
        scratch_shapes=[pltpu.VMEM((d, f), F32), pltpu.VMEM((f, d), F32)] if final else [],
    )
    return pl.pallas_call(
        functools.partial(mlp_kernel, prev is not None, final),
        grid_spec=grid_spec,
        out_shape=(
            jax.ShapeDtypeStruct((tok, d), BF),
            jax.ShapeDtypeStruct((tok, d), BF),
            jax.ShapeDtypeStruct((d, f), kind),
            jax.ShapeDtypeStruct((f, d), kind),
            jax.ShapeDtypeStruct((8, d), F32),
            jax.ShapeDtypeStruct((8, f), F32),
        ),
        compiler_params=pltpu.CompilerParams(vmem_limit_bytes=VMEM_LIMIT),
        cost_estimate=pl.CostEstimate(
            flops=12 * tok * d * f, bytes_accessed=8 * tok * d + 12 * d * f, transcendentals=2 * tok * f
        ),
        name="mlp",
    )(pos, x, dy, wu, wd, bu, gain, shift, *(prev or ()))


def proj_kernel(nh, prev, pos, *refs):
    x_ref, dy_ref, wq, wk, wv, bq, bk, bv, wo, gain, shift, cos, sin = refs[:13]
    qt, kt, vt, dot, kn, vn, na_ref = refs[13 + (7 if prev else 0) :]
    normed, _unused = norm_parts(x_ref[...])
    na = (normed * gain[...].astype(F32) + shift[...].astype(F32)).astype(BF)
    na_ref[...] = na
    co = cos[...]
    si = sin[...]

    def rotated(t, scale):
        rows = []
        for h in range(nh):
            u = t[h * HD : (h + 1) * HD]
            u1 = u[:HALF]
            u2 = u[HALF:ROT]
            rows += [u1 * co - u2 * si, u2 * co + u1 * si, u[ROT:]]
        out = jnp.concatenate(rows, axis=0).astype(BF)
        return out if scale is None else out * jnp.asarray(scale, BF)

    def triple(w, b):
        return (mm(na, w[...]) + b[...].astype(F32)).astype(BF)

    qt[...] = rotated(triple(wq, bq).astype(F32).T, HD**-0.5)
    keys = rotated(triple(wk, bk).astype(F32).T, None)
    kt[...] = keys
    kn[...] = keys.T
    values = triple(wv, bv)
    vn[...] = values
    vt[...] = values.T
    dot[...] = mm(wo[...], dy_ref[...], NT).astype(BF)


def proj(pos, x, dy, w_qkv, b_qkv, w_out, gain, shift, cos, sin, n, total, first, prev=None, tt=512):
    tok, d = x.shape
    w = d // n
    nh = w // HD
    off = first // tt
    row = lambda i, p: (i, 0)
    zero = lambda i, p: (0, 0)
    one = pl.Buffered(1)
    wspec = lambda k: pl.BlockSpec((d, w), lambda i, p: (0, k * n + p[0]), pipeline_mode=one)
    bspec = lambda k: pl.BlockSpec((1, w), lambda i, p: (0, k * n + p[0]))
    lane = lambda rows: pl.BlockSpec((rows, tt), lambda i, p: (0, off + i))
    nat = lambda cols: pl.BlockSpec((tt, cols), lambda i, p: (off + i, 0))
    shapes = [(w, total)] * 4 + [(total, w)] * 2 + [(total, d)]
    grid_spec = pltpu.PrefetchScalarGridSpec(
        num_scalar_prefetch=1,
        grid=(tok // tt,),
        in_specs=[pl.BlockSpec((tt, d), row), pl.BlockSpec((tt, d), row)]
        + [wspec(0), wspec(1), wspec(2), bspec(0), bspec(1), bspec(2)]
        + [pl.BlockSpec((w, d), lambda i, p: (p[0], 0), pipeline_mode=one)]
        + [pl.BlockSpec((1, d), zero), pl.BlockSpec((1, d), zero), lane(HALF), lane(HALF)]
        + ([pl.BlockSpec(memory_space=pl.ANY)] * 7 if prev is not None else []),
        out_specs=[lane(w)] * 4 + [nat(w)] * 2 + [nat(d)],
    )
    return pl.pallas_call(
        functools.partial(proj_kernel, nh, prev is not None),
        grid_spec=grid_spec,
        out_shape=tuple(jax.ShapeDtypeStruct(s, BF) for s in shapes),
        input_output_aliases={14 + k: k for k in range(7)} if prev is not None else {},
        compiler_params=pltpu.CompilerParams(vmem_limit_bytes=VMEM_LIMIT),
        cost_estimate=pl.CostEstimate(
            flops=8 * tok * d * w, bytes_accessed=6 * tok * d + 12 * tok * w + 8 * d * w, transcendentals=0
        ),
        name="proj",
    )(pos, x, dy, w_qkv, w_qkv, w_qkv, b_qkv, b_qkv, b_qkv, w_out, gain, shift, cos, sin, *(prev or ()))


def attn_kernel(nh, tok, blk, per, lens, rel, cos, sin, seg_start, qt, kt, vt, dot, kn, vn,
                gt_ref, ctx_ref, exps, peaks, dk, dv, oacc, dqacc, mrow, lrow, drow, qpad, dopad):
    nseq = lens.shape[0]
    nblk = tok // blk
    shift = rel[0]

    def place(b):
        return pl.multiple_of(((b // per) ^ shift) * (per * blk) + (b % per) * blk, blk)

    dk[...] = jnp.zeros_like(dk)
    dv[...] = jnp.zeros_like(dv)
    qpad[...] = jnp.zeros_like(qpad)
    dopad[...] = jnp.zeros_like(dopad)
    rows_iota = lax.broadcasted_iota(jnp.int32, (blk, blk), 0)
    cols_iota = lax.broadcasted_iota(jnp.int32, (1, blk), 1)

    def one_block(i, carry):
        first_tok = i * blk
        begin = jnp.int32(0)
        total = jnp.int32(0)
        for s in range(nseq - 1):
            total = total + lens[s]
            begin = jnp.where(total <= first_tok, total, begin)
        low = begin // blk
        cols = pl.ds(place(i), blk)
        start_row = seg_start[:, cols]
        query_idx = cols_iota + first_tok
        for h in range(nh):
            half = (h % 2) * HD
            qpad[h, half : half + HD, :] = qt[h * HD : (h + 1) * HD, cols]
            dopad[h, half : half + HD, :] = dot[h * HD : (h + 1) * HD, cols]
        mrow[...] = jnp.full_like(mrow, -1e30)
        lrow[...] = jnp.zeros_like(lrow)
        oacc[...] = jnp.zeros_like(oacc)
        dqacc[...] = jnp.zeros_like(dqacc)

        def forward(step, c):
            b = i - step
            krow = place(b)
            kidx = rows_iota + b * blk
            allowed = (kidx >= start_row) & (kidx <= query_idx)
            for h in range(nh):
                pair = (h // 2) * 128
                s = mm(kn[pl.ds(krow, blk), pair : pair + 128], qpad[h])
                s = jnp.where(allowed, s, -1e30)
                old = mrow[h : h + 1, :]
                new = jnp.maximum(old, jnp.max(s, axis=0, keepdims=True))
                e = jnp.exp(s - new)
                alpha = jnp.exp(old - new)
                lrow[h : h + 1, :] = lrow[h : h + 1, :] * alpha + jnp.sum(e, axis=0, keepdims=True)
                mrow[h : h + 1, :] = new
                peaks[step, h : h + 1, :] = new
                exps[h, step] = e
                oacc[h] = oacc[h] * alpha + mm(vt[h * HD : (h + 1) * HD, pl.ds(krow, blk)], e.astype(BF))
            return c

        lax.fori_loop(0, i - low + 1, forward, 0)
        for h in range(nh):
            hs = slice(h * HD, (h + 1) * HD)
            inv = 1.0 / lrow[h : h + 1, :]
            o = oacc[h] * inv
            drow[h : h + 1, :] = jnp.sum(o * dot[hs, cols].astype(F32), axis=0, keepdims=True)
            lrow[h : h + 1, :] = inv
            ctx_ref[hs, cols] = o.astype(BF)

        def backward(step, c):
            kcols = pl.ds(place(i - step), blk)
            for h in range(nh):
                pair = (h // 2) * 128
                hs = slice(h * HD, (h + 1) * HD)
                factor = jnp.exp(peaks[step, h : h + 1, :] - mrow[h : h + 1, :]) * lrow[h : h + 1, :]
                p = exps[h, step] * factor
                dp = mm(vn[kcols, pair : pair + 128], dopad[h])
                ds = (p * (dp - drow[h : h + 1, :])).astype(BF)
                dv[hs, kcols] += mm(dot[hs, cols], p.astype(BF), NT)
                dk[hs, kcols] += mm(qt[hs, cols], ds, NT)
                dqacc[hs, :] += mm(kt[hs, kcols], ds)
            return c

        lax.fori_loop(0, i - low + 1, backward, 0)
        co = cos[:, cols]
        si = sin[:, cols]
        for h in range(nh):
            base = h * HD
            g = dqacc[base : base + HD, :] * (HD**-0.5)
            g1 = g[:HALF]
            g2 = g[HALF:ROT]
            gt_ref[base : base + HD, cols] = jnp.concatenate(
                [g1 * co + g2 * si, g2 * co - g1 * si, g[ROT:]], axis=0
            ).astype(BF)
        return carry

    lax.fori_loop(0, nblk, one_block, 0)

    def finish(i, carry):
        cols = pl.ds(pl.multiple_of(i * blk, blk), blk)
        co = cos[:, cols]
        si = sin[:, cols]
        for h in range(nh):
            base = h * HD
            g = dk[base : base + HD, cols]
            g1 = g[:HALF]
            g2 = g[HALF:ROT]
            gt_ref[nh * HD + base : nh * HD + base + HD, cols] = jnp.concatenate(
                [g1 * co + g2 * si, g2 * co - g1 * si, g[ROT:]], axis=0
            ).astype(BF)
        gt_ref[2 * nh * HD :, cols] = dv[:, cols].astype(BF)
        return carry

    lax.fori_loop(0, nblk, finish, 0)


def attention(lens, rel, cos, sin, seg_start, qt, kt, vt, dot, kn, vn, chunk, maxlen, blk=256):
    width, tok = qt.shape
    nh = width // HD
    wb = maxlen // blk + 1
    vm = pl.BlockSpec(memory_space=pltpu.VMEM)
    sm = pl.BlockSpec(memory_space=pltpu.SMEM)
    return pl.pallas_call(
        functools.partial(attn_kernel, nh, tok, blk, chunk // blk),
        out_shape=(jax.ShapeDtypeStruct((3 * width, tok), BF), jax.ShapeDtypeStruct((width, tok), BF)),
        in_specs=[sm, sm] + [vm] * 9,
        out_specs=(vm, vm),
        scratch_shapes=[
            pltpu.VMEM((nh, wb, blk, blk), F32),
            pltpu.VMEM((wb, 8, blk), F32),
            pltpu.VMEM((width, tok), F32),
            pltpu.VMEM((width, tok), F32),
            pltpu.VMEM((nh, HD, blk), F32),
            pltpu.VMEM((width, blk), F32),
            pltpu.VMEM((8, blk), F32),
            pltpu.VMEM((8, blk), F32),
            pltpu.VMEM((8, blk), F32),
            pltpu.VMEM((nh, 128, blk), BF),
            pltpu.VMEM((nh, 128, blk), BF),
        ],
        compiler_params=pltpu.CompilerParams(vmem_limit_bytes=VMEM_LIMIT),
        cost_estimate=pl.CostEstimate(
            flops=20 * width * tok * maxlen, bytes_accessed=20 * width * tok, transcendentals=nh * tok * maxlen
        ),
        name="attention",
    )(lens, rel, cos, sin, seg_start, qt, kt, vt, dot, kn, vn)


def post_kernel(prev, final, pos, *refs):
    gt_ref, na_ref, x_ref, gm_ref, wq, wk, wv, gain = refs[:8]
    refs = refs[8:]
    if prev:
        pw, pb, psmall = refs[:3]
        refs = refs[3:]
    g_ref, out_w, bias, small = refs[:4]
    dw = refs[4] if final else out_w
    step = pl.program_id(0)

    @pl.when(step == 0)
    def _():
        if prev:
            dw[...] = pw[...]
            bias[...] = pb[...]
            small[...] = psmall[...]
        else:
            dw[...] = jnp.zeros_like(dw)
            bias[...] = jnp.zeros_like(bias)
            small[...] = jnp.zeros_like(small)

    gt = gt_ref[...]
    w = wq.shape[1]
    normed, _unused = norm_parts(x_ref[...])
    scale = gain[...].astype(F32)
    gn = gt.T
    r = mm(gn[:, :w], wq[...], NT) + mm(gn[:, w : 2 * w], wk[...], NT) + mm(gn[:, 2 * w :], wv[...], NT)
    g_ref[...] = (r * scale + gm_ref[...].astype(F32)).astype(BF)
    small[0:1, :] += jnp.sum(r * normed, axis=0, keepdims=True)
    small[1:2, :] += jnp.sum(r, axis=0, keepdims=True)
    bias[0:1, :] += jnp.sum(gn.astype(F32), axis=0, keepdims=True)
    dw[...] += mm(gt, na_ref[...])

    if final:

        @pl.when(step == pl.num_programs(0) - 1)
        def _():
            for b in range(dw.shape[1] // 128):
                out_w[b] = dw[:, b * 128 : (b + 1) * 128].astype(BF)


def post(pos, gt, na, x, gm, w_qkv, gain, n, first, prev=None, final=True, tt=512):
    tok, d = x.shape
    w = d // n
    off = first // tt
    row = lambda i, p: (i, 0)
    zero = lambda i, p: (0, 0)
    one = pl.Buffered(1)
    const = lambda shape: pl.BlockSpec(shape, zero, pipeline_mode=one)
    wspec = lambda k: pl.BlockSpec((d, w), lambda i, p: (0, k * n + p[0]), pipeline_mode=one)
    tail = [const((8, 3 * w)), const((8, d))]
    wout = pl.BlockSpec((d // 128, 3 * w, 128), lambda i, p: (0, 0, 0), pipeline_mode=one) if final else const((3 * w, d))
    grid_spec = pltpu.PrefetchScalarGridSpec(
        num_scalar_prefetch=1,
        grid=(tok // tt,),
        in_specs=[
            pl.BlockSpec((3 * w, tt), lambda i, p: (0, off + i)),
            pl.BlockSpec((tt, d), lambda i, p: (off + i, 0)),
            pl.BlockSpec((tt, d), row),
            pl.BlockSpec((tt, d), row),
            wspec(0),
            wspec(1),
            wspec(2),
            const((1, d)),
        ]
        + ([const((3 * w, d))] + tail if prev is not None else []),
        out_specs=[pl.BlockSpec((tt, d), row), wout] + tail,
        scratch_shapes=[pltpu.VMEM((3 * w, d), F32)] if final else [],
    )
    return pl.pallas_call(
        functools.partial(post_kernel, prev is not None, final),
        grid_spec=grid_spec,
        out_shape=(
            jax.ShapeDtypeStruct((tok, d), BF),
            jax.ShapeDtypeStruct((d // 128, 3 * w, 128), BF) if final else jax.ShapeDtypeStruct((3 * w, d), F32),
            jax.ShapeDtypeStruct((8, 3 * w), F32),
            jax.ShapeDtypeStruct((8, d), F32),
        ),
        compiler_params=pltpu.CompilerParams(vmem_limit_bytes=VMEM_LIMIT),
        cost_estimate=pl.CostEstimate(
            flops=12 * tok * d * w, bytes_accessed=8 * tok * d + 6 * tok * w + 18 * d * w, transcendentals=0
        ),
        name="post",
    )(pos, gt, na, x, gm, w_qkv, w_qkv, w_qkv, gain, *(prev or ()))


def layout(seq_lens, index):
    ends = jnp.cumsum(seq_lens, dtype=jnp.int32)
    starts = ends - seq_lens
    first = jnp.zeros_like(index)
    for s in range(1, seq_lens.shape[0]):
        first = jnp.where(index >= starts[s], starts[s], first)
    return first, index - first


def swap_bits(parts, j):
    low = (j & 1) == 1
    high = (j & 2) == 2
    a, b, c, d = parts
    a, b, c, d = jnp.where(low, b, a), jnp.where(low, a, b), jnp.where(low, d, c), jnp.where(low, c, d)
    return [jnp.where(high, c, a), jnp.where(high, d, b), jnp.where(high, a, c), jnp.where(high, b, d)]


def head_perm(v, bit):
    return lax.ppermute(v, "head", [(k, k ^ bit) for k in range(4)])


def dp_perm(v, bit):
    return lax.ppermute(v, "dp", [(k, k ^ bit) for k in range(8)])


def pick(v, index, axis=0):
    return lax.dynamic_index_in_dim(v, index, axis, keepdims=False)


def dp_scatter(blocks, i):
    x = i & 1
    z = i >> 1
    pairs = blocks.reshape((4, 2) + blocks.shape[1:])
    other = dp_perm(pick(pairs, 1 - x, 1), 1)
    mine = pick(pairs, x, 1).astype(F32) + other.astype(F32)
    low = mine.astype(BF)
    result = pick(mine, z)
    for s in (1, 2, 3):
        result = result + dp_perm(pick(low, z ^ s), 2 * s).astype(F32)
    return result


def sum_all(v):
    for bit in (1, 2):
        v = v + head_perm(v, bit)
    for bit in (1, 2, 4):
        v = v + dp_perm(v, bit)
    return v


def to_owner(v, i, j):
    cols = v.reshape(v.shape[0], 4, v.shape[1] // 4)
    got = []
    for r in range(4):
        pairs = []
        for si in range(8):
            for sj in range(4):
                pairs.append((si * 4 + sj, (2 * sj + si // 4) * 4 + ((si % 4) ^ r)))
        got.append(lax.ppermute(pick(cols, (i % 4) ^ r, 1), ("dp", "head"), pairs))
    return jnp.concatenate(swap_bits(got, j), axis=0)


def qkv_owner(v, j):
    got = []
    for t in range(3):
        pairs = [((3 * dst + t) % 4, dst) for dst in range(4)]
        slot = jnp.int32(0)
        for src, dst in pairs:
            slot = jnp.where(j == src, (3 * dst + t) // 4, slot)
        got.append(lax.ppermute(pick(v, slot), "head", pairs))
    return jnp.concatenate(got, axis=0)


def fast_body(inputs, lengths, attn_gain, attn_shift, mlp_gain, mlp_shift, w_qkv, b_qkv, w_out, b_out,
              w_up, b_up, w_down, b_down, cotangent):
    own, d = inputs.shape
    n = 4
    tok = own * n
    w = d // n
    i = lax.axis_index("dp")
    j = lax.axis_index("head")
    pos = j.astype(jnp.int32).reshape(1)
    rows = lambda v: v.reshape(1, -1)
    ga, sa, gm, sm = rows(attn_gain), rows(attn_shift), rows(mlp_gain), rows(mlp_shift)
    bq, bu = rows(b_qkv), rows(b_up)
    lens = lengths[0]

    x_y = head_perm(inputs, 2)
    x_c = head_perm(inputs, 1)
    dy_c = head_perm(cotangent, 1)
    dy_y = head_perm(cotangent, 2)
    x_a = jnp.concatenate([inputs, x_c], axis=0)
    dy_a = jnp.concatenate([cotangent, dy_c], axis=0)

    lane = jnp.arange(tok, dtype=jnp.int32)
    index = ((lane // own) ^ j) * own + lane % own
    first, position = layout(lens, index)
    freqs = 10000.0 ** (-(2.0 * jnp.arange(HALF, dtype=F32)) / ROT)
    angle = freqs[:, None] * position.astype(F32)[None, :]
    cos, sin = jnp.cos(angle), jnp.sin(angle)
    seg_start = first[None, :]

    part_a, gm_a, *acc_a = mlp(pos, x_a, dy_a, w_up, w_down, bu, gm, sm, n, final=False)
    pre_a = proj(pos, x_a, dy_a, w_qkv, bq, w_out, ga, sa, cos, sin, n, tok, 0)

    x_b = jnp.concatenate([x_y, head_perm(x_y, 1)], axis=0)
    dy_b = jnp.concatenate([dy_y, head_perm(dy_y, 1)], axis=0)
    part_b, gm_b, dwu, dwd, small, smallf = mlp(pos, x_b, dy_b, w_up, w_down, bu, gm, sm, n, prev=tuple(acc_a))
    qt, kt, vt, dot, kn, vn, na = proj(
        pos, x_b, dy_b, w_qkv, bq, w_out, ga, sa, cos, sin, n, tok, 2 * own, prev=tuple(pre_a)
    )

    part_y = part_b[:own].astype(F32) + head_perm(part_b[own:], 1).astype(F32)
    part_0 = part_a[:own].astype(F32) + head_perm(part_a[own:], 1).astype(F32)
    mlp_sum = part_0 + head_perm(part_y.astype(BF), 2).astype(F32)

    up_down = jnp.concatenate([dwu.reshape(8, 128, d), dwd.reshape(8, 128, d)], axis=1)
    up_down = dp_scatter(up_down, i)
    grad_w_up = up_down[:128]
    grad_w_down = to_owner(up_down[128:].astype(BF), i, j).astype(F32)
    slots = jnp.where(jnp.arange(4)[:, None] == j, smallf[0:1], 0.0)
    early = sum_all(jnp.concatenate([small[:2], small[2:3] * 0.25, slots, jnp.zeros((1, d), F32)], axis=0))

    gt, ctx = attention(lens, pos, cos, sin, seg_start, qt, kt, vt, dot, kn, vn, own, tok // 2)

    got = [ctx[:, :own]] + [head_perm(ctx[:, r * own : (r + 1) * own], r) for r in (1, 2, 3)]
    w_rel = w_out.reshape(n, w, d)
    attn_part = mm(jnp.concatenate(got, axis=0), jnp.concatenate([pick(w_rel, j ^ r) for r in range(n)], axis=0), TN)
    bias = b_out.astype(F32) + b_down.astype(F32)
    output = (inputs.astype(F32) + attn_part + mlp_sum + bias).astype(BF)

    dw_out = mm(ctx[:, : 2 * own], dy_a) + mm(ctx[:, 2 * own :], dy_b)

    g_b, dwq, bias_b, small_b = post(pos, gt, na, x_b, gm_b, w_qkv, ga, n, 2 * own, final=False)
    g_y = g_b[:own].astype(F32) + head_perm(g_b[own:], 1).astype(F32)
    g_y = head_perm(g_y.astype(BF), 2)
    g_a, dwq, bias_q, small_q = post(pos, gt, na, x_a, gm_a, w_qkv, ga, n, 0, prev=(dwq, bias_b, small_b))
    g_sum = g_a[:own].astype(F32) + head_perm(g_a[own:], 1).astype(F32) + g_y.astype(F32)

    qkv = dp_scatter(dwq, i)
    grad_w_qkv = qkv_owner(qkv.astype(BF).reshape(3, w, 128), j).astype(F32).T
    out_sum = dp_scatter(dw_out.astype(BF).reshape(8, w // 8, d), i)
    grad_w_out = to_owner(out_sum.astype(BF), i, j).astype(F32)

    slots = jnp.where(jnp.arange(4)[None, :, None] == j, bias_q[0].reshape(3, 1, w), 0.0).reshape(3, d)
    late = sum_all(jnp.concatenate([small_q[:2], slots, jnp.zeros((3, d), F32)], axis=0))

    normed, inv = norm_parts(inputs)
    grad_inputs = cotangent.astype(F32) + inv * (
        g_sum - jnp.mean(g_sum, axis=-1, keepdims=True) - normed * jnp.mean(g_sum * normed, axis=-1, keepdims=True)
    )
    return (output, grad_inputs, late[0], late[1], early[0], early[1], grad_w_qkv, late[2:5].reshape(-1),
            grad_w_out, early[2], grad_w_up, early[3:7].reshape(-1), grad_w_down, early[2])


def general_body(inputs, lengths, attn_gain, attn_shift, mlp_gain, mlp_shift, w_qkv, b_qkv, w_out, b_out,
                 w_up, b_up, w_down, b_down, cotangent):
    own, d = inputs.shape
    n = lax.axis_size("head")
    n_dp = lax.axis_size("dp")
    tok = own * n
    w = d // n
    f = w_up.shape[1] // n
    j = lax.axis_index("head")
    pos = j.astype(jnp.int32).reshape(1)
    rows = lambda v: v.reshape(1, -1)
    ga, sa, gm, sm = rows(attn_gain), rows(attn_shift), rows(mlp_gain), rows(mlp_shift)
    bq, bu = rows(b_qkv), rows(b_up)
    lens = lengths[0]
    gather = lambda v: lax.all_gather(v, "head", axis=0, tiled=True)
    over_dp = lambda v, axis: lax.psum_scatter(v, "dp", scatter_dimension=axis, tiled=True)
    over_head = lambda v: lax.psum_scatter(v, "head", scatter_dimension=0, tiled=True)
    x_all = gather(inputs)
    dy_all = gather(cotangent)
    first, position = layout(lens, jnp.arange(tok, dtype=jnp.int32))
    freqs = 10000.0 ** (-(2.0 * jnp.arange(HALF, dtype=F32)) / ROT)
    angle = freqs[:, None] * position.astype(F32)[None, :]
    cos, sin = jnp.cos(angle), jnp.sin(angle)
    part, g_mlp, dwu, dwd, small, smallf = mlp(pos, x_all, dy_all, w_up, w_down, bu, gm, sm, n)
    qt, kt, vt, dot, kn, vn, na = proj(pos, x_all, dy_all, w_qkv, bq, w_out, ga, sa, cos, sin, n, tok, 0)
    gt, ctx = attention(
        lens, jnp.zeros((1,), jnp.int32), cos, sin, first[None, :], qt, kt, vt, dot, kn, vn, own, tok // 2
    )
    total, dwq, bias_q, small_q = post(pos, gt, na, x_all, g_mlp, w_qkv, ga, n, 0)
    attn_part = mm(ctx, lax.dynamic_slice_in_dim(w_out, j * w, w, 0), TN)
    bias = b_out.astype(F32) + b_down.astype(F32)
    output = inputs.astype(F32) + over_head((attn_part + part.astype(F32)).astype(BF)).astype(F32) + bias
    g_sum = over_head(total).astype(F32)
    normed, inv = norm_parts(inputs)
    grad_inputs = cotangent.astype(F32) + inv * (
        g_sum - jnp.mean(g_sum, axis=-1, keepdims=True) - normed * jnp.mean(g_sum * normed, axis=-1, keepdims=True)
    )
    dw_out = mm(ctx, dy_all).astype(BF)
    spread = lambda v: lax.all_to_all(v, "head", split_axis=1, concat_axis=0, tiled=True)
    grad_w_up = over_dp(dwu, 0).astype(F32)
    grad_w_down = over_dp(spread(dwd), 0).astype(F32)
    grad_w_out = over_dp(spread(dw_out), 0).astype(F32)
    qkv = over_dp(jnp.transpose(dwq, (0, 2, 1)).reshape(d, 3 * w), 0)
    qkv = lax.all_gather(qkv.reshape(d // n_dp, 3, w), "head", axis=2, tiled=True).reshape(d // n_dp, 3 * d)
    grad_w_qkv = lax.dynamic_slice_in_dim(qkv, j * 3 * w, 3 * w, 1).astype(F32)
    slots = jnp.where(jnp.arange(n)[:, None] == j, smallf[0:1], 0.0).reshape(-1)
    slots_q = jnp.where(jnp.arange(n)[None, :, None] == j, bias_q[0].reshape(3, 1, w), 0.0).reshape(-1)
    sums = lax.psum((small_q[0], small_q[1], small[0], small[1], slots_q, small[2] / n, slots), ("dp", "head"))
    return (output.astype(BF), grad_inputs, sums[0], sums[1], sums[2], sums[3], grad_w_qkv, sums[4],
            grad_w_out, sums[5], grad_w_up, sums[6], grad_w_down, sums[5])


def solution(mesh):
    fast = mesh.shape["dp"] == 8 and mesh.shape["head"] == 4
    whole = P(("dp", "head"), None)
    weight = P("dp", "head")
    return jax.shard_map(
        fast_body if fast else general_body,
        mesh=mesh,
        in_specs=(whole, P("dp", None)) + (P(),) * 12 + (whole,),
        out_specs=(whole, whole, P(), P(), P(), P(), weight, P(), weight, P(), weight, P(), weight, P()),
        check_vma=False,
    )
```

time: 1520 us -> 430 us (0.28)
  waiting for transfers between devices: 806 us -> 93.9 us
  matrix products: 334 us -> 10.1 us
  Pallas kernels: 0 us -> 136 us
  blocking collectives: 91.6 us -> 0 us
  starting transfers between devices: 16.6 us -> 105 us
  other arithmetic: 114 us -> 30.8 us
  local copies, waits for them, and re-layouts: 115 us -> 46.1 us
    reduce_scatter x8 -> x0, waiting for transfers between devices: 755 us -> none  [the longest x1 282 us: body(): lax.psum_scatter(matrices[3], 'dp', scatter_dimension=0, tiled=True)]
    dot_general x40 -> x3, matrix products: 334 us -> 10.1 us  [mm(): return lax.dot_general(a, b, dims, preferred_element_type=F32)]
    pallas_call x0 -> x7, Pallas kernels: none -> 136 us  [the longest x1 54.6 us: attention(): pl.pallas_call(functools.partial(attn_kernel, nh, tok, blk, chunk // blk)...]
    ppermute x0 -> x48, starting transfers between devices: none -> 105 us  [the longest x18 56.8 us: dp_perm(): return lax.ppermute(v, 'dp', [(k, k ^ bit) for k in range(8)])]
    ppermute x0 -> x48, waiting for transfers between devices: none -> 93.9 us  [the longest x19 47.2 us: head_perm(): return lax.ppermute(v, 'head', [(k, k ^ bit) for k in range(4)])]
    all_to_all x1 -> x0, blocking collectives: 51.8 us -> none  [body(): lax.all_to_all(grad_heads, 'head', split_axis=0, concat_axis=2, tiled=True)]
    all_to_all x3 -> x0, waiting for transfers between devices: 49.9 us -> none  [the longest x1 42.6 us: body(): lax.all_to_all(triple.reshape(tok_rows, 3, width), 'head', split_axis=2,...]
    dynamic_update_slice x8 -> x0, local copies, waits for them, and re-layouts: 49.7 us -> none  [body(): lax.scan(backward_block, (zeros_kv, zeros_kv), jnp.arange(blocks, dtype=j...]
  transfers between devices with their start and end apart: 11 -> 48, of which waited for: 7 -> 11; matrix products, arithmetic and copies ran while one was open for 35% -> 16% of each run, Pallas kernels for 0% -> 12%
where the time goes in v1:
time: 430 us; the launch traced here: 423 us
  Pallas kernels  136 us (32%)
  starting transfers between devices  105 us (24%)
  waiting for transfers between devices  93.9 us (22%)
  local copies, waits for them, and re-layouts  46.1 us (11%)
  other arithmetic  30.8 us (7%)
  matrix products  10.1 us (2%)
    ppermute x18, starting transfers between devices, dp_perm(): return lax.ppermute(v, 'dp', [(k, k ^ bit) for k in range(8)])  56.8 us
    pallas_call x1, Pallas kernels, attention(): pl.pallas_call(functools.partial(attn_kernel, nh, tok, blk, chunk // blk)...  54.6 us
    ppermute x19, waiting for transfers between devices, head_perm(): return lax.ppermute(v, 'head', [(k, k ^ bit) for k in range(4)])  47.2 us
    pallas_call x2, Pallas kernels, mlp(): pl.pallas_call(functools.partial(mlp_kernel, prev is not None, final), gr...  45.2 us
    ppermute x18, waiting for transfers between devices, dp_perm(): return lax.ppermute(v, 'dp', [(k, k ^ bit) for k in range(8)])  34.6 us
    ppermute x8, starting transfers between devices, to_owner(): got.append(lax.ppermute(pick(cols, i % 4 ^ r, 1), ('dp', 'head'), pairs))  28.3 us
    pallas_call x2, Pallas kernels, post(): pl.pallas_call(functools.partial(post_kernel, prev is not None, final), g...  20.7 us
    ppermute x19, starting transfers between devices, head_perm(): return lax.ppermute(v, 'head', [(k, k ^ bit) for k in range(4)])  15.7 us
  transfers between devices with their start and end apart: 48, of which 11 were waited for; matrix products, arithmetic and copies ran while one was open for 16% of the time, Pallas kernels for 12%

profile of v1, /device:TPU:7, one launch (start us, length us, event | category | flops | bytes accessed | tf_op | source)
XLA Modules:
  0.0 423.5 jit_solution(1547115030329400650)
XLA Ops:
  4.9 2.3 constant_dynamic-update-slice_fusion.7
  16.9 2.6 compare_select_fusion.2.seg_start
  20.4 5.9 %collective-permute-done.2 = bf16[512,1024]{1,0:T(8,128)(2,1)} collective-permute-done((bf16[512,1024]{1,0:T(8,128)(2,1)}, bf16[512,1024]{1,0:T(8,128)(2,1)}, u32[]{:S(2)}, u32[]{:S(2)}) %collective-permute-start.2) | collective-permute-done | bytes 1048608 | tf_op jit(solution)/shard_map/ppermute | solution.py:445
  27.8 21.0 %collective-permute-done = bf16[512,1024]{1,0:T(8,128)(2,1)} collective-permute-done((bf16[512,1024]{1,0:T(8,128)(2,1)}, bf16[512,1024]{1,0:T(8,128)(2,1)}, u32[]{:S(2)}, u32[]{:S(2)}) %collective-permute-start) | collective-permute-done | bytes 1048608 | tf_op jit(solution)/shard_map/ppermute | solution.py:445
  49.8 2.3 constant_dynamic-update-slice_fusion.6.refs_1_
  52.0 2.3 constant_dynamic-update-slice_fusion.4.refs_0_.refs_2_
  54.3 21.5 %mlp.2 = (bf16[1024,1024]{1,0:T(8,128)(2,1)}, bf16[1024,1024]{1,0:T(8,128)(2,1)}, f32[1024,1024]{1,0:T(8,128)}, f32[1024,1024]{1,0:T(8,128)}, f32[8,1024]{1,0:T(8,128)}, /*index=5*/f32[8,1024]{1,0:T(8,128)}) custom-call(s32[1]{0:T(128)} %bitcast.1.pos.rel, bf16[1024,1024]{1,0:T(8,128)(2,1)} %constant_dynamic-update-slice_fusion.4.refs_0_.refs_2_, ...), custom_call_target="tpu_custom_call" | custom-call | flops 12884901888 | bytes 20971520 | tf_op jit(solution)/shard_map/mlp/pallas_call | solution.py:110
  75.8 2.3 slice.106
  80.4 2.3 constant_dynamic-update-slice_fusion.3
  82.7 7.6 %proj.2 = (bf16[256,2048]{1,0:T(8,128)(2,1)}, bf16[256,2048]{1,0:T(8,128)(2,1)}, bf16[256,2048]{1,0:T(8,128)(2,1)}, bf16[256,2048]{1,0:T(8,128)(2,1)}, bf16[2048...) custom-call(s32[1]{0:T(128)} %bitcast.1.pos.rel, ...), custom_call_target="tpu_custom_call" | custom-call | flops 2147483648 | bytes 11534336 | tf_op jit(solution)/shard_map/proj/pallas_call | solution.py:184
  90.3 2.3 constant_dynamic-update-slice_fusion.refs_0_.refs_2_
  92.6 2.3 constant_dynamic-update-slice_fusion.2.refs_1_
  94.9 7.6 %proj.3 = (bf16[256,2048]{1,0:T(8,128)(2,1)}, bf16[256,2048]{1,0:T(8,128)(2,1)}, bf16[256,2048]{1,0:T(8,128)(2,1)}, bf16[256,2048]{1,0:T(8,128)(2,1)}, bf16[2048...) custom-call(s32[1]{0:T(128)} %bitcast.1.pos.rel, ...), custom_call_target="tpu_custom_call", output_to_operand_aliasing={{0}: (14, {}), {1}: (15, {}), {2}: (16, {}), {3}: (17, {}),... | custom-call | flops 2147483648 | bytes 11534336 | tf_op jit(solution)/shard_map/proj/pallas_call | solution.py:184
  102.5 54.6 %attention.1 = (bf16[768,2048]{1,0:T(8,128)(2,1)}, bf16[256,2048]{1,0:T(8,128)(2,1)}) custom-call(s32[4]{0:T(128)} %bitcast.159, s32[1]{0:T(128)} %bitcast.1.pos.rel, f32[8,2048]{1,0:T(8,128)} %get-tuple-element.150.refs_11_.cos, f32[8,2048]{1,0:T(8,128)} %get-tuple-element.149.refs_12_.sin, s32[1,2048]{1,0:T(1,128)} %compare_select_fusion.2.seg_start, ...), custom_call_target="tpu_custom_call" | custom-call | flops 10737418240 | bytes 10485760 | tf_op jit(solution)/shard_map/attention/pallas_call | solution.py:315
  157.1 3.5 fusion.35
  161.6 23.8 %mlp.3 = (bf16[1024,1024]{1,0:T(8,128)(2,1)}, bf16[1024,1024]{1,0:T(8,128)(2,1)}, bf16[1024,1024]{1,0:T(8,128)(2,1)}, bf16[1024,1024]{1,0:T(8,128)(2,1)}, f32[8,1024]{1,0:T(8,128)}, /*index=5*/f32[8,1024]{1,0:T(8,128)}) custom-call(s32[1]{0:T(128)} %bitcast.1.pos.rel, bf16[1024,1024]{1,0:T(8,128)(2,1)} %constant_dynamic-update-slice_fusion.refs_0_.refs_2_, ...), custom_call_target="tpu_custom_call" | custom-call | flops 12884901888 | bytes 20971520 | tf_op jit(solution)/shard_map/mlp/pallas_call | solution.py:110
  186.9 2.7 fusion.24
  190.6 10.0 %post.2 = (bf16[1024,1024]{1,0:T(8,128)(2,1)}, f32[768,1024]{1,0:T(8,128)}, f32[8,768]{1,0:T(8,128)}, f32[8,1024]{1,0:T(8,128)}) custom-call(s32[1]{0:T(128)} %bitcast.1.pos.rel, bf16[768,2048]{1,0:T(8,128)(2,1)} %get-tuple-element.70.refs_0_, bf16[2048,1024]{1,0:T(8,128)(2,1)} %get-tuple-element.71.refs_1_, ...), custom_call_target="tpu_custom_call" | custom-call | flops 3221225472 | bytes 14680064 | tf_op jit(solution)/shard_map/post/pallas_call | solution.py:410
  200.6 10.7 %post.3 = (bf16[1024,1024]{1,0:T(8,128)(2,1)}, bf16[8,768,128]{2,1,0:T(8,128)(2,1)}, f32[8,768]{1,0:T(8,128)}, f32[8,1024]{1,0:T(8,128)}) custom-call(s32[1]{0:T(128)} %bitcast.1.pos.rel, bf16[768,2048]{1,0:T(8,128)(2,1)} %get-tuple-element.70.refs_0_, bf16[2048,1024]{1,0:T(8,128)(2,1)} %get-tuple-element.71.refs_1_, ...), custom_call_target="tpu_custom_call" | custom-call | flops 3221225472 | bytes 14680064 | tf_op jit(solution)/shard_map/post/pallas_call | solution.py:410
  223.9 2.5 slice.112
  226.5 3.0 collective-permute-start.13
  229.7 2.3 collective-permute-start.24
  236.2 2.9 collective-permute-done.19
  245.2 3.1 collective-permute-start.10
  250.3 6.4 %collective-permute-start.36 = (bf16[32,256]{1,0:T(8,128)(2,1)S(1)}, bf16[32,256]{1,0:T(8,128)(2,1)S(1)}, u32[]{:S(2)}, u32[]{:S(2)}) collective-permute-start(bf16[32,256]{1,0:T(8,128)(2,1)S(1)} %bitcast.150), channel_id=1, source_target_pairs={{0,3},{1,11},{2,19},{3,27},{4,2},{5,10},{6,18},{7,26},{8,1},{9,9},... | collective-permute-start | bytes 49160 | tf_op jit(solution)/shard_map/ppermute | solution.py:485
  258.5 4.8 %collective-permute-start.39 = (bf16[32,256]{1,0:T(8,128)(2,1)S(1)}, bf16[32,256]{1,0:T(8,128)(2,1)S(1)}, u32[]{:S(2)}, u32[]{:S(2)}) collective-permute-start(bf16[32,256]{1,0:T(8,128)(2,1)S(1)} %bitcast.148), channel_id=1, source_target_pairs={{0,0},{1,8},{2,16},{3,24},{4,1},{5,9},{6,17},{7,25},{8,2},{9,10},{... | collective-permute-start | bytes 49160 | tf_op jit(solution)/shard_map/ppermute | solution.py:485
  263.4 4.3 %collective-permute-start.38 = (bf16[32,256]{1,0:T(8,128)(2,1)S(1)}, bf16[32,256]{1,0:T(8,128)(2,1)S(1)}, u32[]{:S(2)}, u32[]{:S(2)}) collective-permute-start(bf16[32,256]{1,0:T(8,128)(2,1)S(1)} %bitcast.147), channel_id=1, source_target_pairs={{0,1},{1,9},{2,17},{3,25},{4,0},{5,8},{6,16},{7,24},{8,3},{9,11},{... | collective-permute-start | bytes 49160 | tf_op jit(solution)/shard_map/ppermute | solution.py:485
  267.7 32.5 %collective-permute-start.26 = (bf16[768,128]{1,0:T(8,128)(2,1)S(1)}, bf16[768,128]{1,0:T(8,128)(2,1)S(1)}, u32[]{:S(2)}, u32[]{:S(2)}) collective-permute-start(bf16[768,128]{1,0:T(8,128)(2,1)S(1)} %get-tuple-element.119), channel_id=1, source_target_pairs={{0,8},{4,12},{8,0},{12,4},{16,24},{20,28},{24,16},{28,20},{1,9},{5... | collective-permute-start | bytes 589832 | tf_op jit(solution)/shard_map/ppermute | solution.py:449
  300.2 3.3 collective-permute-start.28
  303.5 2.7 add_convert_fusion
  306.2 3.0 collective-permute-start.27
  309.2 2.6 collective-permute-done.28
  311.9 8.7 %collective-permute-done.27 = bf16[768,128]{1,0:T(8,128)(2,1)S(1)} collective-permute-done((bf16[768,128]{1,0:T(8,128)(2,1)S(1)}, bf16[768,128]{1,0:T(8,128)(2,1)S(1)}, u32[]{:S(2)}, u32[]{:S(2)}) %collective-permute-start.27) | collective-permute-done | bytes 196640 | tf_op jit(solution)/shard_map/ppermute | solution.py:449
  320.7 3.4 collective-permute-start.29
  325.7 12.1 %collective-permute-done.29 = bf16[256,128]{1,0:T(8,128)(2,1)S(1)} collective-permute-done((bf16[256,128]{1,0:T(8,128)(2,1)S(1)}, bf16[256,128]{1,0:T(8,128)(2,1)S(1)}, u32[]{:S(2)}, u32[]{:S(2)}) %collective-permute-start.29) | collective-permute-done | bytes 65568 | tf_op jit(solution)/shard_map/ppermute | solution.py:496
  337.8 2.6 add_convert_fusion.1
  343.3 2.7 fusion.44
  346.9 2.8 fusion.64
  349.9 2.6 collective-permute-start.41
  352.5 2.7 collective-permute-start.43
  355.1 3.2 collective-permute-start.42
  358.4 18.4 %collective-permute-done.11 = bf16[512,1024]{1,0:T(8,128)(2,1)S(1)} collective-permute-done((bf16[512,1024]{1,0:T(8,128)(2,1)}, bf16[512,1024]{1,0:T(8,128)(2,1)S(1)}, u32[]{:S(2)}, u32[]{:S(2)}) %collective-permute-start.11) | collective-permute-done | bytes 1048608 | tf_op jit(solution)/shard_map/ppermute | solution.py:445
  376.9 3.9 fusion.11
  380.8 19.3 %collective-permute-done.42 = bf16[256,1024]{1,0:T(8,128)(2,1)S(1)} collective-permute-done((bf16[256,1024]{1,0:T(8,128)(2,1)S(1)}, bf16[256,1024]{1,0:T(8,128)(2,1)S(1)}, u32[]{:S(2)}, u32[]{:S(2)}) %collective-permute-start.42) | collective-permute-done | bytes 524320 | tf_op jit(solution)/shard_map/ppermute | solution.py:449
  403.8 4.8 %collective-permute-start.47 = (bf16[128,256]{1,0:T(8,128)(2,1)S(1)}, bf16[128,256]{1,0:T(8,128)(2,1)S(1)}, u32[]{:S(2)}, u32[]{:S(2)}) collective-permute-start(bf16[128,256]{1,0:T(8,128)(2,1)S(1)} %bitcast.145), channel_id=1, source_target_pairs={{0,0},{1,8},{2,16},{3,24},{4,1},{5,9},{6,17},{7,25},{8,2},{9,10},{... | collective-permute-start | bytes 196616 | tf_op jit(solution)/shard_map/ppermute | solution.py:485
  408.7 2.9 collective-permute-start.44
  412.4 4.2 %collective-permute-start.46 = (bf16[128,256]{1,0:T(8,128)(2,1)S(1)}, bf16[128,256]{1,0:T(8,128)(2,1)S(1)}, u32[]{:S(2)}, u32[]{:S(2)}) collective-permute-start(bf16[128,256]{1,0:T(8,128)(2,1)S(1)} %bitcast.142), channel_id=1, source_target_pairs={{0,1},{1,9},{2,17},{3,25},{4,0},{5,8},{6,16},{7,24},{8,3},{9,11},{... | collective-permute-start | bytes 196616 | tf_op jit(solution)/shard_map/ppermute | solution.py:485
  416.6 4.2 %fusion.7 = f32[512,1024]{1,0:T(8,128)} fusion(bf16[512,1024]{1,0:T(8,128)(2,1)S(1)} %copy-done, bf16[512,1024]{1,0:T(8,128)(2,1)} %param.29, f32[512]{0:T(512)S(1)} %get-tuple-element.154, f32[512]{0:T(512)S(1)} %get-tuple-element.155, f32[512]{0:T(512)S(1)} %add_rsqrt_fusion, f32[512]{0:T(512)S(1)} %broadcast_multiply_fusion.2, ...), kind=kLoop, calls=%fused_computation.15 | loop fusion | flops 7340032 | bytes 7348224 | tf_op jit(solution)/shard_map/add | solution.py:575
  (226 shorter events, 62.2 us)
Async XLA Ops:
  0.7 49.1 %collective-permute-start.5 = (bf16[512,1024]{1,0:T(8,128)(2,1)}, bf16[512,1024]{1,0:T(8,128)(2,1)}, u32[]{:S(2)}, u32[]{:S(2)}) collective-permute-start(bf16[512,1024]{1,0:T(8,128)(2,1)} %param.29), channel_id=1, source_target_pairs={{0,1},{1,0},{2,3},{3,2},{4,5},{5,4},{6,7},{7,6},{8,9},{9,8},{10,11... | collective-permute-start | bytes 3145736 | tf_op jit(solution)/shard_map/ppermute | solution.py:445
  1.4 25.0 %collective-permute-start.2 = (bf16[512,1024]{1,0:T(8,128)(2,1)}, bf16[512,1024]{1,0:T(8,128)(2,1)}, u32[]{:S(2)}, u32[]{:S(2)}) collective-permute-start(bf16[512,1024]{1,0:T(8,128)(2,1)} %param.29), channel_id=1, source_target_pairs={{0,2},{1,3},{2,0},{3,1},{4,6},{5,7},{6,4},{7,5},{8,10},{9,11},{10,... | collective-permute-start | bytes 3145736 | tf_op jit(solution)/shard_map/ppermute | solution.py:445
  1.6 47.2 %collective-permute-start = (bf16[512,1024]{1,0:T(8,128)(2,1)}, bf16[512,1024]{1,0:T(8,128)(2,1)}, u32[]{:S(2)}, u32[]{:S(2)}) collective-permute-start(bf16[512,1024]{1,0:T(8,128)(2,1)} %param.15), channel_id=1, source_target_pairs={{0,2},{1,3},{2,0},{3,1},{4,6},{5,7},{6,4},{7,5},{8,10},{9,11},{10,... | collective-permute-start | bytes 3145736 | tf_op jit(solution)/shard_map/ppermute | solution.py:445
  2.9 49.2 %collective-permute-start.4 = (bf16[512,1024]{1,0:T(8,128)(2,1)}, bf16[512,1024]{1,0:T(8,128)(2,1)}, u32[]{:S(2)}, u32[]{:S(2)}) collective-permute-start(bf16[512,1024]{1,0:T(8,128)(2,1)} %param.15), channel_id=1, source_target_pairs={{0,1},{1,0},{2,3},{3,2},{4,5},{5,4},{6,7},{7,6},{8,9},{9,8},{10,11... | collective-permute-start | bytes 3145736 | tf_op jit(solution)/shard_map/ppermute | solution.py:445
  26.3 66.3 %collective-permute-start.3 = (bf16[512,1024]{1,0:T(8,128)(2,1)}, bf16[512,1024]{1,0:T(8,128)(2,1)}, u32[]{:S(2)}, u32[]{:S(2)}) collective-permute-start(bf16[512,1024]{1,0:T(8,128)(2,1)} %collective-permute-done.2), channel_id=1, source_target_pairs={{0,1},{1,0},{2,3},{3,2},{4,5},{5,4},{6,7},{7,6},{8,9},{9,8},{10,11... | collective-permute-start | bytes 3145736 | tf_op jit(solution)/shard_map/ppermute | solution.py:445
  48.8 41.5 %collective-permute-start.1 = (bf16[512,1024]{1,0:T(8,128)(2,1)}, bf16[512,1024]{1,0:T(8,128)(2,1)}, u32[]{:S(2)}, u32[]{:S(2)}) collective-permute-start(bf16[512,1024]{1,0:T(8,128)(2,1)} %collective-permute-done), channel_id=1, source_target_pairs={{0,1},{1,0},{2,3},{3,2},{4,5},{5,4},{6,7},{7,6},{8,9},{9,8},{10,11... | collective-permute-start | bytes 3145736 | tf_op jit(solution)/shard_map/ppermute | solution.py:445
  190.6 22.9 %collective-permute-start.20 = (f32[8,1024]{1,0:T(8,128)S(1)}, f32[8,1024]{1,0:T(8,128)S(1)}, u32[]{:S(2)}, u32[]{:S(2)}) collective-permute-start(f32[8,1024]{1,0:T(8,128)S(1)} %maximum_maximum_fusion), channel_id=1, source_target_pairs={{0,1},{1,0},{2,3},{3,2},{4,5},{5,4},{6,7},{7,6},{8,9},{9,8},{10,11... | collective-permute-start | bytes 98312 | tf_op jit(solution)/shard_map/ppermute | solution.py:445
  213.0 1.4 collective-permute-start.15
  213.6 2.8 collective-permute-start.21
  214.4 3.5 collective-permute-start.16
  216.3 2.8 collective-permute-start.22
  216.4 22.8 %collective-permute-start.32 = (bf16[4,32,1024]{2,1,0:T(8,128)(2,1)S(1)}, bf16[4,32,1024]{2,1,0:T(8,128)(2,1)S(1)}, u32[]{:S(2)}, u32[]{:S(2)}) collective-permute-start(bf16[4,32,1024]{2,1,0:T(8,128)(2,1)S(1)} %dynamic-slice_bitcast_fusion.8), channel_id=1, source_target_pairs={{0,4},{4,0},{8,12},{12,8},{16,20},{20,16},{24,28},{28,24},{1,5},{5... | collective-permute-start | bytes 786440 | tf_op jit(solution)/shard_map/ppermute | solution.py:449
  217.9 11.6 %collective-permute-start.17 = (f32[8,1024]{1,0:T(8,128)S(1)}, f32[8,1024]{1,0:T(8,128)S(1)}, u32[]{:S(2)}, u32[]{:S(2)}) collective-permute-start(f32[8,1024]{1,0:T(8,128)S(1)} %add.270), channel_id=1, source_target_pairs={{0,4},{4,0},{8,12},{12,8},{16,20},{20,16},{24,28},{28,24},{1,5},{5... | collective-permute-start | bytes 98312 | tf_op jit(solution)/shard_map/ppermute | solution.py:449
  219.1 10.6 %collective-permute-start.23 = (f32[8,1024]{1,0:T(8,128)S(1)}, f32[8,1024]{1,0:T(8,128)S(1)}, u32[]{:S(2)}, u32[]{:S(2)}) collective-permute-start(f32[8,1024]{1,0:T(8,128)S(1)} %add.276), channel_id=1, source_target_pairs={{0,8},{4,12},{8,0},{12,4},{16,24},{20,28},{24,16},{28,20},{1,9},{5... | collective-permute-start | bytes 98312 | tf_op jit(solution)/shard_map/ppermute | solution.py:449
  223.5 33.1 %collective-permute-start.25 = (bf16[4,768,128]{2,1,0:T(8,128)(2,1)}, bf16[4,768,128]{2,1,0:T(8,128)(2,1)}, u32[]{:S(2)}, u32[]{:S(2)}) collective-permute-start(bf16[4,768,128]{2,1,0:T(8,128)(2,1)} %dynamic-slice_bitcast_fusion), channel_id=1, source_target_pairs={{0,4},{4,0},{8,12},{12,8},{16,20},{20,16},{24,28},{28,24},{1,5},{5... | collective-permute-start | bytes 2359304 | tf_op jit(solution)/shard_map/ppermute | solution.py:449
  226.5 73.7 %collective-permute-start.13 = (bf16[512,1024]{1,0:T(8,128)(2,1)}, bf16[512,1024]{1,0:T(8,128)(2,1)}, u32[]{:S(2)}, u32[]{:S(2)}) collective-permute-start(bf16[512,1024]{1,0:T(8,128)(2,1)} %slice.112), channel_id=1, source_target_pairs={{0,1},{1,0},{2,3},{3,2},{4,5},{5,4},{6,7},{7,6},{8,9},{9,8},{10,11... | collective-permute-start | bytes 3145736 | tf_op jit(solution)/shard_map/ppermute | solution.py:445
  229.5 5.9 %collective-permute-start.18 = (f32[8,1024]{1,0:T(8,128)S(1)}, f32[8,1024]{1,0:T(8,128)S(1)}, u32[]{:S(2)}, u32[]{:S(2)}) collective-permute-start(f32[8,1024]{1,0:T(8,128)S(1)} %add.271), channel_id=1, source_target_pairs={{0,8},{4,12},{8,0},{12,4},{16,24},{20,28},{24,16},{28,20},{1,9},{5... | collective-permute-start | bytes 98312 | tf_op jit(solution)/shard_map/ppermute | solution.py:449
  229.7 5.9 %collective-permute-start.24 = (f32[8,1024]{1,0:T(8,128)S(1)}, f32[8,1024]{1,0:T(8,128)S(1)}, u32[]{:S(2)}, u32[]{:S(2)}) collective-permute-start(f32[8,1024]{1,0:T(8,128)S(1)} %add.277), channel_id=1, source_target_pairs={{0,16},{4,20},{8,24},{12,28},{16,0},{20,4},{24,8},{28,12},{1,17},{... | collective-permute-start | bytes 98312 | tf_op jit(solution)/shard_map/ppermute | solution.py:449
  235.4 3.7 collective-permute-start.19
  240.7 4.5 %collective-permute-start.33 = (bf16[32,1024]{1,0:T(8,128)(2,1)}, bf16[32,1024]{1,0:T(8,128)(2,1)S(1)}, u32[]{:S(2)}, u32[]{:S(2)}) collective-permute-start(bf16[32,1024]{1,0:T(8,128)(2,1)} %get-tuple-element.130), channel_id=1, source_target_pairs={{0,8},{4,12},{8,0},{12,4},{16,24},{20,28},{24,16},{28,20},{1,9},{5... | collective-permute-start | bytes 196616 | tf_op jit(solution)/shard_map/ppermute | solution.py:449
  242.2 6.1 %collective-permute-start.35 = (bf16[32,1024]{1,0:T(8,128)(2,1)S(1)}, bf16[32,1024]{1,0:T(8,128)(2,1)S(1)}, u32[]{:S(2)}, u32[]{:S(2)}) collective-permute-start(bf16[32,1024]{1,0:T(8,128)(2,1)S(1)} %get-tuple-element.131), channel_id=1, source_target_pairs={{0,24},{4,28},{8,16},{12,20},{16,8},{20,12},{24,0},{28,4},{1,25},{... | collective-permute-start | bytes 196616 | tf_op jit(solution)/shard_map/ppermute | solution.py:449
  242.2 6.9 %collective-permute-start.34 = (bf16[32,1024]{1,0:T(8,128)(2,1)S(1)}, bf16[32,1024]{1,0:T(8,128)(2,1)S(1)}, u32[]{:S(2)}, u32[]{:S(2)}) collective-permute-start(bf16[32,1024]{1,0:T(8,128)(2,1)S(1)} %get-tuple-element.132), channel_id=1, source_target_pairs={{0,16},{4,20},{8,24},{12,28},{16,0},{20,4},{24,8},{28,12},{1,17},{... | collective-permute-start | bytes 196616 | tf_op jit(solution)/shard_map/ppermute | solution.py:449
  245.2 79.6 %collective-permute-start.10 = (bf16[512,1024]{1,0:T(8,128)(2,1)}, bf16[512,1024]{1,0:T(8,128)(2,1)}, u32[]{:S(2)}, u32[]{:S(2)}) collective-permute-start(bf16[512,1024]{1,0:T(8,128)(2,1)} %slice.108), channel_id=1, source_target_pairs={{0,1},{1,0},{2,3},{3,2},{4,5},{5,4},{6,7},{7,6},{8,9},{9,8},{10,11... | collective-permute-start | bytes 3145736 | tf_op jit(solution)/shard_map/ppermute | solution.py:445
  248.3 97.8 %collective-permute-start.40 = (bf16[4,256,1024]{2,1,0:T(8,128)(2,1)}, bf16[4,256,1024]{2,1,0:T(8,128)(2,1)}, u32[]{:S(2)}, u32[]{:S(2)}) collective-permute-start(bf16[4,256,1024]{2,1,0:T(8,128)(2,1)} %fusion.13), channel_id=1, source_target_pairs={{0,4},{4,0},{8,12},{12,8},{16,20},{20,16},{24,28},{28,24},{1,5},{5... | collective-permute-start | bytes 6291464 | tf_op jit(solution)/shard_map/ppermute | solution.py:449
  250.3 8.2 %collective-permute-start.36 = (bf16[32,256]{1,0:T(8,128)(2,1)S(1)}, bf16[32,256]{1,0:T(8,128)(2,1)S(1)}, u32[]{:S(2)}, u32[]{:S(2)}) collective-permute-start(bf16[32,256]{1,0:T(8,128)(2,1)S(1)} %bitcast.150), channel_id=1, source_target_pairs={{0,3},{1,11},{2,19},{3,27},{4,2},{5,10},{6,18},{7,26},{8,1},{9,9},... | collective-permute-start | bytes 49160 | tf_op jit(solution)/shard_map/ppermute | solution.py:485
  256.7 6.7 %collective-permute-start.37 = (bf16[32,256]{1,0:T(8,128)(2,1)S(1)}, bf16[32,256]{1,0:T(8,128)(2,1)S(1)}, u32[]{:S(2)}, u32[]{:S(2)}) collective-permute-start(bf16[32,256]{1,0:T(8,128)(2,1)S(1)} %bitcast.149), channel_id=1, source_target_pairs={{0,2},{1,10},{2,18},{3,26},{4,3},{5,11},{6,19},{7,27},{8,0},{9,8},... | collective-permute-start | bytes 49160 | tf_op jit(solution)/shard_map/ppermute | solution.py:485
  258.5 9.2 %collective-permute-start.39 = (bf16[32,256]{1,0:T(8,128)(2,1)S(1)}, bf16[32,256]{1,0:T(8,128)(2,1)S(1)}, u32[]{:S(2)}, u32[]{:S(2)}) collective-permute-start(bf16[32,256]{1,0:T(8,128)(2,1)S(1)} %bitcast.148), channel_id=1, source_target_pairs={{0,0},{1,8},{2,16},{3,24},{4,1},{5,9},{6,17},{7,25},{8,2},{9,10},{... | collective-permute-start | bytes 49160 | tf_op jit(solution)/shard_map/ppermute | solution.py:485
  263.4 42.8 %collective-permute-start.38 = (bf16[32,256]{1,0:T(8,128)(2,1)S(1)}, bf16[32,256]{1,0:T(8,128)(2,1)S(1)}, u32[]{:S(2)}, u32[]{:S(2)}) collective-permute-start(bf16[32,256]{1,0:T(8,128)(2,1)S(1)} %bitcast.147), channel_id=1, source_target_pairs={{0,1},{1,9},{2,17},{3,25},{4,0},{5,8},{6,16},{7,24},{8,3},{9,11},{... | collective-permute-start | bytes 49160 | tf_op jit(solution)/shard_map/ppermute | solution.py:485
  267.7 38.5 %collective-permute-start.26 = (bf16[768,128]{1,0:T(8,128)(2,1)S(1)}, bf16[768,128]{1,0:T(8,128)(2,1)S(1)}, u32[]{:S(2)}, u32[]{:S(2)}) collective-permute-start(bf16[768,128]{1,0:T(8,128)(2,1)S(1)} %get-tuple-element.119), channel_id=1, source_target_pairs={{0,8},{4,12},{8,0},{12,4},{16,24},{20,28},{24,16},{28,20},{1,9},{5... | collective-permute-start | bytes 589832 | tf_op jit(solution)/shard_map/ppermute | solution.py:449
  300.2 11.6 %collective-permute-start.28 = (bf16[768,128]{1,0:T(8,128)(2,1)S(1)}, bf16[768,128]{1,0:T(8,128)(2,1)S(1)}, u32[]{:S(2)}, u32[]{:S(2)}) collective-permute-start(bf16[768,128]{1,0:T(8,128)(2,1)S(1)} %get-tuple-element.120), channel_id=1, source_target_pairs={{0,24},{4,28},{8,16},{12,20},{16,8},{20,12},{24,0},{28,4},{1,25},{... | collective-permute-start | bytes 589832 | tf_op jit(solution)/shard_map/ppermute | solution.py:449
  306.2 35.6 %collective-permute-start.12 = (bf16[512,1024]{1,0:T(8,128)(2,1)}, bf16[512,1024]{1,0:T(8,128)(2,1)}, u32[]{:S(2)}, u32[]{:S(2)}) collective-permute-start(bf16[512,1024]{1,0:T(8,128)(2,1)} %slice.110), channel_id=1, source_target_pairs={{0,1},{1,0},{2,3},{3,2},{4,5},{5,4},{6,7},{7,6},{8,9},{9,8},{10,11... | collective-permute-start | bytes 3145736 | tf_op jit(solution)/shard_map/ppermute | solution.py:445
  306.2 14.4 %collective-permute-start.27 = (bf16[768,128]{1,0:T(8,128)(2,1)S(1)}, bf16[768,128]{1,0:T(8,128)(2,1)S(1)}, u32[]{:S(2)}, u32[]{:S(2)}) collective-permute-start(bf16[768,128]{1,0:T(8,128)(2,1)S(1)} %get-tuple-element.121), channel_id=1, source_target_pairs={{0,16},{4,20},{8,24},{12,28},{16,0},{20,4},{24,8},{28,12},{1,17},{... | collective-permute-start | bytes 589832 | tf_op jit(solution)/shard_map/ppermute | solution.py:449
  311.8 31.4 %collective-permute-start.14 = (bf16[512,1024]{1,0:T(8,128)(2,1)}, bf16[512,1024]{1,0:T(8,128)(2,1)}, u32[]{:S(2)}, u32[]{:S(2)}) collective-permute-start(bf16[512,1024]{1,0:T(8,128)(2,1)} %add_convert_fusion), channel_id=1, source_target_pairs={{0,2},{1,3},{2,0},{3,1},{4,6},{5,7},{6,4},{7,5},{8,10},{9,11},{10,... | collective-permute-start | bytes 3145736 | tf_op jit(solution)/shard_map/ppermute | solution.py:445
  320.7 17.1 %collective-permute-start.29 = (bf16[256,128]{1,0:T(8,128)(2,1)S(1)}, bf16[256,128]{1,0:T(8,128)(2,1)S(1)}, u32[]{:S(2)}, u32[]{:S(2)}) collective-permute-start(bf16[256,128]{1,0:T(8,128)(2,1)S(1)} %get-tuple-element.133), channel_id=1, source_target_pairs={{0,0},{3,1},{2,2},{1,3},{4,4},{7,5},{6,6},{5,7},{8,8},{11,9},{10,1... | collective-permute-start | bytes 196616 | tf_op jit(solution)/shard_map/ppermute | solution.py:496
  324.8 15.6 %collective-permute-start.31 = (bf16[256,128]{1,0:T(8,128)(2,1)S(1)}, bf16[256,128]{1,0:T(8,128)(2,1)S(1)}, u32[]{:S(2)}, u32[]{:S(2)}) collective-permute-start(bf16[256,128]{1,0:T(8,128)(2,1)S(1)} %get-tuple-element.134), channel_id=1, source_target_pairs={{2,0},{1,1},{0,2},{3,3},{6,4},{5,5},{4,6},{7,7},{10,8},{9,9},{8,10... | collective-permute-start | bytes 196616 | tf_op jit(solution)/shard_map/ppermute | solution.py:496
  337.8 3.1 collective-permute-start.30
  340.4 9.5 %collective-permute-start.9 = (bf16[512,1024]{1,0:T(8,128)(2,1)}, bf16[512,1024]{1,0:T(8,128)(2,1)}, u32[]{:S(2)}, u32[]{:S(2)}) collective-permute-start(bf16[512,1024]{1,0:T(8,128)(2,1)} %slice.106), channel_id=1, source_target_pairs={{0,1},{1,0},{2,3},{3,2},{4,5},{5,4},{6,7},{7,6},{8,9},{9,8},{10,11... | collective-permute-start | bytes 3145736 | tf_op jit(solution)/shard_map/ppermute | solution.py:445
  340.9 11.6 %collective-permute-start.8 = (bf16[256,512]{1,0:T(8,128)(2,1)}, bf16[256,512]{1,0:T(8,128)(2,1)}, u32[]{:S(2)}, u32[]{:S(2)}) collective-permute-start(bf16[256,512]{1,0:T(8,128)(2,1)} %get-tuple-element.116), channel_id=1, source_target_pairs={{0,3},{1,2},{2,1},{3,0},{4,7},{5,6},{6,5},{7,4},{8,11},{9,10},{10,... | collective-permute-start | bytes 786440 | tf_op jit(solution)/shard_map/ppermute | solution.py:445
  341.8 13.3 %collective-permute-start.7 = (bf16[256,512]{1,0:T(8,128)(2,1)}, bf16[256,512]{1,0:T(8,128)(2,1)S(1)}, u32[]{:S(2)}, u32[]{:S(2)}) collective-permute-start(bf16[256,512]{1,0:T(8,128)(2,1)} %get-tuple-element.117), channel_id=1, source_target_pairs={{0,2},{1,3},{2,0},{3,1},{4,6},{5,7},{6,4},{7,5},{8,10},{9,11},{10,... | collective-permute-start | bytes 786440 | tf_op jit(solution)/shard_map/ppermute | solution.py:445
  343.3 33.6 %collective-permute-start.11 = (bf16[512,1024]{1,0:T(8,128)(2,1)}, bf16[512,1024]{1,0:T(8,128)(2,1)S(1)}, u32[]{:S(2)}, u32[]{:S(2)}) collective-permute-start(bf16[512,1024]{1,0:T(8,128)(2,1)} %add_convert_fusion.1), channel_id=1, source_target_pairs={{0,2},{1,3},{2,0},{3,1},{4,6},{5,7},{6,4},{7,5},{8,10},{9,11},{10,... | collective-permute-start | bytes 3145736 | tf_op jit(solution)/shard_map/ppermute | solution.py:445
  346.1 12.3 %collective-permute-start.6 = (bf16[256,512]{1,0:T(8,128)(2,1)S(1)}, bf16[256,512]{1,0:T(8,128)(2,1)S(1)}, u32[]{:S(2)}, u32[]{:S(2)}) collective-permute-start(bf16[256,512]{1,0:T(8,128)(2,1)S(1)} %copy-done.21), channel_id=1, source_target_pairs={{0,1},{1,0},{2,3},{3,2},{4,5},{5,4},{6,7},{7,6},{8,9},{9,8},{10,11... | collective-permute-start | bytes 786440 | tf_op jit(solution)/shard_map/ppermute | solution.py:445
  349.9 30.9 %collective-permute-start.41 = (bf16[256,1024]{1,0:T(8,128)(2,1)S(1)}, bf16[256,1024]{1,0:T(8,128)(2,1)S(1)}, u32[]{:S(2)}, u32[]{:S(2)}) collective-permute-start(bf16[256,1024]{1,0:T(8,128)(2,1)S(1)} %get-tuple-element.108), channel_id=1, source_target_pairs={{0,8},{4,12},{8,0},{12,4},{16,24},{20,28},{24,16},{28,20},{1,9},{5... | collective-permute-start | bytes 1572872 | tf_op jit(solution)/shard_map/ppermute | solution.py:449
  352.5 28.3 %collective-permute-start.43 = (bf16[256,1024]{1,0:T(8,128)(2,1)S(1)}, bf16[256,1024]{1,0:T(8,128)(2,1)S(1)}, u32[]{:S(2)}, u32[]{:S(2)}) collective-permute-start(bf16[256,1024]{1,0:T(8,128)(2,1)S(1)} %get-tuple-element.109), channel_id=1, source_target_pairs={{0,24},{4,28},{8,16},{12,20},{16,8},{20,12},{24,0},{28,4},{1,25},{... | collective-permute-start | bytes 1572872 | tf_op jit(solution)/shard_map/ppermute | solution.py:449
  355.1 44.9 %collective-permute-start.42 = (bf16[256,1024]{1,0:T(8,128)(2,1)S(1)}, bf16[256,1024]{1,0:T(8,128)(2,1)S(1)}, u32[]{:S(2)}, u32[]{:S(2)}) collective-permute-start(bf16[256,1024]{1,0:T(8,128)(2,1)S(1)} %get-tuple-element.110), channel_id=1, source_target_pairs={{0,16},{4,20},{8,24},{12,28},{16,0},{20,4},{24,8},{28,12},{1,17},{... | collective-permute-start | bytes 1572872 | tf_op jit(solution)/shard_map/ppermute | solution.py:449
  403.8 17.9 %collective-permute-start.47 = (bf16[128,256]{1,0:T(8,128)(2,1)S(1)}, bf16[128,256]{1,0:T(8,128)(2,1)S(1)}, u32[]{:S(2)}, u32[]{:S(2)}) collective-permute-start(bf16[128,256]{1,0:T(8,128)(2,1)S(1)} %bitcast.145), channel_id=1, source_target_pairs={{0,0},{1,8},{2,16},{3,24},{4,1},{5,9},{6,17},{7,25},{8,2},{9,10},{... | collective-permute-start | bytes 196616 | tf_op jit(solution)/shard_map/ppermute | solution.py:485
  408.7 13.1 %collective-permute-start.44 = (bf16[128,256]{1,0:T(8,128)(2,1)S(1)}, bf16[128,256]{1,0:T(8,128)(2,1)S(1)}, u32[]{:S(2)}, u32[]{:S(2)}) collective-permute-start(bf16[128,256]{1,0:T(8,128)(2,1)S(1)} %bitcast.144), channel_id=1, source_target_pairs={{0,3},{1,11},{2,19},{3,27},{4,2},{5,10},{6,18},{7,26},{8,1},{9,9},... | collective-permute-start | bytes 196616 | tf_op jit(solution)/shard_map/ppermute | solution.py:485
  411.6 10.2 %collective-permute-start.45 = (bf16[128,256]{1,0:T(8,128)(2,1)S(1)}, bf16[128,256]{1,0:T(8,128)(2,1)S(1)}, u32[]{:S(2)}, u32[]{:S(2)}) collective-permute-start(bf16[128,256]{1,0:T(8,128)(2,1)S(1)} %bitcast.143), channel_id=1, source_target_pairs={{0,2},{1,10},{2,18},{3,26},{4,3},{5,11},{6,19},{7,27},{8,0},{9,8},... | collective-permute-start | bytes 196616 | tf_op jit(solution)/shard_map/ppermute | solution.py:485
  412.4 9.3 %collective-permute-start.46 = (bf16[128,256]{1,0:T(8,128)(2,1)S(1)}, bf16[128,256]{1,0:T(8,128)(2,1)S(1)}, u32[]{:S(2)}, u32[]{:S(2)}) collective-permute-start(bf16[128,256]{1,0:T(8,128)(2,1)S(1)} %bitcast.142), channel_id=1, source_target_pairs={{0,1},{1,9},{2,17},{3,25},{4,0},{5,8},{6,16},{7,24},{8,3},{9,11},{... | collective-permute-start | bytes 196616 | tf_op jit(solution)/shard_map/ppermute | solution.py:485
  (32 other events, 587.6 us)

commit v2 on v1

--- a/solution.py
+++ b/solution.py
@@ -194,14 +194,243 @@
     )(pos, x, dy, w_qkv, w_qkv, w_qkv, b_qkv, b_qkv, b_qkv, w_out, gain, shift, cos, sin, *(prev or ()))
 
 
-def attn_kernel(nh, tok, blk, per, lens, rel, cos, sin, seg_start, qt, kt, vt, dot, kn, vn,
+def head_kernel(nh, x_hbm, dy_hbm, wu_hbm, wd_hbm, wqkv_hbm, wo_hbm, bu, bq, gain_m, shift_m, gain_a, shift_a, cos, sin,
+                g_out, na_out, dy_out, qt, kt, vt, dot, kn, vn, p_own, p_far, out_wu, out_wd, small, smallf,
+                xs, dys, wu, wd, wqkv, wt, wo, bias_t, parts, far_in, near_in, dwu, dwd, load, send, recv):
+    step = pl.program_id(0)
+    j = lax.axis_index("head")
+    own, d = x_hbm.shape
+    f = wu.shape[1]
+    w = wo.shape[0]
+    half = own // 2
+    core = {"head": j ^ 1}
+    across = {"head": j ^ 2}
+
+    def remote(src, dst, k, to):
+        return pltpu.make_async_remote_copy(
+            src_ref=src, dst_ref=dst, send_sem=send.at[k], recv_sem=recv.at[k], device_id=to,
+            device_id_type=pl.DeviceIdType.MESH)
+
+    lo, hi = pl.ds(0, half), pl.ds(half, half)
+    copies = [
+        remote(x_hbm, xs.at[1], 0, core),
+        remote(dy_hbm, dys.at[1], 1, core),
+        remote(x_hbm.at[lo], xs.at[2, lo], 2, across),
+        remote(dy_hbm.at[lo], dys.at[2, lo], 3, across),
+        remote(x_hbm.at[hi], xs.at[3, lo], 4, across),
+        remote(dy_hbm.at[hi], dys.at[3, lo], 5, across),
+        remote(xs.at[2, lo], xs.at[2, hi], 6, core),
+        remote(dys.at[2, lo], dys.at[2, hi], 7, core),
+        remote(xs.at[3, lo], xs.at[3, hi], 8, core),
+        remote(dys.at[3, lo], dys.at[3, hi], 9, core),
+        remote(parts.at[1], near_in, 10, core),
+        remote(parts.at[2, hi], far_in.at[lo], 11, core),
+        remote(parts.at[3, hi], far_in.at[hi], 12, core),
+    ]
+    locals_ = [
+        pltpu.make_async_copy(x_hbm, xs.at[0], load.at[0]),
+        pltpu.make_async_copy(dy_hbm, dys.at[0], load.at[1]),
+        pltpu.make_async_copy(wu_hbm.at[:, pl.ds(j * f, f)], wu, load.at[2]),
+        pltpu.make_async_copy(wd_hbm.at[pl.ds(j * f, f)], wd, load.at[3]),
+        pltpu.make_async_copy(wo_hbm.at[pl.ds(j * w, w)], wo, load.at[4]),
+    ] + [
+        pltpu.make_async_copy(wqkv_hbm.at[:, pl.ds(k * d + j * w, w)], wqkv.at[:, pl.ds(k * w, w)], load.at[5 + k])
+        for k in range(3)
+    ]
+
+    @pl.when(step == 0)
+    def _():
+        barrier = pltpu.get_barrier_semaphore()
+        for to in (core, across):
+            pl.semaphore_signal(barrier, inc=1, device_id=to, device_id_type=pl.DeviceIdType.MESH)
+        for c in locals_:
+            c.start()
+        pl.semaphore_wait(barrier, 2)
+        for c in copies[:6]:
+            c.start()
+        dwu[...] = jnp.zeros_like(dwu)
+        dwd[...] = jnp.zeros_like(dwd)
+        small[...] = jnp.zeros_like(small)
+        smallf[...] = jnp.zeros_like(smallf)
+        for c in locals_:
+            c.wait()
+        for k in range(3):
+            wt[k * w : (k + 1) * w, :] = wqkv[:, k * w : (k + 1) * w].T
+            row = bq[:, pl.ds(pl.multiple_of(k * d + j * w, 128), w)].astype(F32)
+            bias_t[k * w : (k + 1) * w, :] = jnp.broadcast_to(row, (128, w)).T
+
+    @pl.when(step == 1)
+    def _():
+        copies[0].wait_recv()
+        copies[1].wait_recv()
+
+    @pl.when(step == 2)
+    def _():
+        copies[6].wait_recv()
+        copies[7].wait_recv()
+
+    @pl.when(step == 3)
+    def _():
+        copies[8].wait_recv()
+        copies[9].wait_recv()
+
+    normed, _unused = norm_parts(xs[step])
+    scale = gain_m[...].astype(F32)
+    nm = (normed * scale + shift_m[...].astype(F32)).astype(BF)
+    na = (normed * gain_a[...].astype(F32) + shift_a[...].astype(F32)).astype(BF)
+    dy = dys[step]
+    na_out[...] = na
+    dy_out[...] = dy
+    pre = mm(nm, wu[...]) + bu[:, pl.ds(pl.multiple_of(j * f, 128), f)].astype(F32)
+    cdf = 0.5 + 0.5 * lax.erf(pre * (0.5**0.5))
+    hid = (pre * cdf).astype(BF)
+    slope = cdf + pre * (jnp.exp(-0.5 * pre * pre) * 0.3989422804014327)
+    gp = (mm(dy, wd[...], NT) * slope).astype(BF)
+    parts[step] = mm(hid, wd[...]).astype(BF)
+    r = mm(gp, wu[...], NT)
+    g_out[...] = (r * scale).astype(BF)
+    smallf[0:1, :] += jnp.sum(gp.astype(F32), axis=0, keepdims=True)
+    small[0:1, :] += jnp.sum(r * normed, axis=0, keepdims=True)
+    small[1:2, :] += jnp.sum(r, axis=0, keepdims=True)
+    small[2:3, :] += jnp.sum(dy.astype(F32), axis=0, keepdims=True)
+    dwd[...] += mm(hid, dy, TN)
+    dwu[...] += mm(nm, gp, TN)
+
+    @pl.when(step == 1)
+    def _():
+        for k in (2, 3):
+            copies[k].wait_recv()
+            copies[k + 4].start()
+        copies[10].start()
+
+    @pl.when(step == 2)
+    def _():
+        for k in (4, 5):
+            copies[k].wait_recv()
+            copies[k + 4].start()
+        copies[11].start()
+
+    @pl.when(step == 3)
+    def _():
+        copies[12].start()
+        for b in range(out_wu.shape[0]):
+            rows = out_wu.shape[1]
+            out_wu[b] = dwu[b * rows : (b + 1) * rows, :].astype(BF)
+        for b in range(out_wd.shape[0]):
+            rows = out_wd.shape[1]
+            out_wd[b] = dwd[b * rows : (b + 1) * rows, :].astype(BF)
+
+    co = cos[...]
+    si = sin[...]
+
+    def projected(k):
+        b = bias_t[k * w : (k + 1) * w, :]
+        t = mm(wt[k * w : (k + 1) * w, :], na, NT)
+        return (t + jnp.concatenate([b] * (own // 128), axis=1)).astype(BF)
+
+    def rotated(t, factor):
+        rows = []
+        for h in range(nh):
+            u = t[h * HD : (h + 1) * HD].astype(F32)
+            u1 = u[:HALF]
+            u2 = u[HALF:ROT]
+            rows += [u1 * co - u2 * si, u2 * co + u1 * si, u[ROT:]]
+        out = jnp.concatenate(rows, axis=0)
+        return (out if factor is None else out * factor).astype(BF)
+
+    qt[...] = rotated(projected(0), HD**-0.5)
+    keys = rotated(projected(1), None)
+    kt[...] = keys
+    kn[...] = keys.T
+    values = projected(2)
+    vt[...] = values
+    vn[...] = values.T
+    dot[...] = mm(wo[...], dy, NT).astype(BF)
+
+    @pl.when(step == 3)
+    def _():
+        copies[10].wait_recv()
+        p_own[...] = (parts[0].astype(F32) + near_in[...].astype(F32)).astype(BF)
+        copies[11].wait_recv()
+        p_far[lo] = (parts[2, lo].astype(F32) + far_in[lo].astype(F32)).astype(BF)
+        copies[12].wait_recv()
+        p_far[hi] = (parts[3, lo].astype(F32) + far_in[hi].astype(F32)).astype(BF)
+        for c in copies:
+            c.wait_send()
+
+
+def head_stage(x, dy, w_up, w_down, w_qkv, w_out, bu, bq, gm, sm, ga, sa, cos, sin, n, cid):
+    own, d = x.shape
+    tok = own * n
+    w = d // n
+    f = w_up.shape[1] // n
+    row = lambda i: (i, 0)
+    lane = lambda rows: pl.BlockSpec((rows, own), lambda i: (0, i))
+    nat = lambda cols: pl.BlockSpec((own, cols), row)
+    one = pl.Buffered(1)
+    const = lambda shape: pl.BlockSpec(shape, lambda i: (0,) * len(shape), pipeline_mode=one)
+    hbm = pl.BlockSpec(memory_space=pl.ANY)
+    sds = jax.ShapeDtypeStruct
+    return pl.pallas_call(
+        functools.partial(head_kernel, w // HD),
+        grid=(n,),
+        in_specs=[hbm] * 6
+        + [const((1, w_up.shape[1])), const((1, 3 * d))]
+        + [const((1, d))] * 4
+        + [lane(HALF), lane(HALF)],
+        out_specs=[nat(d)] * 3
+        + [lane(w)] * 4
+        + [nat(w)] * 2
+        + [const((own, d))] * 2
+        + [const((8, d // 8, f)), const((8, f // 8, d)), const((8, d)), const((8, f))],
+        out_shape=tuple(
+            [sds((tok, d), BF)] * 3
+            + [sds((w, tok), BF)] * 4
+            + [sds((tok, w), BF)] * 2
+            + [sds((own, d), BF)] * 2
+            + [sds((8, d // 8, f), BF), sds((8, f // 8, d), BF), sds((8, d), F32), sds((8, f), F32)]
+        ),
+        scratch_shapes=[
+            pltpu.VMEM((4, own, d), BF),
+            pltpu.VMEM((4, own, d), BF),
+            pltpu.VMEM((d, f), BF),
+            pltpu.VMEM((f, d), BF),
+            pltpu.VMEM((d, 3 * w), BF),
+            pltpu.VMEM((3 * w, d), BF),
+            pltpu.VMEM((w, d), BF),
+            pltpu.VMEM((3 * w, 128), F32),
+            pltpu.VMEM((4, own, d), BF),
+            pltpu.VMEM((own, d), BF),
+            pltpu.VMEM((own, d), BF),
+            pltpu.VMEM((d, f), F32),
+            pltpu.VMEM((f, d), F32),
+            pltpu.SemaphoreType.DMA((8,)),
+            pltpu.SemaphoreType.DMA((13,)),
+            pltpu.SemaphoreType.DMA((13,)),
+        ],
+        compiler_params=pltpu.CompilerParams(
+            vmem_limit_bytes=VMEM_LIMIT, collective_id=cid, has_side_effects=True
+        ),
+        cost_estimate=pl.CostEstimate(
+            flops=12 * tok * d * f + 10 * tok * d * w, bytes_accessed=12 * tok * d + 8 * d * f, transcendentals=2 * tok * f
+        ),
+        name="head_stage",
+    )(x, dy, w_up, w_down, w_qkv, w_out, bu, bq, gm, sm, ga, sa, cos, sin)
+
+
+def attn_kernel(nh, tok, blk, per, halved, lens, rel, cos, sin, seg_start, qt, kt, vt, dot, kn, vn,
                 gt_ref, ctx_ref, exps, peaks, dk, dv, oacc, dqacc, mrow, lrow, drow, qpad, dopad):
     nseq = lens.shape[0]
     nblk = tok // blk
     shift = rel[0]
 
     def place(b):
-        return pl.multiple_of(((b // per) ^ shift) * (per * blk) + (b % per) * blk, blk)
+        chunk = (b // per) ^ shift
+        half = b % per
+        at = chunk * per + half
+        if halved:
+            at = jnp.where(chunk < 2, at, 4 + (chunk - 2) + 2 * half)
+        return pl.multiple_of(at * blk, blk)
 
     dk[...] = jnp.zeros_like(dk)
     dv[...] = jnp.zeros_like(dv)
@@ -306,14 +535,14 @@
     lax.fori_loop(0, nblk, finish, 0)
 
 
-def attention(lens, rel, cos, sin, seg_start, qt, kt, vt, dot, kn, vn, chunk, maxlen, blk=256):
+def attention(lens, rel, cos, sin, seg_start, qt, kt, vt, dot, kn, vn, chunk, maxlen, halved=False, blk=256):
     width, tok = qt.shape
     nh = width // HD
     wb = maxlen // blk + 1
     vm = pl.BlockSpec(memory_space=pltpu.VMEM)
     sm = pl.BlockSpec(memory_space=pltpu.SMEM)
     return pl.pallas_call(
-        functools.partial(attn_kernel, nh, tok, blk, chunk // blk),
+        functools.partial(attn_kernel, nh, tok, blk, chunk // blk, halved),
         out_shape=(jax.ShapeDtypeStruct((3 * width, tok), BF), jax.ShapeDtypeStruct((width, tok), BF)),
         in_specs=[sm, sm] + [vm] * 9,
         out_specs=(vm, vm),
@@ -338,81 +567,69 @@
     )(lens, rel, cos, sin, seg_start, qt, kt, vt, dot, kn, vn)
 
 
-def post_kernel(prev, final, pos, *refs):
-    gt_ref, na_ref, x_ref, gm_ref, wq, wk, wv, gain = refs[:8]
-    refs = refs[8:]
-    if prev:
-        pw, pb, psmall = refs[:3]
-        refs = refs[3:]
-    g_ref, out_w, bias, small = refs[:4]
-    dw = refs[4] if final else out_w
+def post_kernel(pos, gt_ref, na_ref, gm_ref, wq, wk, wv, gain, shift, g_ref, out_w, bias, small, dw):
     step = pl.program_id(0)
 
     @pl.when(step == 0)
     def _():
-        if prev:
-            dw[...] = pw[...]
-            bias[...] = pb[...]
-            small[...] = psmall[...]
-        else:
-            dw[...] = jnp.zeros_like(dw)
-            bias[...] = jnp.zeros_like(bias)
-            small[...] = jnp.zeros_like(small)
+        dw[...] = jnp.zeros_like(dw)
+        bias[...] = jnp.zeros_like(bias)
+        small[...] = jnp.zeros_like(small)
 
     gt = gt_ref[...]
+    na = na_ref[...]
     w = wq.shape[1]
-    normed, _unused = norm_parts(x_ref[...])
     scale = gain[...].astype(F32)
     gn = gt.T
     r = mm(gn[:, :w], wq[...], NT) + mm(gn[:, w : 2 * w], wk[...], NT) + mm(gn[:, 2 * w :], wv[...], NT)
     g_ref[...] = (r * scale + gm_ref[...].astype(F32)).astype(BF)
-    small[0:1, :] += jnp.sum(r * normed, axis=0, keepdims=True)
+    small[0:1, :] += jnp.sum(r * na.astype(F32), axis=0, keepdims=True)
     small[1:2, :] += jnp.sum(r, axis=0, keepdims=True)
     bias[0:1, :] += jnp.sum(gn.astype(F32), axis=0, keepdims=True)
-    dw[...] += mm(gt, na_ref[...])
-
-    if final:
-
-        @pl.when(step == pl.num_programs(0) - 1)
-        def _():
-            for b in range(dw.shape[1] // 128):
-                out_w[b] = dw[:, b * 128 : (b + 1) * 128].astype(BF)
-
-
-def post(pos, gt, na, x, gm, w_qkv, gain, n, first, prev=None, final=True, tt=512):
-    tok, d = x.shape
+    dw[...] += mm(gt, na)
+
+    @pl.when(step == pl.num_programs(0) - 1)
+    def _():
+        for b in range(dw.shape[1] // 128):
+            out_w[b] = dw[:, b * 128 : (b + 1) * 128].astype(BF)
+        small[0:1, :] = (small[0:1, :] - shift[...].astype(F32) * small[1:2, :]) / scale
+
+
+def post(pos, gt, na, gm, w_qkv, gain, shift, n, tt=512):
+    tok, d = na.shape
     w = d // n
-    off = first // tt
     row = lambda i, p: (i, 0)
     zero = lambda i, p: (0, 0)
     one = pl.Buffered(1)
     const = lambda shape: pl.BlockSpec(shape, zero, pipeline_mode=one)
     wspec = lambda k: pl.BlockSpec((d, w), lambda i, p: (0, k * n + p[0]), pipeline_mode=one)
-    tail = [const((8, 3 * w)), const((8, d))]
-    wout = pl.BlockSpec((d // 128, 3 * w, 128), lambda i, p: (0, 0, 0), pipeline_mode=one) if final else const((3 * w, d))
     grid_spec = pltpu.PrefetchScalarGridSpec(
         num_scalar_prefetch=1,
         grid=(tok // tt,),
         in_specs=[
-            pl.BlockSpec((3 * w, tt), lambda i, p: (0, off + i)),
-            pl.BlockSpec((tt, d), lambda i, p: (off + i, 0)),
+            pl.BlockSpec((3 * w, tt), lambda i, p: (0, i)),
             pl.BlockSpec((tt, d), row),
             pl.BlockSpec((tt, d), row),
             wspec(0),
             wspec(1),
             wspec(2),
             const((1, d)),
-        ]
-        + ([const((3 * w, d))] + tail if prev is not None else []),
-        out_specs=[pl.BlockSpec((tt, d), row), wout] + tail,
-        scratch_shapes=[pltpu.VMEM((3 * w, d), F32)] if final else [],
+            const((1, d)),
+        ],
+        out_specs=[
+            pl.BlockSpec((tt, d), row),
+            pl.BlockSpec((d // 128, 3 * w, 128), lambda i, p: (0, 0, 0), pipeline_mode=one),
+            const((8, 3 * w)),
+            const((8, d)),
+        ],
+        scratch_shapes=[pltpu.VMEM((3 * w, d), F32)],
     )
     return pl.pallas_call(
-        functools.partial(post_kernel, prev is not None, final),
+        post_kernel,
         grid_spec=grid_spec,
         out_shape=(
             jax.ShapeDtypeStruct((tok, d), BF),
-            jax.ShapeDtypeStruct((d // 128, 3 * w, 128), BF) if final else jax.ShapeDtypeStruct((3 * w, d), F32),
+            jax.ShapeDtypeStruct((d // 128, 3 * w, 128), BF),
             jax.ShapeDtypeStruct((8, 3 * w), F32),
             jax.ShapeDtypeStruct((8, d), F32),
         ),
@@ -421,7 +638,7 @@
             flops=12 * tok * d * w, bytes_accessed=8 * tok * d + 6 * tok * w + 18 * d * w, transcendentals=0
         ),
         name="post",
-    )(pos, gt, na, x, gm, w_qkv, w_qkv, w_qkv, gain, *(prev or ()))
+    )(pos, gt, na, gm, w_qkv, w_qkv, w_qkv, gain, shift)
 
 
 def layout(seq_lens, index):
@@ -511,57 +728,52 @@
     bq, bu = rows(b_qkv), rows(b_up)
     lens = lengths[0]
 
-    x_y = head_perm(inputs, 2)
-    x_c = head_perm(inputs, 1)
-    dy_c = head_perm(cotangent, 1)
-    dy_y = head_perm(cotangent, 2)
-    x_a = jnp.concatenate([inputs, x_c], axis=0)
-    dy_a = jnp.concatenate([cotangent, dy_c], axis=0)
-
     lane = jnp.arange(tok, dtype=jnp.int32)
-    index = ((lane // own) ^ j) * own + lane % own
+    half = own // 2
+    far = (lane - 2 * own) // half
+    chunk = jnp.where(lane < 2 * own, lane // own, 2 + (far & 1))
+    offset = jnp.where(lane < 2 * own, lane % own, (far >> 1) * half + lane % half)
+    index = (chunk ^ j) * own + offset
     first, position = layout(lens, index)
     freqs = 10000.0 ** (-(2.0 * jnp.arange(HALF, dtype=F32)) / ROT)
     angle = freqs[:, None] * position.astype(F32)[None, :]
     cos, sin = jnp.cos(angle), jnp.sin(angle)
     seg_start = first[None, :]
 
-    part_a, gm_a, *acc_a = mlp(pos, x_a, dy_a, w_up, w_down, bu, gm, sm, n, final=False)
-    pre_a = proj(pos, x_a, dy_a, w_qkv, bq, w_out, ga, sa, cos, sin, n, tok, 0)
-
-    x_b = jnp.concatenate([x_y, head_perm(x_y, 1)], axis=0)
-    dy_b = jnp.concatenate([dy_y, head_perm(dy_y, 1)], axis=0)
-    part_b, gm_b, dwu, dwd, small, smallf = mlp(pos, x_b, dy_b, w_up, w_down, bu, gm, sm, n, prev=tuple(acc_a))
-    qt, kt, vt, dot, kn, vn, na = proj(
-        pos, x_b, dy_b, w_qkv, bq, w_out, ga, sa, cos, sin, n, tok, 2 * own, prev=tuple(pre_a)
+    g_mlp, na, dy_all, qt, kt, vt, dot, kn, vn, p_own, p_far, dwu, dwd, small, smallf = head_stage(
+        inputs, cotangent, w_up, w_down, w_qkv, w_out, bu, bq, gm, sm, ga, sa, cos, sin, n, 0
     )
-
-    part_y = part_b[:own].astype(F32) + head_perm(part_b[own:], 1).astype(F32)
-    part_0 = part_a[:own].astype(F32) + head_perm(part_a[own:], 1).astype(F32)
-    mlp_sum = part_0 + head_perm(part_y.astype(BF), 2).astype(F32)
-
-    up_down = jnp.concatenate([dwu.reshape(8, 128, d), dwd.reshape(8, 128, d)], axis=1)
+    mlp_sum = p_own.astype(F32) + head_perm(p_far, 2).astype(F32)
+
+    up_down = jnp.concatenate([dwu, dwd], axis=1)
     up_down = dp_scatter(up_down, i)
     grad_w_up = up_down[:128]
     grad_w_down = to_owner(up_down[128:].astype(BF), i, j).astype(F32)
     slots = jnp.where(jnp.arange(4)[:, None] == j, smallf[0:1], 0.0)
     early = sum_all(jnp.concatenate([small[:2], small[2:3] * 0.25, slots, jnp.zeros((1, d), F32)], axis=0))
 
-    gt, ctx = attention(lens, pos, cos, sin, seg_start, qt, kt, vt, dot, kn, vn, own, tok // 2)
-
-    got = [ctx[:, :own]] + [head_perm(ctx[:, r * own : (r + 1) * own], r) for r in (1, 2, 3)]
+    gt, ctx = attention(lens, pos, cos, sin, seg_start, qt, kt, vt, dot, kn, vn, own, tok // 2, halved=True)
+
+    far_y = [ctx[:, 2 * own : 2 * own + half], ctx[:, 3 * own : 3 * own + half]]
+    far_d = [ctx[:, 2 * own + half : 3 * own], ctx[:, 3 * own + half :]]
+    got = [
+        ctx[:, :own],
+        head_perm(ctx[:, own : 2 * own], 1),
+        head_perm(jnp.concatenate(far_y, axis=1), 2),
+        head_perm(jnp.concatenate(far_d, axis=1), 3),
+    ]
     w_rel = w_out.reshape(n, w, d)
     attn_part = mm(jnp.concatenate(got, axis=0), jnp.concatenate([pick(w_rel, j ^ r) for r in range(n)], axis=0), TN)
     bias = b_out.astype(F32) + b_down.astype(F32)
     output = (inputs.astype(F32) + attn_part + mlp_sum + bias).astype(BF)
 
-    dw_out = mm(ctx[:, : 2 * own], dy_a) + mm(ctx[:, 2 * own :], dy_b)
-
-    g_b, dwq, bias_b, small_b = post(pos, gt, na, x_b, gm_b, w_qkv, ga, n, 2 * own, final=False)
-    g_y = g_b[:own].astype(F32) + head_perm(g_b[own:], 1).astype(F32)
-    g_y = head_perm(g_y.astype(BF), 2)
-    g_a, dwq, bias_q, small_q = post(pos, gt, na, x_a, gm_a, w_qkv, ga, n, 0, prev=(dwq, bias_b, small_b))
-    g_sum = g_a[:own].astype(F32) + head_perm(g_a[own:], 1).astype(F32) + g_y.astype(F32)
+    dw_out = mm(ctx, dy_all)
+
+    g, dwq, bias_q, small_q = post(pos, gt, na, g_mlp, w_qkv, ga, sa, n)
+    g_far = jnp.concatenate([g[2 * own : 2 * own + half], g[3 * own : 3 * own + half]], axis=0).astype(F32)
+    g_dia = jnp.concatenate([g[2 * own + half : 3 * own], g[3 * own + half :]], axis=0)
+    g_y = head_perm((g_far + head_perm(g_dia, 1).astype(F32)).astype(BF), 2)
+    g_sum = g[:own].astype(F32) + head_perm(g[own : 2 * own], 1).astype(F32) + g_y.astype(F32)
 
     qkv = dp_scatter(dwq, i)
     grad_w_qkv = qkv_owner(qkv.astype(BF).reshape(3, w, 128), j).astype(F32).T
@@ -607,7 +819,7 @@
     gt, ctx = attention(
         lens, jnp.zeros((1,), jnp.int32), cos, sin, first[None, :], qt, kt, vt, dot, kn, vn, own, tok // 2
     )
-    total, dwq, bias_q, small_q = post(pos, gt, na, x_all, g_mlp, w_qkv, ga, n, 0)
+    total, dwq, bias_q, small_q = post(pos, gt, na, g_mlp, w_qkv, ga, sa, n)
     attn_part = mm(ctx, lax.dynamic_slice_in_dim(w_out, j * w, w, 0), TN)
     bias = b_out.astype(F32) + b_down.astype(F32)
     output = inputs.astype(F32) + over_head((attn_part + part.astype(F32)).astype(BF)).astype(F32) + bias

time: 430 us -> 370 us (0.86)
  waiting for transfers between devices: 93.9 us -> 58.6 us
  starting transfers between devices: 105 us -> 95.9 us
  local copies, waits for them, and re-layouts: 46.1 us -> 37.5 us
    ppermute x18, starting transfers between devices: 56.8 us -> 20.8 us  [dp_perm(): return lax.ppermute(v, 'dp', [(k, k ^ bit) for k in range(8)])]
    ppermute x8, starting transfers between devices: 28.3 us -> 59.7 us  [to_owner(): got.append(lax.ppermute(pick(cols, i % 4 ^ r, 1), ('dp', 'head'), pairs))]
    ppermute x19 -> x11, waiting for transfers between devices: 47.2 us -> 16.9 us  [head_perm(): return lax.ppermute(v, 'head', [(k, k ^ bit) for k in range(4)])]
    ppermute x3, waiting for transfers between devices: 12.1 us -> 0.01 us  [qkv_owner(): got.append(lax.ppermute(pick(v, slot), 'head', pairs))]
    concatenate x4 -> x0, local copies, waits for them, and re-layouts: 9.1 us -> none  [the longest x1 2.29 us: fast_body(): x_a = jnp.concatenate([inputs, x_c], axis=0)]
    ppermute x18, waiting for transfers between devices: 34.6 us -> 39.6 us  [dp_perm(): return lax.ppermute(v, 'dp', [(k, k ^ bit) for k in range(8)])]
    unnamed x82 -> x96, local copies, waits for them, and re-layouts: 12 us -> 7.24 us
    ppermute x19 -> x11, starting transfers between devices: 15.7 us -> 11.9 us  [head_perm(): return lax.ppermute(v, 'head', [(k, k ^ bit) for k in range(4)])]
  transfers between devices with their start and end apart: 48 -> 40, of which waited for: 11 -> 14; matrix products, arithmetic and copies ran while one was open for 16% -> 14% of each run, Pallas kernels for 12% -> 0%
where the time goes in v2:
time: 370 us; the launch traced here: 367 us
  Pallas kernels  132 us (36%)
  starting transfers between devices  95.9 us (26%)
  waiting for transfers between devices  58.6 us (16%)
  local copies, waits for them, and re-layouts  37.5 us (10%)
  other arithmetic  34.3 us (9%)
  matrix products  7.18 us (2%)
    pallas_call x1, Pallas kernels, head_stage(): pl.pallas_call(functools.partial(head_kernel, w // HD), grid=(n,), in_spe...  64.7 us
    ppermute x8, starting transfers between devices, to_owner(): got.append(lax.ppermute(pick(cols, i % 4 ^ r, 1), ('dp', 'head'), pairs))  59.7 us
    pallas_call x1, Pallas kernels, attention(): pl.pallas_call(functools.partial(attn_kernel, nh, tok, blk, chunk // blk,...  54.5 us
    ppermute x18, waiting for transfers between devices, dp_perm(): return lax.ppermute(v, 'dp', [(k, k ^ bit) for k in range(8)])  39.6 us
    ppermute x18, starting transfers between devices, dp_perm(): return lax.ppermute(v, 'dp', [(k, k ^ bit) for k in range(8)])  20.8 us
    ppermute x11, waiting for transfers between devices, head_perm(): return lax.ppermute(v, 'head', [(k, k ^ bit) for k in range(4)])  16.9 us
    pallas_call x1, Pallas kernels, post(): pl.pallas_call(post_kernel, grid_spec=grid_spec, out_shape=(jax.ShapeDtyp...  13 us
    ppermute x11, starting transfers between devices, head_perm(): return lax.ppermute(v, 'head', [(k, k ^ bit) for k in range(4)])  11.9 us
  transfers between devices with their start and end apart: 40, of which 14 were waited for; matrix products, arithmetic and copies ran while one was open for 14% of the time, Pallas kernels for 0%

profile of v2, /device:TPU:7, one launch (start us, length us, event | category | flops | bytes accessed | tf_op | source)
XLA Modules:
  0.0 367.1 jit_solution(8045006443812722816)
XLA Ops:
  2.7 2.0 subtract_convert_fusion
  4.7 2.6 compare_select_fusion.2.seg_start
  7.3 1.3 reshape.330.bu
  8.6 1.3 reshape.331.bq
  9.9 1.3 reshape.332.gain_m
  11.2 1.3 reshape.333.shift_m
  12.5 1.3 reshape.334.gain_a.gain
  13.7 1.3 reshape.335.shift_a.shift
  16.0 64.7 %head_stage.1 = (bf16[2048,1024]{1,0:T(8,128)(2,1)}, bf16[2048,1024]{1,0:T(8,128)(2,1)}, bf16[2048,1024]{1,0:T(8,128)(2,1)}, bf16[256,2048]{1,0:T(8,128)(2,1)}, ...) custom-call(bf16[512,1024]{1,0:T(8,128)(2,1)} %x_hbm.1, ...), custom_call_target="tpu_custom_call" | custom-call | flops 31138512896 | bytes 33554432 | tf_op jit(solution)/shard_map/head_stage/pallas_call | solution.py:374
  80.7 54.5 %attention.1 = (bf16[768,2048]{1,0:T(8,128)(2,1)}, bf16[256,2048]{1,0:T(8,128)(2,1)}) custom-call(s32[4]{0:T(128)} %bitcast.155, s32[1]{0:T(128)} %bitcast.1.rel.pos, f32[8,2048]{1,0:T(8,128)} %get-tuple-element.126.cos, f32[8,2048]{1,0:T(8,128)} %get-tuple-element.125.sin, s32[1,2048]{1,0:T(1,128)} %compare_select_fusion.2.seg_start, ...), custom_call_target="tpu_custom_call" | custom-call | flops 10737418240 | bytes 10485760 | tf_op jit(solution)/shard_map/attention/pallas_call | solution.py:544
  135.1 13.0 %post.1 = (bf16[2048,1024]{1,0:T(8,128)(2,1)}, bf16[8,768,128]{2,1,0:T(8,128)(2,1)}, f32[8,768]{1,0:T(8,128)}, f32[8,1024]{1,0:T(8,128)}) custom-call(s32[1]{0:T(128)} %bitcast.1.rel.pos, bf16[768,2048]{1,0:T(8,128)(2,1)} %get-tuple-element.44.gt_ref, bf16[2048,1024]{1,0:T(8,128)(2,1)} %get-tuple-element.45.na_ref, ...), custom_call_target="tpu_custom_call" | custom-call | flops 6442450944 | bytes 24641536 | tf_op jit(solution)/shard_map/post/pallas_call | solution.py:627
  155.3 2.1 dynamic-slice_bitcast_fusion.1
  157.4 3.5 convolution_convert_fusion
  162.4 1.5 collective-permute-start.24
  165.7 3.0 fusion.78
  170.1 2.0 copy-done
  172.2 1.5 dynamic-slice_bitcast_fusion
  173.7 1.3 convert_add_fusion.5
  175.0 1.3 dynamic-slice_bitcast_fusion.8
  183.9 1.2 collective-permute-done.9
  186.0 2.8 collective-permute-start.16
  189.5 2.3 slice.102
  193.0 2.9 collective-permute-start.27
  197.2 4.6 %collective-permute-start.5 = (bf16[512,1024]{1,0:T(8,128)(2,1)}, bf16[512,1024]{1,0:T(8,128)(2,1)}, u32[]{:S(2)}, u32[]{:S(2)}) collective-permute-start(bf16[512,1024]{1,0:T(8,128)(2,1)} %pad_maximum_fusion.1), channel_id=1, source_target_pairs={{0,1},{1,0},{2,3},{3,2},{4,5},{5,4},{6,7},{7,6},{8,9},{9,8},{10,11... | collective-permute-start | bytes 3145736 | tf_op jit(solution)/shard_map/ppermute | solution.py:662
  202.4 7.4 %collective-permute-start.28 = (bf16[32,256]{1,0:T(8,128)(2,1)S(1)}, bf16[32,256]{1,0:T(8,128)(2,1)S(1)}, u32[]{:S(2)}, u32[]{:S(2)}) collective-permute-start(bf16[32,256]{1,0:T(8,128)(2,1)S(1)} %bitcast.145), channel_id=1, source_target_pairs={{0,3},{1,11},{2,19},{3,27},{4,2},{5,10},{6,18},{7,26},{8,1},{9,9},... | collective-permute-start | bytes 49160 | tf_op jit(solution)/shard_map/ppermute | solution.py:702
  210.0 3.7 %collective-permute-start.30 = (bf16[32,256]{1,0:T(8,128)(2,1)S(1)}, bf16[32,256]{1,0:T(8,128)(2,1)S(1)}, u32[]{:S(2)}, u32[]{:S(2)}) collective-permute-start(bf16[32,256]{1,0:T(8,128)(2,1)S(1)} %bitcast.143), channel_id=1, source_target_pairs={{0,1},{1,9},{2,17},{3,25},{4,0},{5,8},{6,16},{7,24},{8,3},{9,11},{... | collective-permute-start | bytes 49160 | tf_op jit(solution)/shard_map/ppermute | solution.py:702
  213.7 1.6 fusion.77
  216.1 38.5 %collective-permute-start.31 = (bf16[32,256]{1,0:T(8,128)(2,1)S(1)}, bf16[32,256]{1,0:T(8,128)(2,1)}, u32[]{:S(2)}, u32[]{:S(2)}) collective-permute-start(bf16[32,256]{1,0:T(8,128)(2,1)S(1)} %bitcast.142), channel_id=1, source_target_pairs={{0,0},{1,8},{2,16},{3,24},{4,1},{5,9},{6,17},{7,25},{8,2},{9,10},{... | collective-permute-start | bytes 49160 | tf_op jit(solution)/shard_map/ppermute | solution.py:702
  257.6 4.1 %collective-permute-done.20 = bf16[768,128]{1,0:T(8,128)(2,1)} collective-permute-done((bf16[768,128]{1,0:T(8,128)(2,1)}, bf16[768,128]{1,0:T(8,128)(2,1)}, u32[]{:S(2)}, u32[]{:S(2)}) %collective-permute-start.20) | collective-permute-done | bytes 196640 | tf_op jit(solution)/shard_map/ppermute | solution.py:666
  261.6 7.5 %collective-permute-start.18 = (bf16[768,128]{1,0:T(8,128)(2,1)}, bf16[768,128]{1,0:T(8,128)(2,1)S(1)}, u32[]{:S(2)}, u32[]{:S(2)}) collective-permute-start(bf16[768,128]{1,0:T(8,128)(2,1)} %get-tuple-element.95), channel_id=1, source_target_pairs={{0,8},{4,12},{8,0},{12,4},{16,24},{20,28},{24,16},{28,20},{1,9},{5... | collective-permute-start | bytes 589832 | tf_op jit(solution)/shard_map/ppermute | solution.py:666
  270.5 2.5 collective-permute-done.19
  273.0 1.7 collective-permute-start.2
  274.7 3.2 collective-permute-done.18
  278.4 1.2 fusion.35
  279.6 1.7 collective-permute-done.2
  283.2 2.6 add_convert_fusion
  285.8 1.5 collective-permute-done.1
  288.3 2.7 collective-permute-start.21
  292.0 3.7 fusion.11
  296.6 3.3 fusion.75
  300.1 2.6 collective-permute-start.35
  303.7 12.4 %collective-permute-done.6 = bf16[512,1024]{1,0:T(8,128)(2,1)S(1)} collective-permute-done((bf16[512,1024]{1,0:T(8,128)(2,1)}, bf16[512,1024]{1,0:T(8,128)(2,1)S(1)}, u32[]{:S(2)}, u32[]{:S(2)}) %collective-permute-start.6) | collective-permute-done | bytes 1048608 | tf_op jit(solution)/shard_map/ppermute | solution.py:662
  316.1 2.1 fusion.36
  318.2 28.0 %collective-permute-done.34 = bf16[256,1024]{1,0:T(8,128)(2,1)S(1)} collective-permute-done((bf16[256,1024]{1,0:T(8,128)(2,1)S(1)}, bf16[256,1024]{1,0:T(8,128)(2,1)S(1)}, u32[]{:S(2)}, u32[]{:S(2)}) %collective-permute-start.34) | collective-permute-done | bytes 524320 | tf_op jit(solution)/shard_map/ppermute | solution.py:666
  350.0 3.7 collective-permute-start.36
  354.3 2.7 collective-permute-start.38
  357.1 3.1 collective-permute-start.39
  360.2 3.6 fusion.7
  (217 shorter events, 46.3 us)
Async XLA Ops:
  135.1 22.3 %copy-start.11 = (bf16[256,2048]{1,0:T(8,128)(2,1)S(1)}, bf16[256,2048]{1,0:T(8,128)(2,1)}, u32[]{:S(2)}) copy-start(bf16[256,2048]{1,0:T(8,128)(2,1)} %get-tuple-element.41) | copy-start | bytes 3145732
  151.1 26.9 %collective-permute-start.7 = (f32[8,1024]{1,0:T(8,128)}, f32[8,1024]{1,0:T(8,128)}, u32[]{:S(2)}, u32[]{:S(2)}) collective-permute-start(f32[8,1024]{1,0:T(8,128)} %pad_maximum_fusion.4), channel_id=1, source_target_pairs={{0,1},{1,0},{2,3},{3,2},{4,5},{5,4},{6,7},{7,6},{8,9},{9,8},{10,11... | collective-permute-start | bytes 98312 | tf_op jit(solution)/shard_map/ppermute | solution.py:662
  154.8 21.6 %collective-permute-start.12 = (f32[8,1024]{1,0:T(8,128)}, f32[8,1024]{1,0:T(8,128)}, u32[]{:S(2)}, u32[]{:S(2)}) collective-permute-start(f32[8,1024]{1,0:T(8,128)} %maximum_maximum_fusion), channel_id=1, source_target_pairs={{0,1},{1,0},{2,3},{3,2},{4,5},{5,4},{6,7},{7,6},{8,9},{9,8},{10,11... | collective-permute-start | bytes 98312 | tf_op jit(solution)/shard_map/ppermute | solution.py:662
  157.4 52.6 %collective-permute-start.17 = (bf16[4,768,128]{2,1,0:T(8,128)(2,1)}, bf16[4,768,128]{2,1,0:T(8,128)(2,1)}, u32[]{:S(2)}, u32[]{:S(2)}) collective-permute-start(bf16[4,768,128]{2,1,0:T(8,128)(2,1)} %dynamic-slice_bitcast_fusion.1), channel_id=1, source_target_pairs={{0,4},{4,0},{8,12},{12,8},{16,20},{20,16},{24,28},{28,24},{1,5},{5... | collective-permute-start | bytes 2359304 | tf_op jit(solution)/shard_map/ppermute | solution.py:666
  162.4 29.5 %collective-permute-start.24 = (bf16[4,32,1024]{2,1,0:T(8,128)(2,1)}, bf16[4,32,1024]{2,1,0:T(8,128)(2,1)}, u32[]{:S(2)}, u32[]{:S(2)}) collective-permute-start(bf16[4,32,1024]{2,1,0:T(8,128)(2,1)} %dynamic-slice_bitcast_fusion.9), channel_id=1, source_target_pairs={{0,4},{4,0},{8,12},{12,8},{16,20},{20,16},{24,28},{28,24},{1,5},{5... | collective-permute-start | bytes 786440 | tf_op jit(solution)/shard_map/ppermute | solution.py:666
  177.2 3.2 collective-permute-start.13
  178.7 3.2 collective-permute-start.8
  180.4 2.8 collective-permute-start.14
  182.0 3.2 collective-permute-start.9
  183.2 2.8 collective-permute-start.15
  185.1 6.7 %collective-permute-start.10 = (f32[8,1024]{1,0:T(8,128)S(1)}, f32[8,1024]{1,0:T(8,128)S(1)}, u32[]{:S(2)}, u32[]{:S(2)}) collective-permute-start(f32[8,1024]{1,0:T(8,128)S(1)} %add.341), channel_id=1, source_target_pairs={{0,8},{4,12},{8,0},{12,4},{16,24},{20,28},{24,16},{28,20},{1,9},{5... | collective-permute-start | bytes 98312 | tf_op jit(solution)/shard_map/ppermute | solution.py:666
  186.0 5.9 %collective-permute-start.16 = (f32[8,1024]{1,0:T(8,128)S(1)}, f32[8,1024]{1,0:T(8,128)S(1)}, u32[]{:S(2)}, u32[]{:S(2)}) collective-permute-start(f32[8,1024]{1,0:T(8,128)S(1)} %add.347), channel_id=1, source_target_pairs={{0,16},{4,20},{8,24},{12,28},{16,0},{20,4},{24,8},{28,12},{1,17},{... | collective-permute-start | bytes 98312 | tf_op jit(solution)/shard_map/ppermute | solution.py:666
  191.8 5.4 %collective-permute-start.11 = (f32[8,1024]{1,0:T(8,128)S(1)}, f32[8,1024]{1,0:T(8,128)S(1)}, u32[]{:S(2)}, u32[]{:S(2)}) collective-permute-start(f32[8,1024]{1,0:T(8,128)S(1)} %add.342), channel_id=1, source_target_pairs={{0,16},{4,20},{8,24},{12,28},{16,0},{20,4},{24,8},{28,12},{1,17},{... | collective-permute-start | bytes 98312 | tf_op jit(solution)/shard_map/ppermute | solution.py:666
  193.0 8.9 %collective-permute-start.27 = (bf16[32,1024]{1,0:T(8,128)(2,1)S(1)}, bf16[32,1024]{1,0:T(8,128)(2,1)S(1)}, u32[]{:S(2)}, u32[]{:S(2)}) collective-permute-start(bf16[32,1024]{1,0:T(8,128)(2,1)S(1)} %get-tuple-element.107), channel_id=1, source_target_pairs={{0,24},{4,28},{8,16},{12,20},{16,8},{20,12},{24,0},{28,4},{1,25},{... | collective-permute-start | bytes 196616 | tf_op jit(solution)/shard_map/ppermute | solution.py:666
  195.9 6.3 %collective-permute-start.26 = (bf16[32,1024]{1,0:T(8,128)(2,1)S(1)}, bf16[32,1024]{1,0:T(8,128)(2,1)S(1)}, u32[]{:S(2)}, u32[]{:S(2)}) collective-permute-start(bf16[32,1024]{1,0:T(8,128)(2,1)S(1)} %get-tuple-element.108), channel_id=1, source_target_pairs={{0,16},{4,20},{8,24},{12,28},{16,0},{20,4},{24,8},{28,12},{1,17},{... | collective-permute-start | bytes 196616 | tf_op jit(solution)/shard_map/ppermute | solution.py:666
  195.9 6.3 %collective-permute-start.25 = (bf16[32,1024]{1,0:T(8,128)(2,1)S(1)}, bf16[32,1024]{1,0:T(8,128)(2,1)S(1)}, u32[]{:S(2)}, u32[]{:S(2)}) collective-permute-start(bf16[32,1024]{1,0:T(8,128)(2,1)S(1)} %get-tuple-element.106), channel_id=1, source_target_pairs={{0,8},{4,12},{8,0},{12,4},{16,24},{20,28},{24,16},{28,20},{1,9},{5... | collective-permute-start | bytes 196616 | tf_op jit(solution)/shard_map/ppermute | solution.py:666
  197.2 169.3 %copy-start.36 = (f32[1,1024]{1,0:T(1,128)}, f32[1,1024]{1,0:T(1,128)S(1)}, u32[]{:S(2)}) copy-start(f32[1,1024]{1,0:T(1,128)S(1)} %get-tuple-element.120) | copy-start | bytes 12292
  197.2 85.2 %collective-permute-start.5 = (bf16[512,1024]{1,0:T(8,128)(2,1)}, bf16[512,1024]{1,0:T(8,128)(2,1)}, u32[]{:S(2)}, u32[]{:S(2)}) collective-permute-start(bf16[512,1024]{1,0:T(8,128)(2,1)} %pad_maximum_fusion.1), channel_id=1, source_target_pairs={{0,1},{1,0},{2,3},{3,2},{4,5},{5,4},{6,7},{7,6},{8,9},{9,8},{10,11... | collective-permute-start | bytes 3145736 | tf_op jit(solution)/shard_map/ppermute | solution.py:662
  201.9 94.7 %collective-permute-start.32 = (bf16[4,256,1024]{2,1,0:T(8,128)(2,1)}, bf16[4,256,1024]{2,1,0:T(8,128)(2,1)}, u32[]{:S(2)}, u32[]{:S(2)}) collective-permute-start(bf16[4,256,1024]{2,1,0:T(8,128)(2,1)} %dynamic-slice_bitcast_fusion), channel_id=1, source_target_pairs={{0,4},{4,0},{8,12},{12,8},{16,20},{20,16},{24,28},{28,24},{1,5},{5... | collective-permute-start | bytes 6291464 | tf_op jit(solution)/shard_map/ppermute | solution.py:666
  202.4 13.7 %collective-permute-start.28 = (bf16[32,256]{1,0:T(8,128)(2,1)S(1)}, bf16[32,256]{1,0:T(8,128)(2,1)S(1)}, u32[]{:S(2)}, u32[]{:S(2)}) collective-permute-start(bf16[32,256]{1,0:T(8,128)(2,1)S(1)} %bitcast.145), channel_id=1, source_target_pairs={{0,3},{1,11},{2,19},{3,27},{4,2},{5,10},{6,18},{7,26},{8,1},{9,9},... | collective-permute-start | bytes 49160 | tf_op jit(solution)/shard_map/ppermute | solution.py:702
  209.8 6.3 %collective-permute-start.29 = (bf16[32,256]{1,0:T(8,128)(2,1)S(1)}, bf16[32,256]{1,0:T(8,128)(2,1)S(1)}, u32[]{:S(2)}, u32[]{:S(2)}) collective-permute-start(bf16[32,256]{1,0:T(8,128)(2,1)S(1)} %bitcast.144), channel_id=1, source_target_pairs={{0,2},{1,10},{2,18},{3,26},{4,3},{5,11},{6,19},{7,27},{8,0},{9,8},... | collective-permute-start | bytes 49160 | tf_op jit(solution)/shard_map/ppermute | solution.py:702
  210.0 63.0 %copy-start.21 = (bf16[256,512]{1,0:T(8,128)(2,1)S(1)}, bf16[256,512]{1,0:T(8,128)(2,1)}, u32[]{:S(2)}) copy-start(bf16[256,512]{1,0:T(8,128)(2,1)} %pad_maximum_fusion.3) | copy-start | bytes 786436
  210.0 44.6 %collective-permute-start.30 = (bf16[32,256]{1,0:T(8,128)(2,1)S(1)}, bf16[32,256]{1,0:T(8,128)(2,1)S(1)}, u32[]{:S(2)}, u32[]{:S(2)}) collective-permute-start(bf16[32,256]{1,0:T(8,128)(2,1)S(1)} %bitcast.143), channel_id=1, source_target_pairs={{0,1},{1,9},{2,17},{3,25},{4,0},{5,8},{6,16},{7,24},{8,3},{9,11},{... | collective-permute-start | bytes 49160 | tf_op jit(solution)/shard_map/ppermute | solution.py:702
  215.3 67.9 %copy-start.7 = (bf16[256,1024]{1,0:T(8,128)(2,1)S(1)}, bf16[256,1024]{1,0:T(8,128)(2,1)}, u32[]{:S(2)}) copy-start(bf16[256,1024]{1,0:T(8,128)(2,1)} %get-tuple-element.78) | copy-start | bytes 1572868
  216.1 72.2 %collective-permute-start.3 = (bf16[512,1024]{1,0:T(8,128)(2,1)}, bf16[512,1024]{1,0:T(8,128)(2,1)}, u32[]{:S(2)}, u32[]{:S(2)}) collective-permute-start(bf16[512,1024]{1,0:T(8,128)(2,1)} %get-tuple-element.43), channel_id=1, source_target_pairs={{0,2},{1,3},{2,0},{3,1},{4,6},{5,7},{6,4},{7,5},{8,10},{9,11},{10,... | collective-permute-start | bytes 3145736 | tf_op jit(solution)/shard_map/ppermute | solution.py:662
  216.1 41.4 %collective-permute-start.31 = (bf16[32,256]{1,0:T(8,128)(2,1)S(1)}, bf16[32,256]{1,0:T(8,128)(2,1)}, u32[]{:S(2)}, u32[]{:S(2)}) collective-permute-start(bf16[32,256]{1,0:T(8,128)(2,1)S(1)} %bitcast.142), channel_id=1, source_target_pairs={{0,0},{1,8},{2,16},{3,24},{4,1},{5,9},{6,17},{7,25},{8,2},{9,10},{... | collective-permute-start | bytes 49160 | tf_op jit(solution)/shard_map/ppermute | solution.py:702
  254.6 7.0 %collective-permute-start.20 = (bf16[768,128]{1,0:T(8,128)(2,1)}, bf16[768,128]{1,0:T(8,128)(2,1)}, u32[]{:S(2)}, u32[]{:S(2)}) collective-permute-start(bf16[768,128]{1,0:T(8,128)(2,1)} %get-tuple-element.96), channel_id=1, source_target_pairs={{0,24},{4,28},{8,16},{12,20},{16,8},{20,12},{24,0},{28,4},{1,25},{... | collective-permute-start | bytes 589832 | tf_op jit(solution)/shard_map/ppermute | solution.py:666
  255.9 27.3 %copy-start.8 = (bf16[256,1024]{1,0:T(8,128)(2,1)S(1)}, bf16[256,1024]{1,0:T(8,128)(2,1)}, u32[]{:S(2)}) copy-start(bf16[256,1024]{1,0:T(8,128)(2,1)} %get-tuple-element.81) | copy-start | bytes 1572868
  257.6 15.4 %collective-permute-start.19 = (bf16[768,128]{1,0:T(8,128)(2,1)}, bf16[768,128]{1,0:T(8,128)(2,1)S(1)}, u32[]{:S(2)}, u32[]{:S(2)}) collective-permute-start(bf16[768,128]{1,0:T(8,128)(2,1)} %get-tuple-element.97), channel_id=1, source_target_pairs={{0,16},{4,20},{8,24},{12,28},{16,0},{20,4},{24,8},{28,12},{1,17},{... | collective-permute-start | bytes 589832 | tf_op jit(solution)/shard_map/ppermute | solution.py:666
  261.6 16.2 %collective-permute-start.18 = (bf16[768,128]{1,0:T(8,128)(2,1)}, bf16[768,128]{1,0:T(8,128)(2,1)S(1)}, u32[]{:S(2)}, u32[]{:S(2)}) collective-permute-start(bf16[768,128]{1,0:T(8,128)(2,1)} %get-tuple-element.95), channel_id=1, source_target_pairs={{0,8},{4,12},{8,0},{12,4},{16,24},{20,28},{24,16},{28,20},{1,9},{5... | collective-permute-start | bytes 589832 | tf_op jit(solution)/shard_map/ppermute | solution.py:666
  273.0 8.4 %collective-permute-start.2 = (bf16[256,512]{1,0:T(8,128)(2,1)S(1)}, bf16[256,512]{1,0:T(8,128)(2,1)S(1)}, u32[]{:S(2)}, u32[]{:S(2)}) collective-permute-start(bf16[256,512]{1,0:T(8,128)(2,1)S(1)} %copy-done.21), channel_id=1, source_target_pairs={{0,3},{1,2},{2,1},{3,0},{4,7},{5,6},{6,5},{7,4},{8,11},{9,10},{10,... | collective-permute-start | bytes 786440 | tf_op jit(solution)/shard_map/ppermute | solution.py:662
  277.8 9.5 %collective-permute-start.1 = (bf16[256,512]{1,0:T(8,128)(2,1)}, bf16[256,512]{1,0:T(8,128)(2,1)S(1)}, u32[]{:S(2)}, u32[]{:S(2)}) collective-permute-start(bf16[256,512]{1,0:T(8,128)(2,1)} %pad_maximum_fusion.2), channel_id=1, source_target_pairs={{0,2},{1,3},{2,0},{3,1},{4,6},{5,7},{6,4},{7,5},{8,10},{9,11},{10,... | collective-permute-start | bytes 786440 | tf_op jit(solution)/shard_map/ppermute | solution.py:662
  278.4 13.6 %copy-start.22 = (bf16[256,512]{1,0:T(8,128)(2,1)S(1)}, bf16[256,512]{1,0:T(8,128)(2,1)}, u32[]{:S(2)}) copy-start(bf16[256,512]{1,0:T(8,128)(2,1)} %get-tuple-element.89) | copy-start | bytes 786436
  281.4 6.9 %collective-permute-start = (bf16[256,512]{1,0:T(8,128)(2,1)}, bf16[256,512]{1,0:T(8,128)(2,1)S(1)}, u32[]{:S(2)}, u32[]{:S(2)}) collective-permute-start(bf16[256,512]{1,0:T(8,128)(2,1)} %get-tuple-element.90), channel_id=1, source_target_pairs={{0,1},{1,0},{2,3},{3,2},{4,5},{5,4},{6,7},{7,6},{8,9},{9,8},{10,11... | collective-permute-start | bytes 786440 | tf_op jit(solution)/shard_map/ppermute | solution.py:662
  282.5 8.5 %collective-permute-start.23 = (bf16[256,128]{1,0:T(8,128)(2,1)S(1)}, bf16[256,128]{1,0:T(8,128)(2,1)S(1)}, u32[]{:S(2)}, u32[]{:S(2)}) collective-permute-start(bf16[256,128]{1,0:T(8,128)(2,1)S(1)} %get-tuple-element.110), channel_id=1, source_target_pairs={{2,0},{1,1},{0,2},{3,3},{6,4},{5,5},{4,6},{7,7},{10,8},{9,9},{8,10... | collective-permute-start | bytes 196616 | tf_op jit(solution)/shard_map/ppermute | solution.py:713
  287.3 16.4 %collective-permute-start.4 = (bf16[512,1024]{1,0:T(8,128)(2,1)}, bf16[512,1024]{1,0:T(8,128)(2,1)S(1)}, u32[]{:S(2)}, u32[]{:S(2)}) collective-permute-start(bf16[512,1024]{1,0:T(8,128)(2,1)} %slice.102), channel_id=1, source_target_pairs={{0,1},{1,0},{2,3},{3,2},{4,5},{5,4},{6,7},{7,6},{8,9},{9,8},{10,11... | collective-permute-start | bytes 3145736 | tf_op jit(solution)/shard_map/ppermute | solution.py:662
  288.2 7.4 %collective-permute-start.22 = (bf16[256,128]{1,0:T(8,128)(2,1)S(1)}, bf16[256,128]{1,0:T(8,128)(2,1)S(1)}, u32[]{:S(2)}, u32[]{:S(2)}) collective-permute-start(bf16[256,128]{1,0:T(8,128)(2,1)S(1)} %get-tuple-element.111), channel_id=1, source_target_pairs={{1,0},{0,1},{3,2},{2,3},{5,4},{4,5},{7,6},{6,7},{9,8},{8,9},{11,10... | collective-permute-start | bytes 196616 | tf_op jit(solution)/shard_map/ppermute | solution.py:713
  288.3 7.4 %collective-permute-start.21 = (bf16[256,128]{1,0:T(8,128)(2,1)S(1)}, bf16[256,128]{1,0:T(8,128)(2,1)S(1)}, u32[]{:S(2)}, u32[]{:S(2)}) collective-permute-start(bf16[256,128]{1,0:T(8,128)(2,1)S(1)} %get-tuple-element.109), channel_id=1, source_target_pairs={{0,0},{3,1},{2,2},{1,3},{4,4},{7,5},{6,6},{5,7},{8,8},{11,9},{10,1... | collective-permute-start | bytes 196616 | tf_op jit(solution)/shard_map/ppermute | solution.py:713
  291.0 25.0 %collective-permute-start.6 = (bf16[512,1024]{1,0:T(8,128)(2,1)}, bf16[512,1024]{1,0:T(8,128)(2,1)S(1)}, u32[]{:S(2)}, u32[]{:S(2)}) collective-permute-start(bf16[512,1024]{1,0:T(8,128)(2,1)} %add_convert_fusion), channel_id=1, source_target_pairs={{0,2},{1,3},{2,0},{3,1},{4,6},{5,7},{6,4},{7,5},{8,10},{9,11},{10,... | collective-permute-start | bytes 3145736 | tf_op jit(solution)/shard_map/ppermute | solution.py:662
  299.9 16.1 %copy-start.34 = (f32[512]{0:T(512)S(1)}, f32[512]{0:T(512)}, u32[]{:S(2)}) copy-start(f32[512]{0:T(512)} %copy-done.33) | copy-start | bytes 6148
  299.9 16.1 %copy-start.35 = (f32[512]{0:T(512)S(1)}, f32[512]{0:T(512)}, u32[]{:S(2)}) copy-start(f32[512]{0:T(512)} %add_rsqrt_fusion) | copy-start | bytes 6148
  300.1 18.1 %collective-permute-start.35 = (bf16[256,1024]{1,0:T(8,128)(2,1)S(1)}, bf16[256,1024]{1,0:T(8,128)(2,1)S(1)}, u32[]{:S(2)}, u32[]{:S(2)}) collective-permute-start(bf16[256,1024]{1,0:T(8,128)(2,1)S(1)} %get-tuple-element.83), channel_id=1, source_target_pairs={{0,24},{4,28},{8,16},{12,20},{16,8},{20,12},{24,0},{28,4},{1,25},{... | collective-permute-start | bytes 1572872 | tf_op jit(solution)/shard_map/ppermute | solution.py:666
  302.7 43.5 %collective-permute-start.34 = (bf16[256,1024]{1,0:T(8,128)(2,1)S(1)}, bf16[256,1024]{1,0:T(8,128)(2,1)S(1)}, u32[]{:S(2)}, u32[]{:S(2)}) collective-permute-start(bf16[256,1024]{1,0:T(8,128)(2,1)S(1)} %get-tuple-element.84), channel_id=1, source_target_pairs={{0,16},{4,20},{8,24},{12,28},{16,0},{20,4},{24,8},{28,12},{1,17},{... | collective-permute-start | bytes 1572872 | tf_op jit(solution)/shard_map/ppermute | solution.py:666
  302.7 43.5 %collective-permute-start.33 = (bf16[256,1024]{1,0:T(8,128)(2,1)S(1)}, bf16[256,1024]{1,0:T(8,128)(2,1)S(1)}, u32[]{:S(2)}, u32[]{:S(2)}) collective-permute-start(bf16[256,1024]{1,0:T(8,128)(2,1)S(1)} %get-tuple-element.82), channel_id=1, source_target_pairs={{0,8},{4,12},{8,0},{12,4},{16,24},{20,28},{24,16},{28,20},{1,9},{5... | collective-permute-start | bytes 1572872 | tf_op jit(solution)/shard_map/ppermute | solution.py:666
  350.0 14.6 %collective-permute-start.36 = (bf16[128,256]{1,0:T(8,128)(2,1)S(1)}, bf16[128,256]{1,0:T(8,128)(2,1)S(1)}, u32[]{:S(2)}, u32[]{:S(2)}) collective-permute-start(bf16[128,256]{1,0:T(8,128)(2,1)S(1)} %bitcast.137), channel_id=1, source_target_pairs={{0,3},{1,11},{2,19},{3,27},{4,2},{5,10},{6,18},{7,26},{8,1},{9,9},... | collective-permute-start | bytes 196616 | tf_op jit(solution)/shard_map/ppermute | solution.py:702
  353.7 11.0 %collective-permute-start.37 = (bf16[128,256]{1,0:T(8,128)(2,1)S(1)}, bf16[128,256]{1,0:T(8,128)(2,1)S(1)}, u32[]{:S(2)}, u32[]{:S(2)}) collective-permute-start(bf16[128,256]{1,0:T(8,128)(2,1)S(1)} %bitcast.138), channel_id=1, source_target_pairs={{0,2},{1,10},{2,18},{3,26},{4,3},{5,11},{6,19},{7,27},{8,0},{9,8},... | collective-permute-start | bytes 196616 | tf_op jit(solution)/shard_map/ppermute | solution.py:702
  354.3 10.3 %collective-permute-start.38 = (bf16[128,256]{1,0:T(8,128)(2,1)S(1)}, bf16[128,256]{1,0:T(8,128)(2,1)S(1)}, u32[]{:S(2)}, u32[]{:S(2)}) collective-permute-start(bf16[128,256]{1,0:T(8,128)(2,1)S(1)} %bitcast.139), channel_id=1, source_target_pairs={{0,1},{1,9},{2,17},{3,25},{4,0},{5,8},{6,16},{7,24},{8,3},{9,11},{... | collective-permute-start | bytes 196616 | tf_op jit(solution)/shard_map/ppermute | solution.py:702
  357.1 8.6 %collective-permute-start.39 = (bf16[128,256]{1,0:T(8,128)(2,1)S(1)}, bf16[128,256]{1,0:T(8,128)(2,1)S(1)}, u32[]{:S(2)}, u32[]{:S(2)}) collective-permute-start(bf16[128,256]{1,0:T(8,128)(2,1)S(1)} %bitcast.140), channel_id=1, source_target_pairs={{0,0},{1,8},{2,16},{3,24},{4,1},{5,9},{6,17},{7,25},{8,2},{9,10},{... | collective-permute-start | bytes 196616 | tf_op jit(solution)/shard_map/ppermute | solution.py:702
  (33 other events, 170.6 us)

commit v3 on v2

--- a/solution.py
+++ b/solution.py
@@ -2,6 +2,7 @@
 
 import jax
 import jax.numpy as jnp
+import numpy as np
 from jax import lax
 from jax.experimental import pallas as pl
 from jax.experimental.pallas import tpu as pltpu
@@ -13,6 +14,7 @@
 NN = (((1,), (0,)), ((), ()))
 NT = (((1,), (1,)), ((), ()))
 TN = (((0,), (0,)), ((), ()))
+FREQS = (10000.0 ** (-(2.0 * np.arange(HALF)) / ROT)).astype(np.float32)
 BF = jnp.bfloat16
 F32 = jnp.float32
 VMEM_LIMIT = 62 * 1024 * 1024
@@ -55,7 +57,7 @@
             small[...] = jnp.zeros_like(small)
             smallf[...] = jnp.zeros_like(smallf)
 
-    normed, _unused = norm_parts(x_ref[...])
+    normed, _ = norm_parts(x_ref[...])
     scale = gain[...].astype(F32)
     nm = (normed * scale + shift[...].astype(F32)).astype(BF)
     dy = dy_ref[...]
@@ -129,7 +131,7 @@
 def proj_kernel(nh, prev, pos, *refs):
     x_ref, dy_ref, wq, wk, wv, bq, bk, bv, wo, gain, shift, cos, sin = refs[:13]
     qt, kt, vt, dot, kn, vn, na_ref = refs[13 + (7 if prev else 0) :]
-    normed, _unused = norm_parts(x_ref[...])
+    normed, _ = norm_parts(x_ref[...])
     na = (normed * gain[...].astype(F32) + shift[...].astype(F32)).astype(BF)
     na_ref[...] = na
     co = cos[...]
@@ -194,10 +196,12 @@
     )(pos, x, dy, w_qkv, w_qkv, w_qkv, b_qkv, b_qkv, b_qkv, w_out, gain, shift, cos, sin, *(prev or ()))
 
 
-def head_kernel(nh, x_hbm, dy_hbm, wu_hbm, wd_hbm, wqkv_hbm, wo_hbm, bu, bq, gain_m, shift_m, gain_a, shift_a, cos, sin,
-                g_out, na_out, dy_out, qt, kt, vt, dot, kn, vn, p_own, p_far, out_wu, out_wd, small, smallf,
+def head_kernel(nh, x_hbm, dy_hbm, wu_hbm, wd_hbm, wqkv_hbm, wo_hbm, bu, bq, gain_m, shift_m, gain_a, shift_a, freqs, lens,
+                g_out, na_out, dy_out, qt, kt, vt, dot, kn, vn, cos, sin, p_own, p_far, up_keep, up_send, dn_keep, dn_send,
+                small, smallf,
                 xs, dys, wu, wd, wqkv, wt, wo, bias_t, parts, far_in, near_in, dwu, dwd, load, send, recv):
     step = pl.program_id(0)
+    i = lax.axis_index("dp")
     j = lax.axis_index("head")
     own, d = x_hbm.shape
     f = wu.shape[1]
@@ -274,7 +278,7 @@
         copies[8].wait_recv()
         copies[9].wait_recv()
 
-    normed, _unused = norm_parts(xs[step])
+    normed, _ = norm_parts(xs[step])
     scale = gain_m[...].astype(F32)
     nm = (normed * scale + shift_m[...].astype(F32)).astype(BF)
     na = (normed * gain_a[...].astype(F32) + shift_a[...].astype(F32)).astype(BF)
@@ -313,15 +317,29 @@
     @pl.when(step == 3)
     def _():
         copies[12].start()
-        for b in range(out_wu.shape[0]):
-            rows = out_wu.shape[1]
-            out_wu[b] = dwu[b * rows : (b + 1) * rows, :].astype(BF)
-        for b in range(out_wd.shape[0]):
-            rows = out_wd.shape[1]
-            out_wd[b] = dwd[b * rows : (b + 1) * rows, :].astype(BF)
-
-    co = cos[...]
-    si = sin[...]
+        rows = up_keep.shape[1]
+        for b in range(4):
+            for ref, acc, at in (
+                (up_keep, dwu, 2 * b + i % 2),
+                (up_send, dwu, 2 * b + 1 - i % 2),
+                (dn_keep, dwd, 4 * (b // 2) + 2 * ((i // 2) % 2) + b % 2),
+                (dn_send, dwd, 4 * (b // 2) + 2 * (1 - (i // 2) % 2) + b % 2),
+            ):
+                ref[b] = acc[pl.ds(pl.multiple_of(at * rows, rows), rows), :].astype(BF)
+
+    lane = lax.broadcasted_iota(jnp.int32, (1, own), 1)
+    far = jnp.where(lane < half, j ^ 2, j ^ 3) * own + (step - 2) * half + lane % half
+    index = jnp.where(step == 0, j * own + lane, jnp.where(step == 1, (j ^ 1) * own + lane, far))
+    begin = jnp.zeros_like(index)
+    total = jnp.int32(0)
+    for s in range(lens.shape[0] - 1):
+        total = total + lens[s]
+        begin = jnp.where(index >= total, total, begin)
+    angle = jnp.concatenate([freqs[...]] * (own // 128), axis=1) * (index - begin).astype(F32)
+    co = jnp.cos(angle)
+    si = jnp.sin(angle)
+    cos[...] = co
+    sin[...] = si
 
     def projected(k):
         b = bias_t[k * w : (k + 1) * w, :]
@@ -359,7 +377,7 @@
             c.wait_send()
 
 
-def head_stage(x, dy, w_up, w_down, w_qkv, w_out, bu, bq, gm, sm, ga, sa, cos, sin, n, cid):
+def head_stage(x, dy, w_up, w_down, w_qkv, w_out, bu, bq, gm, sm, ga, sa, freqs, lens, n, cid):
     own, d = x.shape
     tok = own * n
     w = d // n
@@ -377,18 +395,24 @@
         in_specs=[hbm] * 6
         + [const((1, w_up.shape[1])), const((1, 3 * d))]
         + [const((1, d))] * 4
-        + [lane(HALF), lane(HALF)],
+        + [const((HALF, 128)), pl.BlockSpec(memory_space=pltpu.SMEM)],
         out_specs=[nat(d)] * 3
         + [lane(w)] * 4
         + [nat(w)] * 2
+        + [lane(HALF)] * 2
         + [const((own, d))] * 2
-        + [const((8, d // 8, f)), const((8, f // 8, d)), const((8, d)), const((8, f))],
+        + [const((4, d // 8, f))] * 2
+        + [const((4, f // 8, d))] * 2
+        + [const((8, d)), const((8, f))],
         out_shape=tuple(
             [sds((tok, d), BF)] * 3
             + [sds((w, tok), BF)] * 4
             + [sds((tok, w), BF)] * 2
+            + [sds((HALF, tok), F32)] * 2
             + [sds((own, d), BF)] * 2
-            + [sds((8, d // 8, f), BF), sds((8, f // 8, d), BF), sds((8, d), F32), sds((8, f), F32)]
+            + [sds((4, d // 8, f), BF)] * 2
+            + [sds((4, f // 8, d), BF)] * 2
+            + [sds((8, d), F32), sds((8, f), F32)]
         ),
         scratch_shapes=[
             pltpu.VMEM((4, own, d), BF),
@@ -415,10 +439,10 @@
             flops=12 * tok * d * f + 10 * tok * d * w, bytes_accessed=12 * tok * d + 8 * d * f, transcendentals=2 * tok * f
         ),
         name="head_stage",
-    )(x, dy, w_up, w_down, w_qkv, w_out, bu, bq, gm, sm, ga, sa, cos, sin)
-
-
-def attn_kernel(nh, tok, blk, per, halved, lens, rel, cos, sin, seg_start, qt, kt, vt, dot, kn, vn,
+    )(x, dy, w_up, w_down, w_qkv, w_out, bu, bq, gm, sm, ga, sa, freqs, lens)
+
+
+def attn_kernel(nh, tok, blk, per, halved, lens, rel, cos, sin, qt, kt, vt, dot, kn, vn,
                 gt_ref, ctx_ref, exps, peaks, dk, dv, oacc, dqacc, mrow, lrow, drow, qpad, dopad):
     nseq = lens.shape[0]
     nblk = tok // blk
@@ -448,8 +472,12 @@
             begin = jnp.where(total <= first_tok, total, begin)
         low = begin // blk
         cols = pl.ds(place(i), blk)
-        start_row = seg_start[:, cols]
         query_idx = cols_iota + first_tok
+        start_row = jnp.zeros_like(query_idx)
+        total = jnp.int32(0)
+        for s in range(nseq - 1):
+            total = total + lens[s]
+            start_row = jnp.where(query_idx >= total, total, start_row)
         for h in range(nh):
             half = (h % 2) * HD
             qpad[h, half : half + HD, :] = qt[h * HD : (h + 1) * HD, cols]
@@ -535,7 +563,7 @@
     lax.fori_loop(0, nblk, finish, 0)
 
 
-def attention(lens, rel, cos, sin, seg_start, qt, kt, vt, dot, kn, vn, chunk, maxlen, halved=False, blk=256):
+def attention(lens, rel, cos, sin, qt, kt, vt, dot, kn, vn, chunk, maxlen, halved=False, blk=256):
     width, tok = qt.shape
     nh = width // HD
     wb = maxlen // blk + 1
@@ -544,7 +572,7 @@
     return pl.pallas_call(
         functools.partial(attn_kernel, nh, tok, blk, chunk // blk, halved),
         out_shape=(jax.ShapeDtypeStruct((3 * width, tok), BF), jax.ShapeDtypeStruct((width, tok), BF)),
-        in_specs=[sm, sm] + [vm] * 9,
+        in_specs=[sm, sm] + [vm] * 8,
         out_specs=(vm, vm),
         scratch_shapes=[
             pltpu.VMEM((nh, wb, blk, blk), F32),
@@ -564,7 +592,7 @@
             flops=20 * width * tok * maxlen, bytes_accessed=20 * width * tok, transcendentals=nh * tok * maxlen
         ),
         name="attention",
-    )(lens, rel, cos, sin, seg_start, qt, kt, vt, dot, kn, vn)
+    )(lens, rel, cos, sin, qt, kt, vt, dot, kn, vn)
 
 
 def post_kernel(pos, gt_ref, na_ref, gm_ref, wq, wk, wv, gain, shift, g_ref, out_w, bias, small, dw):
@@ -641,6 +669,346 @@
     )(pos, gt, na, gm, w_qkv, w_qkv, w_qkv, gain, shift)
 
 
+def tail_kernel(gt_h, na_h, gm_h, ctx_h, dya_h, wqkv_h, wo_h, upk_h, upo_h, dnk_h, dno_h, x_h, dyo_h, pown_h, py_h,
+                ga, sa, bo, bd, small, smallf,
+                out_ref, gin_ref, wup_ref, wdn_ref, wq_ref, wout_ref, sums_ref,
+                gt, na, gm, ctx, dya, wqkv, wo, upk, upo, dnk, dno, xo, dyo, pown, py,
+                ctx_in, up4, dn4, up_in, dn_in, up2, dn2, up_in2, dn_in2,
+                dwq, qa_in, qb_in, qa4, qb4, qa_in2, qb_in2, qa2, qb2, qa_in3, qb_in3, qfin, q_own,
+                dwo, wo_in, wo4, wo_in2, wo2, wo_in3, piece, owner_in,
+                far_in, near_in, far_sum, y_in, sm, sm_in, load, send, recv):
+    i = lax.axis_index("dp")
+    j = lax.axis_index("head")
+    own, d = x_h.shape
+    w = wqkv.shape[1] // 3
+    half = own // 2
+    bx = i % 2
+    b0 = (i // 2) % 2
+    b1 = i // 4
+    mesh_id = pl.DeviceIdType.MESH
+    core, across, diag = {"head": j ^ 1}, {"head": j ^ 2}, {"head": j ^ 3}
+    px, p0, p1 = {"dp": i ^ 1}, {"dp": i ^ 2}, {"dp": i ^ 4}
+    lo, hi = pl.ds(0, half), pl.ds(half, half)
+    count = [0]
+
+    def remote(src, dst, to):
+        k = count[0]
+        count[0] += 1
+        return pltpu.make_async_remote_copy(
+            src_ref=src, dst_ref=dst, send_sem=send.at[k], recv_sem=recv.at[k], device_id=to, device_id_type=mesh_id)
+
+    def local(src, dst, k):
+        return pltpu.make_async_copy(src, dst, load.at[k])
+
+    loads = [
+        local(upk_h, upk, 0), local(upo_h, upo, 1), local(dnk_h, dnk, 2), local(dno_h, dno, 3),
+        local(gt_h, gt, 4), local(na_h, na, 5), local(ctx_h, ctx, 6), local(dya_h, dya, 7), local(gm_h, gm, 8),
+        local(wqkv_h.at[:, pl.ds(j * w, w)], wqkv.at[:, pl.ds(0, w)], 9),
+        local(wqkv_h.at[:, pl.ds(d + j * w, w)], wqkv.at[:, pl.ds(w, w)], 10),
+        local(wqkv_h.at[:, pl.ds(2 * d + j * w, w)], wqkv.at[:, pl.ds(2 * w, w)], 11),
+        local(wo_h, wo, 12), local(x_h, xo, 13), local(dyo_h, dyo, 14), local(pown_h, pown, 15), local(py_h, py, 16),
+    ]
+    c_ctx = [
+        remote(ctx_h.at[:, pl.ds(2 * own, half)], ctx_in.at[1, :, lo], across),
+        remote(ctx_h.at[:, pl.ds(3 * own, half)], ctx_in.at[1, :, hi], across),
+        remote(ctx_h.at[:, pl.ds(2 * own + half, half)], ctx_in.at[2, :, lo], diag),
+        remote(ctx_h.at[:, pl.ds(3 * own + half, half)], ctx_in.at[2, :, hi], diag),
+        remote(ctx_h.at[:, pl.ds(own, own)], ctx_in.at[0], core),
+    ]
+    c_up0 = remote(up4.at[:, 1 - b0], up_in, p0)
+    c_dnx = remote(dn4.at[:, 1 - bx], dn_in, px)
+    c_up1 = remote(up2.at[1 - b1], up_in2, p1)
+    c_dn1 = remote(dn2.at[1 - b1], dn_in2, p1)
+    rows = dwq.shape[3] // 2
+    ra, rb = pl.ds(0, rows), pl.ds(rows, rows)
+    c_qa = remote(dwq.at[:, :, 1 - bx, ra], qa_in, px)
+    c_qb = remote(dwq.at[:, 1 - b0, :, rb], qb_in, p0)
+    c_qa0 = remote(qa4.at[:, 1 - b0], qa_in2, p0)
+    c_qbx = remote(qb4.at[:, 1 - bx], qb_in2, px)
+    c_qa1 = remote(qa2.at[1 - b1], qa_in3, p1)
+    c_qb1 = remote(qb2.at[1 - b1], qb_in3, p1)
+    c_wox = remote(dwo.at[:, :, 1 - bx], wo_in, px)
+    c_wo0 = remote(wo4.at[:, 1 - b0], wo_in2, p0)
+    c_wo1 = remote(wo2.at[1 - b1], wo_in3, p1)
+    c_g = [
+        remote(gm.at[pl.ds(2 * own + half, half)], far_in.at[lo], core),
+        remote(gm.at[pl.ds(3 * own + half, half)], far_in.at[hi], core),
+        remote(gm.at[pl.ds(own, own)], near_in, core),
+    ]
+    c_y = [remote(far_sum.at[lo], y_in.at[lo], across), remote(far_sum.at[hi], y_in.at[hi], across)]
+    c_sm = [remote(sm.at[s], sm_in.at[s], to) for s, to in enumerate((core, across, px, p0, p1))]
+    dests = []
+    c_own = []
+    for r in range(4):
+        di, dj = 2 * j + i // 4, (i % 4) ^ r
+        dests.append((di, dj))
+        c_own.append(remote(piece.at[:, pl.ds(pl.multiple_of(dj * w, 128), w)], owner_in.at[i % 4], {"dp": di, "head": dj}))
+    c_q = []
+    q_dst = []
+    for t in range(3):
+        dst = (t - j + 4) % 4
+        q_dst.append(dst)
+        c_q.append(remote(qfin.at[(3 * dst + t) // 4], q_own.at[t], {"head": dst}))
+
+    barrier = pltpu.get_barrier_semaphore()
+    for to in (core, across, diag, px, p0, p1):
+        pl.semaphore_signal(barrier, inc=1, device_id=to, device_id_type=mesh_id)
+    for c in loads:
+        c.start()
+    for r in range(4):
+        si, sj = 4 * (i % 2) + (j ^ r), i // 2
+
+        @pl.when((si != i) | (sj != j))
+        def _():
+            pl.semaphore_signal(barrier, inc=1, device_id={"dp": si, "head": sj}, device_id_type=mesh_id)
+
+    to_self = jnp.where(2 * j + i // 4 == i, 1, 0)
+    pl.semaphore_wait(barrier, 10 - to_self)
+
+    for c in c_ctx:
+        c.start()
+
+    def added(a, b):
+        return a.astype(F32) + b.astype(F32)
+
+    for k in range(4):
+        loads[k].wait()
+    up4[:, 1 - b0] = added(upk[:, 1 - b0], upo[:, 1 - b0]).astype(BF)
+    c_up0.start()
+    dn4[:, 1 - bx] = added(dnk[:, 1 - bx], dno[:, 1 - bx]).astype(BF)
+    c_dnx.start()
+
+    loads[4].wait()
+    loads[5].wait()
+    for k in range(4):
+        t = mm(gt[...], na[:, 256 * k : 256 * (k + 1)]).astype(BF)
+        dwq[k // 2, k % 2, 0] = t[:, :128]
+        dwq[k // 2, k % 2, 1] = t[:, 128:]
+    c_qa.start()
+    c_qb.start()
+    loads[6].wait()
+    loads[7].wait()
+    t = mm(ctx[...], dya[...]).astype(BF)
+    for b in range(8):
+        dwo[b // 4, (b // 2) % 2, b % 2] = t[32 * b : 32 * (b + 1)]
+    c_wox.start()
+
+    for k in range(8, 12):
+        loads[k].wait()
+    scale = ga[...].astype(F32)
+    ones = jnp.zeros((1, d), F32)
+    s_gain, s_shift, s_bias = ones, ones, jnp.zeros((1, 3 * w), F32)
+
+    def tile(at, size, sums):
+        ts = slice(at, at + size)
+        gn = gt[:, ts].T
+        r = mm(gn, wqkv[...], NT)
+        gm[ts, :] = (r * scale + gm[ts, :].astype(F32)).astype(BF)
+        return (
+            sums[0] + jnp.sum(r * na[ts, :].astype(F32), axis=0, keepdims=True),
+            sums[1] + jnp.sum(r, axis=0, keepdims=True),
+            sums[2] + jnp.sum(gn.astype(F32), axis=0, keepdims=True),
+        )
+
+    sums = (s_gain, s_shift, s_bias)
+    sums = tile(2 * own, own, sums)
+    c_g[0].start()
+    sums = tile(3 * own, own, sums)
+    c_g[1].start()
+    c_up0.wait_recv()
+    mine = added(upk[:, b0], upo[:, b0]) + up_in[...].astype(F32)
+    up2[...] = mine.astype(BF)
+    c_up1.start()
+    c_g[0].wait_recv()
+    far_sum[lo] = added(gm[2 * own : 2 * own + half], far_in[lo]).astype(BF)
+    c_y[0].start()
+    c_dnx.wait_recv()
+    mine = added(dnk[:, bx], dno[:, bx]) + dn_in[...].astype(F32)
+    dn2[...] = mine.astype(BF)
+    c_dn1.start()
+    c_g[1].wait_recv()
+    far_sum[hi] = added(gm[3 * own : 3 * own + half], far_in[hi]).astype(BF)
+    c_y[1].start()
+    sums = tile(own, own, sums)
+    c_g[2].start()
+    sums = tile(0, own, sums)
+
+    sm[0] = jnp.zeros((16, d), F32)
+    shift = sa[...].astype(F32)
+    sm[0, 0:1, :] = (sums[0] - shift * sums[1]) / scale
+    sm[0, 1:2, :] = sums[1]
+    for k in range(3):
+        sm[0, 2 + k : 3 + k, pl.ds(pl.multiple_of(j * w, 128), w)] = sums[2][:, k * w : (k + 1) * w]
+    sm[0, 5:7, :] = small[0:2, :]
+    sm[0, 7:8, :] = small[2:3, :] * 0.25
+    sm[0, pl.ds(8 + j, 1), :] = smallf[0:1, :]
+    c_sm[0].start()
+
+    c_qa.wait_recv()
+    qa4[...] = added(dwq[:, :, bx, ra], qa_in[...]).astype(BF)
+    c_qa0.start()
+    c_qb.wait_recv()
+    qb4[...] = added(dwq[:, b0, :, rb], qb_in[...]).astype(BF)
+    c_qbx.start()
+    c_wox.wait_recv()
+    wo4[...] = added(dwo[:, :, bx], wo_in[...]).astype(BF)
+    c_wo0.start()
+
+    def small_step(s):
+        c_sm[s].wait_recv()
+        sm[s + 1] = sm[s] + sm_in[s]
+        if s < 4:
+            c_sm[s + 1].start()
+
+    small_step(0)
+    for k in range(12, 17):
+        loads[k].wait()
+    attn = mm(ctx[:, :own], wo[pl.ds(pl.multiple_of(j * w, 128), w), :], TN)
+    c_ctx[4].wait_recv()
+    attn += mm(ctx_in[0], wo[pl.ds(pl.multiple_of((j ^ 1) * w, 128), w), :], TN)
+    for k in range(4):
+        c_ctx[k].wait_recv()
+    attn += mm(ctx_in[1], wo[pl.ds(pl.multiple_of((j ^ 2) * w, 128), w), :], TN)
+    attn += mm(ctx_in[2], wo[pl.ds(pl.multiple_of((j ^ 3) * w, 128), w), :], TN)
+    out_ref[...] = (
+        xo[...].astype(F32) + attn + added(pown[...], py[...]) + (bo[...].astype(F32) + bd[...].astype(F32))
+    ).astype(BF)
+    small_step(1)
+
+    c_qa0.wait_recv()
+    qa2[...] = added(qa4[:, b0], qa_in2[...]).astype(BF)
+    c_qa1.start()
+    c_qbx.wait_recv()
+    qb2[...] = added(qb4[:, bx], qb_in2[...]).astype(BF)
+    c_qb1.start()
+    c_wo0.wait_recv()
+    wo2[...] = added(wo4[:, b0], wo_in2[...]).astype(BF)
+    c_wo1.start()
+    small_step(2)
+    c_up1.wait_recv()
+    wup_ref[...] = added(up2[b1], up_in2[...])
+    c_dn1.wait_recv()
+    piece[: dn2.shape[1], :] = added(dn2[b1], dn_in2[...]).astype(BF)
+    small_step(3)
+    c_qa1.wait_recv()
+    c_qb1.wait_recv()
+    done = jnp.concatenate([added(qa2[b1], qa_in3[...]), added(qb2[b1], qb_in3[...])], axis=0).astype(BF)
+    for k in range(3):
+        qfin[k] = done[k * w : (k + 1) * w]
+    for t in range(3):
+
+        @pl.when(q_dst[t] != j)
+        def _():
+            c_q[t].start()
+
+        @pl.when(q_dst[t] == j)
+        def _():
+            q_own[t] = qfin[(3 * j + t) // 4]
+
+    c_wo1.wait_recv()
+    piece[dn2.shape[1] :, :] = added(wo2[b1], wo_in3[...]).astype(BF)
+    for r in range(4):
+        di, dj = dests[r]
+
+        @pl.when((di != i) | (dj != j))
+        def _():
+            c_own[r].start()
+
+        @pl.when((di == i) & (dj == j))
+        def _():
+            owner_in[i % 4] = piece[:, pl.ds(pl.multiple_of(dj * w, 128), w)]
+
+    small_step(4)
+    sums_ref[...] = sm[5]
+
+    c_g[2].wait_recv()
+    near = added(gm[0:own], near_in[...])
+    normed, inv = norm_parts(xo[...])
+    c_y[0].wait_recv()
+    c_y[1].wait_recv()
+    g = near + y_in[...].astype(F32)
+    gin_ref[...] = dyo[...].astype(F32) + inv * (
+        g - jnp.mean(g, axis=-1, keepdims=True) - normed * jnp.mean(g * normed, axis=-1, keepdims=True)
+    )
+
+    for t in range(3):
+
+        @pl.when(q_dst[t] != j)
+        def _():
+            c_q[t].wait_recv()
+
+        wq_ref[:, t * w : (t + 1) * w] = q_own[t].astype(F32).T
+    for r in range(4):
+        di, dj = dests[r]
+
+        @pl.when((di != i) | (dj != j))
+        def _():
+            c_own[r].wait_recv()
+
+    nd = dn2.shape[1]
+    no = wo2.shape[1]
+    for a in range(4):
+        wdn_ref[a * nd : (a + 1) * nd, :] = owner_in[a, :nd].astype(F32)
+        wout_ref[a * no : (a + 1) * no, :] = owner_in[a, nd:].astype(F32)
+
+    for c in c_ctx + [c_up0, c_dnx, c_up1, c_dn1, c_qa, c_qb, c_qa0, c_qbx, c_qa1, c_qb1, c_wox, c_wo0, c_wo1] + c_g + c_y + c_sm:
+        c.wait_send()
+    for t in range(3):
+
+        @pl.when(q_dst[t] != j)
+        def _():
+            c_q[t].wait_send()
+
+    for r in range(4):
+        di, dj = dests[r]
+
+        @pl.when((di != i) | (dj != j))
+        def _():
+            c_own[r].wait_send()
+
+
+def tail_stage(gt, na, gm, ctx, dya, w_qkv, w_out, upk, upo, dnk, dno, x, dy, pown, py, ga, sa, bo, bd, small, smallf, cid):
+    own, d = x.shape
+    tok = na.shape[0]
+    w = d // 4
+    vm = pl.BlockSpec(memory_space=pltpu.VMEM)
+    hbm = pl.BlockSpec(memory_space=pl.ANY)
+    sds = jax.ShapeDtypeStruct
+    big = lambda *s: pltpu.VMEM(s, BF)
+    nb = d // 8
+    no = w // 8
+    r2 = 3 * w // 2
+    return pl.pallas_call(
+        tail_kernel,
+        in_specs=[hbm] * 15 + [vm] * 6,
+        out_specs=[vm] * 7,
+        out_shape=(
+            sds((own, d), BF), sds((own, d), F32), sds((nb, d), F32), sds((4 * nb, w), F32),
+            sds((nb, 3 * w), F32), sds((4 * no, w), F32), sds((16, d), F32),
+        ),
+        scratch_shapes=[
+            big(3 * w, tok), big(tok, d), big(tok, d), big(w, tok), big(tok, d), big(d, 3 * w), big(d, d),
+            big(2, 2, nb, d), big(2, 2, nb, d), big(2, 2, nb, d), big(2, 2, nb, d),
+            big(own, d), big(own, d), big(own, d), big(own, d),
+            big(3, w, own), big(2, 2, nb, d), big(2, 2, nb, d), big(2, nb, d), big(2, nb, d),
+            big(2, nb, d), big(2, nb, d), big(nb, d), big(nb, d),
+            big(2, 2, 2, 3 * w, 128), big(2, 2, r2, 128), big(2, 2, r2, 128), big(2, 2, r2, 128), big(2, 2, r2, 128),
+            big(2, r2, 128), big(2, r2, 128), big(2, r2, 128), big(2, r2, 128), big(r2, 128), big(r2, 128),
+            big(3, w, 128), big(3, w, 128),
+            big(2, 2, 2, no, d), big(2, 2, no, d), big(2, 2, no, d), big(2, no, d), big(2, no, d), big(no, d),
+            big(nb + no, d), big(4, nb + no, w),
+            big(own, d), big(own, d), big(own, d), big(own, d),
+            pltpu.VMEM((6, 16, d), F32), pltpu.VMEM((5, 16, d), F32),
+            pltpu.SemaphoreType.DMA((17,)), pltpu.SemaphoreType.DMA((40,)), pltpu.SemaphoreType.DMA((40,)),
+        ],
+        compiler_params=pltpu.CompilerParams(vmem_limit_bytes=VMEM_LIMIT, collective_id=cid, has_side_effects=True),
+        cost_estimate=pl.CostEstimate(
+            flops=14 * tok * d * w, bytes_accessed=10 * tok * d, transcendentals=0
+        ),
+        name="tail_stage",
+    )(gt, na, gm, ctx, dya, w_qkv, w_out, upk, upo, dnk, dno, x, dy, pown, py, ga, sa, bo, bd, small, smallf)
+
+
 def layout(seq_lens, index):
     ends = jnp.cumsum(seq_lens, dtype=jnp.int32)
     starts = ends - seq_lens
@@ -650,14 +1018,6 @@
     return first, index - first
 
 
-def swap_bits(parts, j):
-    low = (j & 1) == 1
-    high = (j & 2) == 2
-    a, b, c, d = parts
-    a, b, c, d = jnp.where(low, b, a), jnp.where(low, a, b), jnp.where(low, d, c), jnp.where(low, c, d)
-    return [jnp.where(high, c, a), jnp.where(high, d, b), jnp.where(high, a, c), jnp.where(high, b, d)]
-
-
 def head_perm(v, bit):
     return lax.ppermute(v, "head", [(k, k ^ bit) for k in range(4)])
 
@@ -666,61 +1026,11 @@
     return lax.ppermute(v, "dp", [(k, k ^ bit) for k in range(8)])
 
 
-def pick(v, index, axis=0):
-    return lax.dynamic_index_in_dim(v, index, axis, keepdims=False)
-
-
-def dp_scatter(blocks, i):
-    x = i & 1
-    z = i >> 1
-    pairs = blocks.reshape((4, 2) + blocks.shape[1:])
-    other = dp_perm(pick(pairs, 1 - x, 1), 1)
-    mine = pick(pairs, x, 1).astype(F32) + other.astype(F32)
-    low = mine.astype(BF)
-    result = pick(mine, z)
-    for s in (1, 2, 3):
-        result = result + dp_perm(pick(low, z ^ s), 2 * s).astype(F32)
-    return result
-
-
-def sum_all(v):
-    for bit in (1, 2):
-        v = v + head_perm(v, bit)
-    for bit in (1, 2, 4):
-        v = v + dp_perm(v, bit)
-    return v
-
-
-def to_owner(v, i, j):
-    cols = v.reshape(v.shape[0], 4, v.shape[1] // 4)
-    got = []
-    for r in range(4):
-        pairs = []
-        for si in range(8):
-            for sj in range(4):
-                pairs.append((si * 4 + sj, (2 * sj + si // 4) * 4 + ((si % 4) ^ r)))
-        got.append(lax.ppermute(pick(cols, (i % 4) ^ r, 1), ("dp", "head"), pairs))
-    return jnp.concatenate(swap_bits(got, j), axis=0)
-
-
-def qkv_owner(v, j):
-    got = []
-    for t in range(3):
-        pairs = [((3 * dst + t) % 4, dst) for dst in range(4)]
-        slot = jnp.int32(0)
-        for src, dst in pairs:
-            slot = jnp.where(j == src, (3 * dst + t) // 4, slot)
-        got.append(lax.ppermute(pick(v, slot), "head", pairs))
-    return jnp.concatenate(got, axis=0)
-
-
 def fast_body(inputs, lengths, attn_gain, attn_shift, mlp_gain, mlp_shift, w_qkv, b_qkv, w_out, b_out,
               w_up, b_up, w_down, b_down, cotangent):
-    own, d = inputs.shape
+    own, _ = inputs.shape
     n = 4
     tok = own * n
-    w = d // n
-    i = lax.axis_index("dp")
     j = lax.axis_index("head")
     pos = j.astype(jnp.int32).reshape(1)
     rows = lambda v: v.reshape(1, -1)
@@ -728,67 +1038,20 @@
     bq, bu = rows(b_qkv), rows(b_up)
     lens = lengths[0]
 
-    lane = jnp.arange(tok, dtype=jnp.int32)
-    half = own // 2
-    far = (lane - 2 * own) // half
-    chunk = jnp.where(lane < 2 * own, lane // own, 2 + (far & 1))
-    offset = jnp.where(lane < 2 * own, lane % own, (far >> 1) * half + lane % half)
-    index = (chunk ^ j) * own + offset
-    first, position = layout(lens, index)
-    freqs = 10000.0 ** (-(2.0 * jnp.arange(HALF, dtype=F32)) / ROT)
-    angle = freqs[:, None] * position.astype(F32)[None, :]
-    cos, sin = jnp.cos(angle), jnp.sin(angle)
-    seg_start = first[None, :]
-
-    g_mlp, na, dy_all, qt, kt, vt, dot, kn, vn, p_own, p_far, dwu, dwd, small, smallf = head_stage(
-        inputs, cotangent, w_up, w_down, w_qkv, w_out, bu, bq, gm, sm, ga, sa, cos, sin, n, 0
+    freqs = jnp.asarray(np.broadcast_to(FREQS[:, None], (HALF, 128)))
+    (g_mlp, na, dy_all, qt, kt, vt, dot, kn, vn, cos, sin, p_own, p_far, up_keep, up_send, dn_keep, dn_send, small,
+     smallf) = head_stage(inputs, cotangent, w_up, w_down, w_qkv, w_out, bu, bq, gm, sm, ga, sa, freqs, lens, n, 0)
+    up_other = dp_perm(up_send, 1)
+    dn_other = dp_perm(dn_send, 2)
+    p_y = head_perm(p_far, 2)
+    gt, ctx = attention(lens, pos, cos, sin, qt, kt, vt, dot, kn, vn, own, tok // 2, halved=True)
+    quad = lambda v: v.reshape(2, 2, v.shape[1], v.shape[2])
+    output, grad_inputs, grad_w_up, grad_w_down, grad_w_qkv, grad_w_out, sums = tail_stage(
+        gt, na, g_mlp, ctx, dy_all, w_qkv, w_out, quad(up_keep), quad(up_other), quad(dn_keep), quad(dn_other),
+        inputs, cotangent, p_own, p_y, ga, sa, rows(b_out), rows(b_down), small, smallf, 1
     )
-    mlp_sum = p_own.astype(F32) + head_perm(p_far, 2).astype(F32)
-
-    up_down = jnp.concatenate([dwu, dwd], axis=1)
-    up_down = dp_scatter(up_down, i)
-    grad_w_up = up_down[:128]
-    grad_w_down = to_owner(up_down[128:].astype(BF), i, j).astype(F32)
-    slots = jnp.where(jnp.arange(4)[:, None] == j, smallf[0:1], 0.0)
-    early = sum_all(jnp.concatenate([small[:2], small[2:3] * 0.25, slots, jnp.zeros((1, d), F32)], axis=0))
-
-    gt, ctx = attention(lens, pos, cos, sin, seg_start, qt, kt, vt, dot, kn, vn, own, tok // 2, halved=True)
-
-    far_y = [ctx[:, 2 * own : 2 * own + half], ctx[:, 3 * own : 3 * own + half]]
-    far_d = [ctx[:, 2 * own + half : 3 * own], ctx[:, 3 * own + half :]]
-    got = [
-        ctx[:, :own],
-        head_perm(ctx[:, own : 2 * own], 1),
-        head_perm(jnp.concatenate(far_y, axis=1), 2),
-        head_perm(jnp.concatenate(far_d, axis=1), 3),
-    ]
-    w_rel = w_out.reshape(n, w, d)
-    attn_part = mm(jnp.concatenate(got, axis=0), jnp.concatenate([pick(w_rel, j ^ r) for r in range(n)], axis=0), TN)
-    bias = b_out.astype(F32) + b_down.astype(F32)
-    output = (inputs.astype(F32) + attn_part + mlp_sum + bias).astype(BF)
-
-    dw_out = mm(ctx, dy_all)
-
-    g, dwq, bias_q, small_q = post(pos, gt, na, g_mlp, w_qkv, ga, sa, n)
-    g_far = jnp.concatenate([g[2 * own : 2 * own + half], g[3 * own : 3 * own + half]], axis=0).astype(F32)
-    g_dia = jnp.concatenate([g[2 * own + half : 3 * own], g[3 * own + half :]], axis=0)
-    g_y = head_perm((g_far + head_perm(g_dia, 1).astype(F32)).astype(BF), 2)
-    g_sum = g[:own].astype(F32) + head_perm(g[own : 2 * own], 1).astype(F32) + g_y.astype(F32)
-
-    qkv = dp_scatter(dwq, i)
-    grad_w_qkv = qkv_owner(qkv.astype(BF).reshape(3, w, 128), j).astype(F32).T
-    out_sum = dp_scatter(dw_out.astype(BF).reshape(8, w // 8, d), i)
-    grad_w_out = to_owner(out_sum.astype(BF), i, j).astype(F32)
-
-    slots = jnp.where(jnp.arange(4)[None, :, None] == j, bias_q[0].reshape(3, 1, w), 0.0).reshape(3, d)
-    late = sum_all(jnp.concatenate([small_q[:2], slots, jnp.zeros((3, d), F32)], axis=0))
-
-    normed, inv = norm_parts(inputs)
-    grad_inputs = cotangent.astype(F32) + inv * (
-        g_sum - jnp.mean(g_sum, axis=-1, keepdims=True) - normed * jnp.mean(g_sum * normed, axis=-1, keepdims=True)
-    )
-    return (output, grad_inputs, late[0], late[1], early[0], early[1], grad_w_qkv, late[2:5].reshape(-1),
-            grad_w_out, early[2], grad_w_up, early[3:7].reshape(-1), grad_w_down, early[2])
+    return (output, grad_inputs, sums[0], sums[1], sums[5], sums[6], grad_w_qkv, sums[2:5].reshape(-1),
+            grad_w_out, sums[7], grad_w_up, sums[8:12].reshape(-1), grad_w_down, sums[7])
 
 
 def general_body(inputs, lengths, attn_gain, attn_shift, mlp_gain, mlp_shift, w_qkv, b_qkv, w_out, b_out,
@@ -798,7 +1061,6 @@
     n_dp = lax.axis_size("dp")
     tok = own * n
     w = d // n
-    f = w_up.shape[1] // n
     j = lax.axis_index("head")
     pos = j.astype(jnp.int32).reshape(1)
     rows = lambda v: v.reshape(1, -1)
@@ -810,14 +1072,14 @@
     over_head = lambda v: lax.psum_scatter(v, "head", scatter_dimension=0, tiled=True)
     x_all = gather(inputs)
     dy_all = gather(cotangent)
-    first, position = layout(lens, jnp.arange(tok, dtype=jnp.int32))
+    _, position = layout(lens, jnp.arange(tok, dtype=jnp.int32))
     freqs = 10000.0 ** (-(2.0 * jnp.arange(HALF, dtype=F32)) / ROT)
     angle = freqs[:, None] * position.astype(F32)[None, :]
     cos, sin = jnp.cos(angle), jnp.sin(angle)
     part, g_mlp, dwu, dwd, small, smallf = mlp(pos, x_all, dy_all, w_up, w_down, bu, gm, sm, n)
     qt, kt, vt, dot, kn, vn, na = proj(pos, x_all, dy_all, w_qkv, bq, w_out, ga, sa, cos, sin, n, tok, 0)
     gt, ctx = attention(
-        lens, jnp.zeros((1,), jnp.int32), cos, sin, first[None, :], qt, kt, vt, dot, kn, vn, own, tok // 2
+        lens, jnp.zeros((1,), jnp.int32), cos, sin, qt, kt, vt, dot, kn, vn, own, tok // 2
     )
     total, dwq, bias_q, small_q = post(pos, gt, na, g_mlp, w_qkv, ga, sa, n)
     attn_part = mm(ctx, lax.dynamic_slice_in_dim(w_out, j * w, w, 0), TN)

time: 370 us -> 230 us (0.62)
  the two profiles are of different devices: /device:TPU:7 before, /device:TPU:16 now
where the time goes in v3:
time: 230 us
  Pallas kernels  200 us (87%)
  local copies, waits for them, and re-layouts  24.7 us (11%)
  starting transfers between devices  4.22 us (2%)
    pallas_call x1, Pallas kernels, tail_stage(): pl.pallas_call(tail_kernel, in_specs=[hbm] * 15 + [vm] * 6, out_specs=[vm...  89.7 us
    pallas_call x1, Pallas kernels, head_stage(): pl.pallas_call(functools.partial(head_kernel, w // HD), grid=(n,), in_spe...  64.6 us
    pallas_call x1, Pallas kernels, attention(): pl.pallas_call(functools.partial(attn_kernel, nh, tok, blk, chunk // blk,...  45.8 us
    unnamed x25, local copies, waits for them, and re-layouts  11.5 us
    reshape x8, local copies, waits for them, and re-layouts, fast_body(): rows = lambda v: v.reshape(1, -1)  8.91 us
  transfers between devices with their start and end apart: 3, of which 0 were waited for; matrix products, arithmetic and copies ran while one was open for 1% of the time, Pallas kernels for 20%

profile of v3, /device:TPU:16, one launch (start us, length us, event | category | flops | bytes accessed | tf_op | source)
XLA Modules:
  0.0 229.7 jit_solution(5348151399450268256)
XLA Ops:
  0.6 1.3 reshape.78.gain_a.ga
  1.9 1.3 reshape.79.shift_a.sa
  3.2 1.3 reshape.74.bu
  4.5 1.3 reshape.75.bq
  5.8 1.3 reshape.76.gain_m
  7.1 1.3 reshape.77.shift_m
  8.4 1.3 jit_solution_.3.freqs
  9.7 0.0 copy-start.6
  9.7 0.0 copy-start.7
  9.7 64.6 %head_stage.1 = (bf16[2048,1024]{1,0:T(8,128)(2,1)}, bf16[2048,1024]{1,0:T(8,128)(2,1)}, bf16[2048,1024]{1,0:T(8,128)(2,1)}, bf16[256,2048]{1,0:T(8,128)(2,1)}, ...) custom-call(bf16[512,1024]{1,0:T(8,128)(2,1)} %x_h.1, ...), custom_call_target="tpu_custom_call" | custom-call | flops 31138512896 | bytes 33554432 | tf_op jit(solution)/shard_map/head_stage/pallas_call | solution.py:392
  74.3 1.6 collective-permute-start
  75.8 1.6 collective-permute-start.1
  77.4 1.1 collective-permute-start.2
  78.5 0.0 copy-done.6
  78.5 0.6 reshape.84.bo
  79.1 0.0 copy-done.7
  79.1 0.6 reshape.85.bd
  79.7 45.8 %attention.1 = (bf16[768,2048]{1,0:T(8,128)(2,1)}, bf16[256,2048]{1,0:T(8,128)(2,1)}) custom-call(s32[4]{0:T(128)} %bitcast.27, s32[1]{0:T(128)} %bitcast.1.rel, f32[8,2048]{1,0:T(8,128)} %get-tuple-element.42.cos, f32[8,2048]{1,0:T(8,128)} %get-tuple-element.43.sin, bf16[256,2048]{1,0:T(8,128)(2,1)} %get-tuple-element.44.qt, ...), custom_call_target="tpu_custom_call" | custom-call | flops 10737418240 | bytes 10485760 | tf_op jit(solution)/shard_map/attention/pallas_call | solution.py:572
  125.5 0.0 collective-permute-done
  125.5 0.0 copy-start
  125.5 0.0 collective-permute-done.1
  125.5 0.0 collective-permute-done.2.py_h
  125.5 0.9 copy-done
  126.4 89.7 %tail_stage.1 = (bf16[512,1024]{1,0:T(8,128)(2,1)}, f32[512,1024]{1,0:T(8,128)}, f32[128,1024]{1,0:T(8,128)}, f32[512,256]{1,0:T(8,128)}, f32[128,768]{1,0:T(8,1...) custom-call(bf16[768,2048]{1,0:T(8,128)(2,1)} %get-tuple-element.50.gt_h, bf16[2048,1024]{1,0:T(8,128)(2,1)} %get-tuple-element.51.na_h, ...), custom_call_target="tpu_custom_call" | custom-call | flops 7516192768 | bytes 20971520 | tf_op jit(solution)/shard_map/tail_stage/pallas_call | solution.py:981
  216.1 0.0 copy-start.3
  216.2 0.0 copy-start.4
  216.2 0.0 copy-start.2
  216.2 0.8 slice_bitcast_fusion
  217.0 0.8 slice.26
  217.8 1.6 fusion
  219.4 0.0 copy-start.5
  219.4 0.6 copy.32
  220.0 0.6 reshape.86
  220.6 0.6 copy.40
  221.2 0.0 copy-start.1
  221.2 2.3 %copy.41 = bf16[512,1024]{1,0:T(8,128)(2,1)} copy(bf16[512,1024]{1,0:T(8,128)(2,1)} %get-tuple-element.117) | data formatting | bytes 2097152
  223.5 3.2 %copy.42 = f32[512,1024]{1,0:T(8,128)} copy(f32[512,1024]{1,0:T(8,128)} %get-tuple-element.118) | data formatting | bytes 4194304
  226.7 0.0 copy-done.3
  226.7 0.7 copy.43
  227.4 0.0 copy-done.4
  227.4 0.7 copy.44
  228.1 0.0 copy-done.2
  228.1 0.8 copy.45
  228.9 0.0 copy-done.5
  228.9 0.0 copy-done.1
  228.9 0.8 copy.46
Async XLA Ops:
  9.7 68.8 %copy-start.6 = (bf16[1024]{0:T(1024)(128)(2,1)S(1)}, bf16[1024]{0:T(1024)(128)(2,1)}, u32[]{:S(2)}) copy-start(bf16[1024]{0:T(1024)(128)(2,1)} %param.25) | copy-start | bytes 6148
  9.7 69.4 %copy-start.7 = (bf16[1024]{0:T(1024)(128)(2,1)S(1)}, bf16[1024]{0:T(1024)(128)(2,1)}, u32[]{:S(2)}) copy-start(bf16[1024]{0:T(1024)(128)(2,1)} %param.29) | copy-start | bytes 6148
  74.3 51.2 %collective-permute-start = (bf16[4,128,1024]{2,1,0:T(8,128)(2,1)}, bf16[4,128,1024]{2,1,0:T(8,128)(2,1)S(1)}, u32[]{:S(2)}, u32[]{:S(2)}) collective-permute-start(bf16[4,128,1024]{2,1,0:T(8,128)(2,1)} %get-tuple-element.56), channel_id=1, source_target_pairs={{0,4},{4,0},{8,12},{12,8},{16,20},{20,16},{24,28},{28,24},{1,5},{5... | collective-permute-start | bytes 3145736 | tf_op jit(solution)/shard_map/ppermute | solution.py:1026
  75.8 49.6 %collective-permute-start.1 = (bf16[4,128,1024]{2,1,0:T(8,128)(2,1)}, bf16[4,128,1024]{2,1,0:T(8,128)(2,1)}, u32[]{:S(2)}, u32[]{:S(2)}) collective-permute-start(bf16[4,128,1024]{2,1,0:T(8,128)(2,1)} %get-tuple-element.58), channel_id=1, source_target_pairs={{0,8},{4,12},{8,0},{12,4},{16,24},{20,28},{24,16},{28,20},{1,9},{5... | collective-permute-start | bytes 3145736 | tf_op jit(solution)/shard_map/ppermute | solution.py:1026
  77.4 48.1 %collective-permute-start.2 = (bf16[512,1024]{1,0:T(8,128)(2,1)}, bf16[512,1024]{1,0:T(8,128)(2,1)}, u32[]{:S(2)}, u32[]{:S(2)}) collective-permute-start(bf16[512,1024]{1,0:T(8,128)(2,1)} %get-tuple-element.60), channel_id=1, source_target_pairs={{0,2},{1,3},{2,0},{3,1},{4,6},{5,7},{6,4},{7,5},{8,10},{9,11},{10,... | collective-permute-start | bytes 3145736 | tf_op jit(solution)/shard_map/ppermute | solution.py:1022
  125.5 1.0 copy-start
  216.1 10.6 %copy-start.3 = (f32[128,768]{1,0:T(8,128)S(1)}, f32[128,768]{1,0:T(8,128)}, u32[]{:S(2)}) copy-start(f32[128,768]{1,0:T(8,128)} %get-tuple-element.123) | copy-start | bytes 1179652
  216.2 11.3 %copy-start.4 = (f32[128,256]{1,0:T(8,128)S(1)}, f32[128,256]{1,0:T(8,128)}, u32[]{:S(2)}) copy-start(f32[128,256]{1,0:T(8,128)} %get-tuple-element.125) | copy-start | bytes 393220
  216.2 11.9 %copy-start.2 = (f32[128,1024]{1,0:T(8,128)S(1)}, f32[128,1024]{1,0:T(8,128)}, u32[]{:S(2)}) copy-start(f32[128,1024]{1,0:T(8,128)} %get-tuple-element.127) | copy-start | bytes 1572868
  219.4 9.5 %copy-start.5 = (f32[1,1024]{1,0:T(1,128)}, f32[1,1024]{1,0:T(1,128)S(1)}, u32[]{:S(2)}) copy-start(f32[1,1024]{1,0:T(1,128)S(1)} %get-tuple-element.70) | copy-start | bytes 12292
  221.2 7.7 %copy-start.1 = (f32[512,256]{1,0:T(8,128)S(1)}, f32[512,256]{1,0:T(8,128)}, u32[]{:S(2)}) copy-start(f32[512,256]{1,0:T(8,128)} %get-tuple-element.129) | copy-start | bytes 1572868

commit v4 on v3

--- a/solution.py
+++ b/solution.py
@@ -57,7 +57,7 @@
             small[...] = jnp.zeros_like(small)
             smallf[...] = jnp.zeros_like(smallf)
 
-    normed, _ = norm_parts(x_ref[...])
+    normed, _unused = norm_parts(x_ref[...])
     scale = gain[...].astype(F32)
     nm = (normed * scale + shift[...].astype(F32)).astype(BF)
     dy = dy_ref[...]
@@ -131,7 +131,7 @@
 def proj_kernel(nh, prev, pos, *refs):
     x_ref, dy_ref, wq, wk, wv, bq, bk, bv, wo, gain, shift, cos, sin = refs[:13]
     qt, kt, vt, dot, kn, vn, na_ref = refs[13 + (7 if prev else 0) :]
-    normed, _ = norm_parts(x_ref[...])
+    normed, _unused = norm_parts(x_ref[...])
     na = (normed * gain[...].astype(F32) + shift[...].astype(F32)).astype(BF)
     na_ref[...] = na
     co = cos[...]
@@ -196,8 +196,8 @@
     )(pos, x, dy, w_qkv, w_qkv, w_qkv, b_qkv, b_qkv, b_qkv, w_out, gain, shift, cos, sin, *(prev or ()))
 
 
-def head_kernel(nh, x_hbm, dy_hbm, wu_hbm, wd_hbm, wqkv_hbm, wo_hbm, bu, bq, gain_m, shift_m, gain_a, shift_a, freqs, lens,
-                g_out, na_out, dy_out, qt, kt, vt, dot, kn, vn, cos, sin, p_own, p_far, up_keep, up_send, dn_keep, dn_send,
+def head_kernel(nh, x_hbm, dy_hbm, wu_hbm, wd_hbm, wqkv_hbm, wo_hbm, vec, lens,
+                g_out, na_out, dy_out, qt, kt, vt, dot, kn, vn, cos, sin, p_own, p_far, up_keep, up_send, dn0, dn1, dn2, dn3,
                 small, smallf,
                 xs, dys, wu, wd, wqkv, wt, wo, bias_t, parts, far_in, near_in, dwu, dwd, load, send, recv):
     step = pl.program_id(0)
@@ -260,7 +260,7 @@
             c.wait()
         for k in range(3):
             wt[k * w : (k + 1) * w, :] = wqkv[:, k * w : (k + 1) * w].T
-            row = bq[:, pl.ds(pl.multiple_of(k * d + j * w, 128), w)].astype(F32)
+            row = vec[8 + k : 9 + k, pl.ds(pl.multiple_of(j * w, 128), w)]
             bias_t[k * w : (k + 1) * w, :] = jnp.broadcast_to(row, (128, w)).T
 
     @pl.when(step == 1)
@@ -278,14 +278,14 @@
         copies[8].wait_recv()
         copies[9].wait_recv()
 
-    normed, _ = norm_parts(xs[step])
-    scale = gain_m[...].astype(F32)
-    nm = (normed * scale + shift_m[...].astype(F32)).astype(BF)
-    na = (normed * gain_a[...].astype(F32) + shift_a[...].astype(F32)).astype(BF)
+    normed, _unused = norm_parts(xs[step])
+    scale = vec[2:3, :]
+    nm = (normed * scale + vec[3:4, :]).astype(BF)
+    na = (normed * vec[0:1, :] + vec[1:2, :]).astype(BF)
     dy = dys[step]
     na_out[...] = na
     dy_out[...] = dy
-    pre = mm(nm, wu[...]) + bu[:, pl.ds(pl.multiple_of(j * f, 128), f)].astype(F32)
+    pre = mm(nm, wu[...]) + vec[pl.ds(4 + j, 1), :]
     cdf = 0.5 + 0.5 * lax.erf(pre * (0.5**0.5))
     hid = (pre * cdf).astype(BF)
     slope = cdf + pre * (jnp.exp(-0.5 * pre * pre) * 0.3989422804014327)
@@ -319,13 +319,12 @@
         copies[12].start()
         rows = up_keep.shape[1]
         for b in range(4):
-            for ref, acc, at in (
-                (up_keep, dwu, 2 * b + i % 2),
-                (up_send, dwu, 2 * b + 1 - i % 2),
-                (dn_keep, dwd, 4 * (b // 2) + 2 * ((i // 2) % 2) + b % 2),
-                (dn_send, dwd, 4 * (b // 2) + 2 * (1 - (i // 2) % 2) + b % 2),
-            ):
-                ref[b] = acc[pl.ds(pl.multiple_of(at * rows, rows), rows), :].astype(BF)
+            for ref, at in ((up_keep, 2 * b + i % 2), (up_send, 2 * b + 1 - i % 2)):
+                ref[b] = dwu[pl.ds(pl.multiple_of(at * rows, rows), rows), :].astype(BF)
+            ref = (dn0, dn1, dn2, dn3)[b]
+            for x in range(2):
+                at = 2 * ((i // 2) ^ b) + x
+                ref[x] = dwd[pl.ds(pl.multiple_of(at * rows, rows), rows), :].astype(BF)
 
     lane = lax.broadcasted_iota(jnp.int32, (1, own), 1)
     far = jnp.where(lane < half, j ^ 2, j ^ 3) * own + (step - 2) * half + lane % half
@@ -335,7 +334,11 @@
     for s in range(lens.shape[0] - 1):
         total = total + lens[s]
         begin = jnp.where(index >= total, total, begin)
-    angle = jnp.concatenate([freqs[...]] * (own // 128), axis=1) * (index - begin).astype(F32)
+    sub = lax.broadcasted_iota(jnp.int32, (HALF, own), 0)
+    freqs = jnp.zeros((HALF, own), F32)
+    for k in range(HALF):
+        freqs = jnp.where(sub == k, float(FREQS[k]), freqs)
+    angle = freqs * (index - begin).astype(F32)
     co = jnp.cos(angle)
     si = jnp.sin(angle)
     cos[...] = co
@@ -377,7 +380,7 @@
             c.wait_send()
 
 
-def head_stage(x, dy, w_up, w_down, w_qkv, w_out, bu, bq, gm, sm, ga, sa, freqs, lens, n, cid):
+def head_stage(x, dy, w_up, w_down, w_qkv, w_out, vec, lens, n, cid):
     own, d = x.shape
     tok = own * n
     w = d // n
@@ -393,16 +396,14 @@
         functools.partial(head_kernel, w // HD),
         grid=(n,),
         in_specs=[hbm] * 6
-        + [const((1, w_up.shape[1])), const((1, 3 * d))]
-        + [const((1, d))] * 4
-        + [const((HALF, 128)), pl.BlockSpec(memory_space=pltpu.SMEM)],
+        + [const((16, d)), pl.BlockSpec(memory_space=pltpu.SMEM)],
         out_specs=[nat(d)] * 3
         + [lane(w)] * 4
         + [nat(w)] * 2
         + [lane(HALF)] * 2
         + [const((own, d))] * 2
         + [const((4, d // 8, f))] * 2
-        + [const((4, f // 8, d))] * 2
+        + [const((2, f // 8, d))] * 4
         + [const((8, d)), const((8, f))],
         out_shape=tuple(
             [sds((tok, d), BF)] * 3
@@ -411,7 +412,7 @@
             + [sds((HALF, tok), F32)] * 2
             + [sds((own, d), BF)] * 2
             + [sds((4, d // 8, f), BF)] * 2
-            + [sds((4, f // 8, d), BF)] * 2
+            + [sds((2, f // 8, d), BF)] * 4
             + [sds((8, d), F32), sds((8, f), F32)]
         ),
         scratch_shapes=[
@@ -439,7 +440,7 @@
             flops=12 * tok * d * f + 10 * tok * d * w, bytes_accessed=12 * tok * d + 8 * d * f, transcendentals=2 * tok * f
         ),
         name="head_stage",
-    )(x, dy, w_up, w_down, w_qkv, w_out, bu, bq, gm, sm, ga, sa, freqs, lens)
+    )(x, dy, w_up, w_down, w_qkv, w_out, vec, lens)
 
 
 def attn_kernel(nh, tok, blk, per, halved, lens, rel, cos, sin, qt, kt, vt, dot, kn, vn,
@@ -669,11 +670,11 @@
     )(pos, gt, na, gm, w_qkv, w_qkv, w_qkv, gain, shift)
 
 
-def tail_kernel(gt_h, na_h, gm_h, ctx_h, dya_h, wqkv_h, wo_h, upk_h, upo_h, dnk_h, dno_h, x_h, dyo_h, pown_h, py_h,
-                ga, sa, bo, bd, small, smallf,
-                out_ref, gin_ref, wup_ref, wdn_ref, wq_ref, wout_ref, sums_ref,
-                gt, na, gm, ctx, dya, wqkv, wo, upk, upo, dnk, dno, xo, dyo, pown, py,
-                ctx_in, up4, dn4, up_in, dn_in, up2, dn2, up_in2, dn_in2,
+def tail_kernel(gt_h, na_h, gm_h, ctx_h, dya_h, wqkv_h, wo_h, upk_h, upo_h, dn0_h, dn1_h, dn2_h, dn3_h, x_h, pown_h, py_h,
+                vec, small, smallf,
+                out_ref, g_ref, wup_ref, wdn_ref, wq_ref, wout_ref, sums_ref,
+                gt, na, gm, ctx, dya, wqkv, wo, upk, upo, dn, xo, pown, py,
+                ctx_in, up4, up_in, dn_in, up2, dn2, up_in2,
                 dwq, qa_in, qb_in, qa4, qb4, qa_in2, qb_in2, qa2, qb2, qa_in3, qb_in3, qfin, q_own,
                 dwo, wo_in, wo4, wo_in2, wo2, wo_in3, piece, owner_in,
                 far_in, near_in, far_sum, y_in, sm, sm_in, load, send, recv):
@@ -701,12 +702,13 @@
         return pltpu.make_async_copy(src, dst, load.at[k])
 
     loads = [
-        local(upk_h, upk, 0), local(upo_h, upo, 1), local(dnk_h, dnk, 2), local(dno_h, dno, 3),
+        local(upk_h, upk, 0), local(upo_h, upo, 1), local(dn0_h, dn.at[0], 2), local(dn1_h, dn.at[1], 3),
         local(gt_h, gt, 4), local(na_h, na, 5), local(ctx_h, ctx, 6), local(dya_h, dya, 7), local(gm_h, gm, 8),
         local(wqkv_h.at[:, pl.ds(j * w, w)], wqkv.at[:, pl.ds(0, w)], 9),
         local(wqkv_h.at[:, pl.ds(d + j * w, w)], wqkv.at[:, pl.ds(w, w)], 10),
         local(wqkv_h.at[:, pl.ds(2 * d + j * w, w)], wqkv.at[:, pl.ds(2 * w, w)], 11),
-        local(wo_h, wo, 12), local(x_h, xo, 13), local(dyo_h, dyo, 14), local(pown_h, pown, 15), local(py_h, py, 16),
+        local(wo_h, wo, 12), local(x_h, xo, 13), local(pown_h, pown, 14), local(py_h, py, 15),
+        local(dn2_h, dn.at[2], 16), local(dn3_h, dn.at[3], 17),
     ]
     c_ctx = [
         remote(ctx_h.at[:, pl.ds(2 * own, half)], ctx_in.at[1, :, lo], across),
@@ -716,9 +718,8 @@
         remote(ctx_h.at[:, pl.ds(own, own)], ctx_in.at[0], core),
     ]
     c_up0 = remote(up4.at[:, 1 - b0], up_in, p0)
-    c_dnx = remote(dn4.at[:, 1 - bx], dn_in, px)
+    c_dnx = remote(dn2.at[1 - bx], dn_in, px)
     c_up1 = remote(up2.at[1 - b1], up_in2, p1)
-    c_dn1 = remote(dn2.at[1 - b1], dn_in2, p1)
     rows = dwq.shape[3] // 2
     ra, rb = pl.ds(0, rows), pl.ds(rows, rows)
     c_qa = remote(dwq.at[:, :, 1 - bx, ra], qa_in, px)
@@ -775,7 +776,9 @@
         loads[k].wait()
     up4[:, 1 - b0] = added(upk[:, 1 - b0], upo[:, 1 - b0]).astype(BF)
     c_up0.start()
-    dn4[:, 1 - bx] = added(dnk[:, 1 - bx], dno[:, 1 - bx]).astype(BF)
+    loads[16].wait()
+    loads[17].wait()
+    dn2[...] = (added(dn[0], dn[1]) + added(dn[2], dn[3])).astype(BF)
     c_dnx.start()
 
     loads[4].wait()
@@ -795,7 +798,7 @@
 
     for k in range(8, 12):
         loads[k].wait()
-    scale = ga[...].astype(F32)
+    scale = vec[0:1, :]
     ones = jnp.zeros((1, d), F32)
     s_gain, s_shift, s_bias = ones, ones, jnp.zeros((1, 3 * w), F32)
 
@@ -822,10 +825,6 @@
     c_g[0].wait_recv()
     far_sum[lo] = added(gm[2 * own : 2 * own + half], far_in[lo]).astype(BF)
     c_y[0].start()
-    c_dnx.wait_recv()
-    mine = added(dnk[:, bx], dno[:, bx]) + dn_in[...].astype(F32)
-    dn2[...] = mine.astype(BF)
-    c_dn1.start()
     c_g[1].wait_recv()
     far_sum[hi] = added(gm[3 * own : 3 * own + half], far_in[hi]).astype(BF)
     c_y[1].start()
@@ -834,7 +833,7 @@
     sums = tile(0, own, sums)
 
     sm[0] = jnp.zeros((16, d), F32)
-    shift = sa[...].astype(F32)
+    shift = vec[1:2, :]
     sm[0, 0:1, :] = (sums[0] - shift * sums[1]) / scale
     sm[0, 1:2, :] = sums[1]
     for k in range(3):
@@ -861,7 +860,7 @@
             c_sm[s + 1].start()
 
     small_step(0)
-    for k in range(12, 17):
+    for k in range(12, 16):
         loads[k].wait()
     attn = mm(ctx[:, :own], wo[pl.ds(pl.multiple_of(j * w, 128), w), :], TN)
     c_ctx[4].wait_recv()
@@ -871,7 +870,7 @@
     attn += mm(ctx_in[1], wo[pl.ds(pl.multiple_of((j ^ 2) * w, 128), w), :], TN)
     attn += mm(ctx_in[2], wo[pl.ds(pl.multiple_of((j ^ 3) * w, 128), w), :], TN)
     out_ref[...] = (
-        xo[...].astype(F32) + attn + added(pown[...], py[...]) + (bo[...].astype(F32) + bd[...].astype(F32))
+        xo[...].astype(F32) + attn + added(pown[...], py[...]) + (vec[11:12, :] + vec[12:13, :])
     ).astype(BF)
     small_step(1)
 
@@ -886,9 +885,9 @@
     c_wo1.start()
     small_step(2)
     c_up1.wait_recv()
-    wup_ref[...] = added(up2[b1], up_in2[...])
-    c_dn1.wait_recv()
-    piece[: dn2.shape[1], :] = added(dn2[b1], dn_in2[...]).astype(BF)
+    wup_ref[...] = added(up2[b1], up_in2[...]).astype(BF)
+    c_dnx.wait_recv()
+    piece[: dn2.shape[1], :] = added(dn2[bx], dn_in[...]).astype(BF)
     small_step(3)
     c_qa1.wait_recv()
     c_qb1.wait_recv()
@@ -923,13 +922,9 @@
 
     c_g[2].wait_recv()
     near = added(gm[0:own], near_in[...])
-    normed, inv = norm_parts(xo[...])
     c_y[0].wait_recv()
     c_y[1].wait_recv()
-    g = near + y_in[...].astype(F32)
-    gin_ref[...] = dyo[...].astype(F32) + inv * (
-        g - jnp.mean(g, axis=-1, keepdims=True) - normed * jnp.mean(g * normed, axis=-1, keepdims=True)
-    )
+    g_ref[...] = near + y_in[...].astype(F32)
 
     for t in range(3):
 
@@ -937,7 +932,7 @@
         def _():
             c_q[t].wait_recv()
 
-        wq_ref[:, t * w : (t + 1) * w] = q_own[t].astype(F32).T
+        wq_ref[:, t * w : (t + 1) * w] = q_own[t].astype(F32).T.astype(BF)
     for r in range(4):
         di, dj = dests[r]
 
@@ -948,10 +943,10 @@
     nd = dn2.shape[1]
     no = wo2.shape[1]
     for a in range(4):
-        wdn_ref[a * nd : (a + 1) * nd, :] = owner_in[a, :nd].astype(F32)
-        wout_ref[a * no : (a + 1) * no, :] = owner_in[a, nd:].astype(F32)
-
-    for c in c_ctx + [c_up0, c_dnx, c_up1, c_dn1, c_qa, c_qb, c_qa0, c_qbx, c_qa1, c_qb1, c_wox, c_wo0, c_wo1] + c_g + c_y + c_sm:
+        wdn_ref[a * nd : (a + 1) * nd, :] = owner_in[a, :nd]
+        wout_ref[a * no : (a + 1) * no, :] = owner_in[a, nd:]
+
+    for c in c_ctx + [c_up0, c_dnx, c_up1, c_qa, c_qb, c_qa0, c_qbx, c_qa1, c_qb1, c_wox, c_wo0, c_wo1] + c_g + c_y + c_sm:
         c.wait_send()
     for t in range(3):
 
@@ -967,7 +962,7 @@
             c_own[r].wait_send()
 
 
-def tail_stage(gt, na, gm, ctx, dya, w_qkv, w_out, upk, upo, dnk, dno, x, dy, pown, py, ga, sa, bo, bd, small, smallf, cid):
+def tail_stage(gt, na, gm, ctx, dya, w_qkv, w_out, upk, upo, dn, x, pown, py, vec, small, smallf, cid):
     own, d = x.shape
     tok = na.shape[0]
     w = d // 4
@@ -980,18 +975,18 @@
     r2 = 3 * w // 2
     return pl.pallas_call(
         tail_kernel,
-        in_specs=[hbm] * 15 + [vm] * 6,
+        in_specs=[hbm] * 16 + [vm] * 3,
         out_specs=[vm] * 7,
         out_shape=(
-            sds((own, d), BF), sds((own, d), F32), sds((nb, d), F32), sds((4 * nb, w), F32),
-            sds((nb, 3 * w), F32), sds((4 * no, w), F32), sds((16, d), F32),
+            sds((own, d), BF), sds((own, d), F32), sds((nb, d), BF), sds((4 * nb, w), BF),
+            sds((nb, 3 * w), BF), sds((4 * no, w), BF), sds((16, d), F32),
         ),
         scratch_shapes=[
             big(3 * w, tok), big(tok, d), big(tok, d), big(w, tok), big(tok, d), big(d, 3 * w), big(d, d),
-            big(2, 2, nb, d), big(2, 2, nb, d), big(2, 2, nb, d), big(2, 2, nb, d),
-            big(own, d), big(own, d), big(own, d), big(own, d),
-            big(3, w, own), big(2, 2, nb, d), big(2, 2, nb, d), big(2, nb, d), big(2, nb, d),
-            big(2, nb, d), big(2, nb, d), big(nb, d), big(nb, d),
+            big(2, 2, nb, d), big(2, 2, nb, d), big(4, 2, nb, d),
+            big(own, d), big(own, d), big(own, d),
+            big(3, w, own), big(2, 2, nb, d), big(2, nb, d), big(nb, d),
+            big(2, nb, d), big(2, nb, d), big(nb, d),
             big(2, 2, 2, 3 * w, 128), big(2, 2, r2, 128), big(2, 2, r2, 128), big(2, 2, r2, 128), big(2, 2, r2, 128),
             big(2, r2, 128), big(2, r2, 128), big(2, r2, 128), big(2, r2, 128), big(r2, 128), big(r2, 128),
             big(3, w, 128), big(3, w, 128),
@@ -999,14 +994,56 @@
             big(nb + no, d), big(4, nb + no, w),
             big(own, d), big(own, d), big(own, d), big(own, d),
             pltpu.VMEM((6, 16, d), F32), pltpu.VMEM((5, 16, d), F32),
-            pltpu.SemaphoreType.DMA((17,)), pltpu.SemaphoreType.DMA((40,)), pltpu.SemaphoreType.DMA((40,)),
+            pltpu.SemaphoreType.DMA((18,)), pltpu.SemaphoreType.DMA((40,)), pltpu.SemaphoreType.DMA((40,)),
         ],
         compiler_params=pltpu.CompilerParams(vmem_limit_bytes=VMEM_LIMIT, collective_id=cid, has_side_effects=True),
         cost_estimate=pl.CostEstimate(
             flops=14 * tok * d * w, bytes_accessed=10 * tok * d, transcendentals=0
         ),
         name="tail_stage",
-    )(gt, na, gm, ctx, dya, w_qkv, w_out, upk, upo, dnk, dno, x, dy, pown, py, ga, sa, bo, bd, small, smallf)
+    )(gt, na, gm, ctx, dya, w_qkv, w_out, upk, upo, *dn, x, pown, py, vec, small, smallf)
+
+
+def final_kernel(out_t, g_ref, x_ref, dy_ref, wup, wdn, wq, wout, sums,
+                 out, gin, ga, sa, gm, sm, dwq, bq, dwout, bo, dwup, bu, dwdn, bd):
+    out[...] = out_t[...]
+    normed, inv = norm_parts(x_ref[...])
+    g = g_ref[...]
+    gin[...] = dy_ref[...].astype(F32) + inv * (
+        g - jnp.mean(g, axis=-1, keepdims=True) - normed * jnp.mean(g * normed, axis=-1, keepdims=True)
+    )
+
+    @pl.when(pl.program_id(0) == 0)
+    def _():
+        d = sums.shape[1]
+        for ref, first, count in ((ga, 0, 1), (sa, 1, 1), (bq, 2, 3), (gm, 5, 1), (sm, 6, 1), (bo, 7, 1), (bd, 7, 1), (bu, 8, 4)):
+            for k in range(count):
+                ref[k * d : (k + 1) * d] = sums[first + k, :]
+        dwup[...] = wup[...].astype(F32)
+        dwdn[...] = wdn[...].astype(F32)
+        dwq[...] = wq[...].astype(F32)
+        dwout[...] = wout[...].astype(F32)
+
+
+def final_stage(out_t, g, x, dy, wup, wdn, wq, wout, sums, steps=4):
+    own, d = x.shape
+    row = pl.BlockSpec((own // steps, d), lambda i: (i, 0))
+    const = lambda v: pl.BlockSpec(v.shape, lambda i: (0,) * len(v.shape))
+    sds = lambda *s: jax.ShapeDtypeStruct(s, F32)
+    like = lambda v: sds(*v.shape)
+    outs = (
+        jax.ShapeDtypeStruct((own, d), BF), sds(own, d), sds(d), sds(d), sds(d), sds(d), like(wq), sds(3 * d),
+        like(wout), sds(d), like(wup), sds(4 * d), like(wdn), sds(d),
+    )
+    return pl.pallas_call(
+        final_kernel,
+        grid=(steps,),
+        in_specs=[row, row, row, row] + [const(v) for v in (wup, wdn, wq, wout, sums)],
+        out_specs=[row, row] + [const(v) for v in outs[2:]],
+        out_shape=outs,
+        compiler_params=pltpu.CompilerParams(vmem_limit_bytes=VMEM_LIMIT),
+        name="final_stage",
+    )(out_t, g, x, dy, wup, wdn, wq, wout, sums)
 
 
 def layout(seq_lens, index):
@@ -1028,30 +1065,26 @@
 
 def fast_body(inputs, lengths, attn_gain, attn_shift, mlp_gain, mlp_shift, w_qkv, b_qkv, w_out, b_out,
               w_up, b_up, w_down, b_down, cotangent):
-    own, _ = inputs.shape
+    own, d = inputs.shape
     n = 4
     tok = own * n
-    j = lax.axis_index("head")
-    pos = j.astype(jnp.int32).reshape(1)
-    rows = lambda v: v.reshape(1, -1)
-    ga, sa, gm, sm = rows(attn_gain), rows(attn_shift), rows(mlp_gain), rows(mlp_shift)
-    bq, bu = rows(b_qkv), rows(b_up)
+    w = d // n
+    pos = lax.axis_index("head").astype(jnp.int32).reshape(1)
     lens = lengths[0]
-
-    freqs = jnp.asarray(np.broadcast_to(FREQS[:, None], (HALF, 128)))
-    (g_mlp, na, dy_all, qt, kt, vt, dot, kn, vn, cos, sin, p_own, p_far, up_keep, up_send, dn_keep, dn_send, small,
-     smallf) = head_stage(inputs, cotangent, w_up, w_down, w_qkv, w_out, bu, bq, gm, sm, ga, sa, freqs, lens, n, 0)
+    vec = jnp.concatenate(
+        [attn_gain, attn_shift, mlp_gain, mlp_shift, b_up, b_qkv, b_out, b_down, jnp.zeros((3 * d,), BF)]
+    ).astype(F32).reshape(16, d)
+    (g_mlp, na, dy_all, qt, kt, vt, dot, kn, vn, cos, sin, p_own, p_far, up_keep, up_send, *dn, small,
+     smallf) = head_stage(inputs, cotangent, w_up, w_down, w_qkv, w_out, vec, lens, n, 0)
     up_other = dp_perm(up_send, 1)
-    dn_other = dp_perm(dn_send, 2)
+    dn = [dn[0]] + [dp_perm(dn[k], 2 * k) for k in (1, 2, 3)]
     p_y = head_perm(p_far, 2)
     gt, ctx = attention(lens, pos, cos, sin, qt, kt, vt, dot, kn, vn, own, tok // 2, halved=True)
     quad = lambda v: v.reshape(2, 2, v.shape[1], v.shape[2])
-    output, grad_inputs, grad_w_up, grad_w_down, grad_w_qkv, grad_w_out, sums = tail_stage(
-        gt, na, g_mlp, ctx, dy_all, w_qkv, w_out, quad(up_keep), quad(up_other), quad(dn_keep), quad(dn_other),
-        inputs, cotangent, p_own, p_y, ga, sa, rows(b_out), rows(b_down), small, smallf, 1
+    out_t, g, wup, wdn, wq, wout, sums = tail_stage(
+        gt, na, g_mlp, ctx, dy_all, w_qkv, w_out, quad(up_keep), quad(up_other), dn, inputs, p_own, p_y, vec, small, smallf, 1
     )
-    return (output, grad_inputs, sums[0], sums[1], sums[5], sums[6], grad_w_qkv, sums[2:5].reshape(-1),
-            grad_w_out, sums[7], grad_w_up, sums[8:12].reshape(-1), grad_w_down, sums[7])
+    return tuple(final_stage(out_t, g, inputs, cotangent, wup, wdn, wq, wout, sums))
 
 
 def general_body(inputs, lengths, attn_gain, attn_shift, mlp_gain, mlp_shift, w_qkv, b_qkv, w_out, b_out,
@@ -1061,6 +1094,7 @@
     n_dp = lax.axis_size("dp")
     tok = own * n
     w = d // n
+    f = w_up.shape[1] // n
     j = lax.axis_index("head")
     pos = j.astype(jnp.int32).reshape(1)
     rows = lambda v: v.reshape(1, -1)
@@ -1072,7 +1106,7 @@
     over_head = lambda v: lax.psum_scatter(v, "head", scatter_dimension=0, tiled=True)
     x_all = gather(inputs)
     dy_all = gather(cotangent)
-    _, position = layout(lens, jnp.arange(tok, dtype=jnp.int32))
+    first, position = layout(lens, jnp.arange(tok, dtype=jnp.int32))
     freqs = 10000.0 ** (-(2.0 * jnp.arange(HALF, dtype=F32)) / ROT)
     angle = freqs[:, None] * position.astype(F32)[None, :]
     cos, sin = jnp.cos(angle), jnp.sin(angle)

time: 230 us -> 216 us (0.939)
  the two profiles are of different devices: /device:TPU:16 before, /device:TPU:7 now
where the time goes in v4:
time: 216 us
  Pallas kernels  203 us (94%)
  local copies, waits for them, and re-layouts  7.26 us (3%)
  starting transfers between devices  4.59 us (2%)
    pallas_call x1, Pallas kernels, tail_stage(): pl.pallas_call(tail_kernel, in_specs=[hbm] * 16 + [vm] * 3, out_specs=[vm...  81.9 us
    pallas_call x1, Pallas kernels, head_stage(): pl.pallas_call(functools.partial(head_kernel, w // HD), grid=(n,), in_spe...  64.8 us
    pallas_call x1, Pallas kernels, attention(): pl.pallas_call(functools.partial(attn_kernel, nh, tok, blk, chunk // blk,...  50.1 us
    unnamed x12, local copies, waits for them, and re-layouts  6.61 us
    pallas_call x1, Pallas kernels, final_stage(): pl.pallas_call(final_kernel, grid=(steps,), in_specs=[row, row, row, row]...  6.43 us
  transfers between devices with their start and end apart: 5, of which 0 were waited for; matrix products, arithmetic and copies ran while one was open for 0% of the time, Pallas kernels for 23%

profile of v4, /device:TPU:7, one launch (start us, length us, event | category | flops | bytes accessed | tf_op | source)
XLA Modules:
  0.0 216.0 jit_solution(6905898474006787928)
XLA Ops:
  0.6 0.7 constant_dynamic-update-slice_fusion.8
  1.3 0.7 constant_dynamic-update-slice_fusion.7
  2.0 0.7 constant_dynamic-update-slice_fusion.6
  2.7 0.7 constant_dynamic-update-slice_fusion.5
  3.4 0.7 constant_dynamic-update-slice_fusion.4
  4.1 0.7 constant_dynamic-update-slice_fusion.3
  4.8 0.7 constant_dynamic-update-slice_fusion.2
  5.5 0.7 constant_dynamic-update-slice_fusion.1
  6.2 0.6 reshape.44.vec
  6.8 64.8 %head_stage.1 = (bf16[2048,1024]{1,0:T(8,128)(2,1)}, bf16[2048,1024]{1,0:T(8,128)(2,1)}, bf16[2048,1024]{1,0:T(8,128)(2,1)}, bf16[256,2048]{1,0:T(8,128)(2,1)}, ...) custom-call(bf16[512,1024]{1,0:T(8,128)(2,1)} %x_ref.1, ...), custom_call_target="tpu_custom_call" | custom-call | flops 31138512896 | bytes 33554432 | tf_op jit(solution)/shard_map/head_stage/pallas_call | solution.py:395
  71.7 0.3 collective-permute-start
  72.0 0.7 collective-permute-start.4
  72.6 1.3 collective-permute-start.1
  73.9 2.3 %collective-permute-start.2 = (bf16[2,128,1024]{2,1,0:T(8,128)(2,1)}, bf16[2,128,1024]{2,1,0:T(8,128)(2,1)}, u32[]{:S(2)}, u32[]{:S(2)}) collective-permute-start(bf16[2,128,1024]{2,1,0:T(8,128)(2,1)} %get-tuple-element.61), channel_id=1, source_target_pairs={{0,16},{4,20},{8,24},{12,28},{16,0},{20,4},{24,8},{28,12},{1,17},{... | collective-permute-start | bytes 1572872 | tf_op jit(solution)/shard_map/ppermute | solution.py:1063
  76.2 0.0 collective-permute-start.3
  76.2 50.1 %attention.1 = (bf16[768,2048]{1,0:T(8,128)(2,1)}, bf16[256,2048]{1,0:T(8,128)(2,1)}) custom-call(s32[4]{0:T(128)} %bitcast.7, s32[1]{0:T(128)} %bitcast.1.rel, f32[8,2048]{1,0:T(8,128)} %get-tuple-element.44.cos, f32[8,2048]{1,0:T(8,128)} %get-tuple-element.45.sin, bf16[256,2048]{1,0:T(8,128)(2,1)} %get-tuple-element.46.qt, ...), custom_call_target="tpu_custom_call" | custom-call | flops 10737418240 | bytes 10485760 | tf_op jit(solution)/shard_map/attention/pallas_call | solution.py:573
  126.3 0.0 collective-permute-done.1.dn1_h
  126.3 0.0 copy-start.1
  126.3 0.0 collective-permute-done.2.dn2_h
  126.3 0.0 collective-permute-done.3.dn3_h
  126.4 0.0 collective-permute-done
  126.4 0.0 copy-start
  126.4 0.0 collective-permute-done.4.py_h
  126.4 0.7 copy-done.1
  127.1 0.3 copy-done
  127.5 81.9 %tail_stage.1 = (bf16[512,1024]{1,0:T(8,128)(2,1)}, f32[512,1024]{1,0:T(8,128)}, bf16[128,1024]{1,0:T(8,128)(2,1)}, bf16[512,256]{1,0:T(8,128)(2,1)}, bf16[128,7...) custom-call(bf16[768,2048]{1,0:T(8,128)(2,1)} %get-tuple-element.52.gt_h, ...), custom_call_target="tpu_custom_call" | custom-call | flops 7516192768 | bytes 20971520 | tf_op jit(solution)/shard_map/tail_stage/pallas_call | solution.py:976
  209.4 6.4 %final_stage.1 = (bf16[512,1024]{1,0:T(8,128)(2,1)}, f32[512,1024]{1,0:T(8,128)}, f32[1024]{0:T(1024)}, f32[1024]{0:T(1024)}, f32[1024]{0:T(1024)}, /*index=5*/f...) custom-call(bf16[512,1024]{1,0:T(8,128)(2,1)} %get-tuple-element.67., ...), custom_call_target="tpu_custom_call" | custom-call | tf_op jit(solution)/shard_map/final_stage/pallas_call | solution.py:1038
  (1 shorter events, 0.0 us)
Async XLA Ops:
  71.7 54.7 %collective-permute-start = (bf16[4,128,1024]{2,1,0:T(8,128)(2,1)}, bf16[4,128,1024]{2,1,0:T(8,128)(2,1)S(1)}, u32[]{:S(2)}, u32[]{:S(2)}) collective-permute-start(bf16[4,128,1024]{2,1,0:T(8,128)(2,1)} %get-tuple-element.58), channel_id=1, source_target_pairs={{0,4},{4,0},{8,12},{12,8},{16,20},{20,16},{24,28},{28,24},{1,5},{5... | collective-permute-start | bytes 3145736 | tf_op jit(solution)/shard_map/ppermute | solution.py:1063
  72.0 54.4 %collective-permute-start.4 = (bf16[512,1024]{1,0:T(8,128)(2,1)}, bf16[512,1024]{1,0:T(8,128)(2,1)}, u32[]{:S(2)}, u32[]{:S(2)}) collective-permute-start(bf16[512,1024]{1,0:T(8,128)(2,1)} %get-tuple-element.64), channel_id=1, source_target_pairs={{0,2},{1,3},{2,0},{3,1},{4,6},{5,7},{6,4},{7,5},{8,10},{9,11},{10,... | collective-permute-start | bytes 3145736 | tf_op jit(solution)/shard_map/ppermute | solution.py:1059
  72.6 53.7 %collective-permute-start.1 = (bf16[2,128,1024]{2,1,0:T(8,128)(2,1)}, bf16[2,128,1024]{2,1,0:T(8,128)(2,1)S(1)}, u32[]{:S(2)}, u32[]{:S(2)}) collective-permute-start(bf16[2,128,1024]{2,1,0:T(8,128)(2,1)} %get-tuple-element.60), channel_id=1, source_target_pairs={{0,8},{4,12},{8,0},{12,4},{16,24},{20,28},{24,16},{28,20},{1,9},{5... | collective-permute-start | bytes 1572872 | tf_op jit(solution)/shard_map/ppermute | solution.py:1063
  73.9 52.4 %collective-permute-start.2 = (bf16[2,128,1024]{2,1,0:T(8,128)(2,1)}, bf16[2,128,1024]{2,1,0:T(8,128)(2,1)}, u32[]{:S(2)}, u32[]{:S(2)}) collective-permute-start(bf16[2,128,1024]{2,1,0:T(8,128)(2,1)} %get-tuple-element.61), channel_id=1, source_target_pairs={{0,16},{4,20},{8,24},{12,28},{16,0},{20,4},{24,8},{28,12},{1,17},{... | collective-permute-start | bytes 1572872 | tf_op jit(solution)/shard_map/ppermute | solution.py:1063
  76.2 50.1 %collective-permute-start.3 = (bf16[2,128,1024]{2,1,0:T(8,128)(2,1)}, bf16[2,128,1024]{2,1,0:T(8,128)(2,1)}, u32[]{:S(2)}, u32[]{:S(2)}) collective-permute-start(bf16[2,128,1024]{2,1,0:T(8,128)(2,1)} %get-tuple-element.62), channel_id=1, source_target_pairs={{0,24},{4,28},{8,16},{12,20},{16,8},{20,12},{24,0},{28,4},{1,25},{... | collective-permute-start | bytes 1572872 | tf_op jit(solution)/shard_map/ppermute | solution.py:1063
  126.3 0.8 copy-start.1
  126.4 1.1 copy-start

commit v5 on v4

--- a/solution.py
+++ b/solution.py
@@ -22,6 +22,10 @@
 
 def mm(a, b, dims=NN):
     return lax.dot_general(a, b, dims, preferred_element_type=F32)
+
+
+def flat(v):
+    return v.astype(F32).reshape(1, v.shape[0])
 
 
 def norm_parts(x):
@@ -196,7 +200,7 @@
     )(pos, x, dy, w_qkv, w_qkv, w_qkv, b_qkv, b_qkv, b_qkv, w_out, gain, shift, cos, sin, *(prev or ()))
 
 
-def head_kernel(nh, x_hbm, dy_hbm, wu_hbm, wd_hbm, wqkv_hbm, wo_hbm, vec, lens,
+def head_kernel(nh, x_hbm, dy_hbm, wu_hbm, wd_hbm, wqkv_hbm, wo_hbm, gain_a, shift_a, gain_m, shift_m, bu, bq, lens,
                 g_out, na_out, dy_out, qt, kt, vt, dot, kn, vn, cos, sin, p_own, p_far, up_keep, up_send, dn0, dn1, dn2, dn3,
                 small, smallf,
                 xs, dys, wu, wd, wqkv, wt, wo, bias_t, parts, far_in, near_in, dwu, dwd, load, send, recv):
@@ -260,7 +264,7 @@
             c.wait()
         for k in range(3):
             wt[k * w : (k + 1) * w, :] = wqkv[:, k * w : (k + 1) * w].T
-            row = vec[8 + k : 9 + k, pl.ds(pl.multiple_of(j * w, 128), w)]
+            row = flat(bq[pl.ds(pl.multiple_of(k * d + j * w, 256), w)])
             bias_t[k * w : (k + 1) * w, :] = jnp.broadcast_to(row, (128, w)).T
 
     @pl.when(step == 1)
@@ -279,13 +283,13 @@
         copies[9].wait_recv()
 
     normed, _unused = norm_parts(xs[step])
-    scale = vec[2:3, :]
-    nm = (normed * scale + vec[3:4, :]).astype(BF)
-    na = (normed * vec[0:1, :] + vec[1:2, :]).astype(BF)
+    scale = flat(gain_m[...])
+    nm = (normed * scale + flat(shift_m[...])).astype(BF)
+    na = (normed * flat(gain_a[...]) + flat(shift_a[...])).astype(BF)
     dy = dys[step]
     na_out[...] = na
     dy_out[...] = dy
-    pre = mm(nm, wu[...]) + vec[pl.ds(4 + j, 1), :]
+    pre = mm(nm, wu[...]) + flat(bu[pl.ds(pl.multiple_of(j * f, 1024), f)])
     cdf = 0.5 + 0.5 * lax.erf(pre * (0.5**0.5))
     hid = (pre * cdf).astype(BF)
     slope = cdf + pre * (jnp.exp(-0.5 * pre * pre) * 0.3989422804014327)
@@ -380,7 +384,7 @@
             c.wait_send()
 
 
-def head_stage(x, dy, w_up, w_down, w_qkv, w_out, vec, lens, n, cid):
+def head_stage(x, dy, w_up, w_down, w_qkv, w_out, ga, sa, gm, sm, bu, bq, lens, n, cid):
     own, d = x.shape
     tok = own * n
     w = d // n
@@ -396,7 +400,8 @@
         functools.partial(head_kernel, w // HD),
         grid=(n,),
         in_specs=[hbm] * 6
-        + [const((16, d)), pl.BlockSpec(memory_space=pltpu.SMEM)],
+        + [const(v.shape) for v in (ga, sa, gm, sm, bu, bq)]
+        + [pl.BlockSpec(memory_space=pltpu.SMEM)],
         out_specs=[nat(d)] * 3
         + [lane(w)] * 4
         + [nat(w)] * 2
@@ -440,14 +445,15 @@
             flops=12 * tok * d * f + 10 * tok * d * w, bytes_accessed=12 * tok * d + 8 * d * f, transcendentals=2 * tok * f
         ),
         name="head_stage",
-    )(x, dy, w_up, w_down, w_qkv, w_out, vec, lens)
+    )(x, dy, w_up, w_down, w_qkv, w_out, ga, sa, gm, sm, bu, bq, lens)
 
 
 def attn_kernel(nh, tok, blk, per, halved, lens, rel, cos, sin, qt, kt, vt, dot, kn, vn,
-                gt_ref, ctx_ref, exps, peaks, dk, dv, oacc, dqacc, mrow, lrow, drow, qpad, dopad):
+                gt_ref, ctx_ref, exps, low_exps, dk, dv, oacc, dqacc, mpart, lpart, rowsc, qpad, dopad):
     nseq = lens.shape[0]
     nblk = tok // blk
     shift = rel[0]
+    heads = range(nh)
 
     def place(b):
         chunk = (b // per) ^ shift
@@ -457,6 +463,23 @@
             at = jnp.where(chunk < 2, at, 4 + (chunk - 2) + 2 * half)
         return pl.multiple_of(at * blk, blk)
 
+    def rows_of(h):
+        return slice(h * HD, (h + 1) * HD)
+
+    def pair_of(h):
+        return slice((h // 2) * 128, (h // 2) * 128 + 128)
+
+    def fold(v, op):
+        return op(v.reshape(blk // 8, 8, blk), axis=0)
+
+    def begin_of(at):
+        begin = jnp.int32(0)
+        total = jnp.int32(0)
+        for s in range(nseq - 1):
+            total = total + lens[s]
+            begin = jnp.where(at >= total, total, begin)
+        return begin
+
     dk[...] = jnp.zeros_like(dk)
     dv[...] = jnp.zeros_like(dv)
     qpad[...] = jnp.zeros_like(qpad)
@@ -466,75 +489,89 @@
 
     def one_block(i, carry):
         first_tok = i * blk
-        begin = jnp.int32(0)
-        total = jnp.int32(0)
-        for s in range(nseq - 1):
-            total = total + lens[s]
-            begin = jnp.where(total <= first_tok, total, begin)
-        low = begin // blk
+        count = i - begin_of(first_tok) // blk + 1
+        last_begin = begin_of(first_tok + blk - 1)
         cols = pl.ds(place(i), blk)
         query_idx = cols_iota + first_tok
-        start_row = jnp.zeros_like(query_idx)
-        total = jnp.int32(0)
-        for s in range(nseq - 1):
-            total = total + lens[s]
-            start_row = jnp.where(query_idx >= total, total, start_row)
-        for h in range(nh):
+        start_row = begin_of(query_idx)
+        for h in heads:
             half = (h % 2) * HD
-            qpad[h, half : half + HD, :] = qt[h * HD : (h + 1) * HD, cols]
-            dopad[h, half : half + HD, :] = dot[h * HD : (h + 1) * HD, cols]
-        mrow[...] = jnp.full_like(mrow, -1e30)
-        lrow[...] = jnp.zeros_like(lrow)
+            qpad[h, half : half + HD, :] = qt[rows_of(h), cols]
+
+        krow = pl.ds(place(i), blk)
+        kidx = rows_iota + first_tok
+        allowed = (kidx >= start_row) & (kidx <= query_idx)
+        for h in heads:
+            s = jnp.where(allowed, mm(kn[krow, pair_of(h)], qpad[h]), -1e30)
+            exps[h, 0] = s
+            mpart[h] = fold(s, jnp.max)
+
+        def scores(step, c):
+            b = i - step
+            krow = pl.ds(place(b), blk)
+            edge = last_begin > b * blk
+
+            @pl.when(edge)
+            def _():
+                allowed = (rows_iota + b * blk) >= start_row
+                for h in heads:
+                    s = jnp.where(allowed, mm(kn[krow, pair_of(h)], qpad[h]), -1e30)
+                    exps[h, step] = s
+                    mpart[h] = jnp.maximum(mpart[h], fold(s, jnp.max))
+
+            @pl.when(jnp.logical_not(edge))
+            def _():
+                for h in heads:
+                    s = mm(kn[krow, pair_of(h)], qpad[h])
+                    exps[h, step] = s
+                    mpart[h] = jnp.maximum(mpart[h], fold(s, jnp.max))
+
+            return c
+
+        lax.fori_loop(1, count, scores, 0)
+        for h in heads:
+            rowsc[h : h + 1, :] = jnp.max(mpart[h], axis=0, keepdims=True)
+        lpart[...] = jnp.zeros_like(lpart)
         oacc[...] = jnp.zeros_like(oacc)
+
+        def weights(step, c):
+            kcols = pl.ds(place(i - step), blk)
+            for h in heads:
+                e = jnp.exp(exps[h, step] - rowsc[h : h + 1, :])
+                exps[h, step] = e
+                lpart[h] += fold(e, jnp.sum)
+                low = e.astype(BF)
+                low_exps[h, step] = low
+                oacc[h] += mm(vt[rows_of(h), kcols], low)
+            return c
+
+        lax.fori_loop(0, count, weights, 0)
+        for h in heads:
+            half = (h % 2) * HD
+            inv = 1.0 / jnp.sum(lpart[h], axis=0, keepdims=True)
+            o = oacc[h] * inv
+            ctx_ref[rows_of(h), cols] = o.astype(BF)
+            scaled = (dot[rows_of(h), cols].astype(F32) * inv).astype(BF)
+            dopad[h, half : half + HD, :] = scaled
+            rowsc[h : h + 1, :] = jnp.sum(o * scaled.astype(F32), axis=0, keepdims=True)
         dqacc[...] = jnp.zeros_like(dqacc)
-
-        def forward(step, c):
-            b = i - step
-            krow = place(b)
-            kidx = rows_iota + b * blk
-            allowed = (kidx >= start_row) & (kidx <= query_idx)
-            for h in range(nh):
-                pair = (h // 2) * 128
-                s = mm(kn[pl.ds(krow, blk), pair : pair + 128], qpad[h])
-                s = jnp.where(allowed, s, -1e30)
-                old = mrow[h : h + 1, :]
-                new = jnp.maximum(old, jnp.max(s, axis=0, keepdims=True))
-                e = jnp.exp(s - new)
-                alpha = jnp.exp(old - new)
-                lrow[h : h + 1, :] = lrow[h : h + 1, :] * alpha + jnp.sum(e, axis=0, keepdims=True)
-                mrow[h : h + 1, :] = new
-                peaks[step, h : h + 1, :] = new
-                exps[h, step] = e
-                oacc[h] = oacc[h] * alpha + mm(vt[h * HD : (h + 1) * HD, pl.ds(krow, blk)], e.astype(BF))
-            return c
-
-        lax.fori_loop(0, i - low + 1, forward, 0)
-        for h in range(nh):
-            hs = slice(h * HD, (h + 1) * HD)
-            inv = 1.0 / lrow[h : h + 1, :]
-            o = oacc[h] * inv
-            drow[h : h + 1, :] = jnp.sum(o * dot[hs, cols].astype(F32), axis=0, keepdims=True)
-            lrow[h : h + 1, :] = inv
-            ctx_ref[hs, cols] = o.astype(BF)
 
         def backward(step, c):
             kcols = pl.ds(place(i - step), blk)
-            for h in range(nh):
-                pair = (h // 2) * 128
-                hs = slice(h * HD, (h + 1) * HD)
-                factor = jnp.exp(peaks[step, h : h + 1, :] - mrow[h : h + 1, :]) * lrow[h : h + 1, :]
-                p = exps[h, step] * factor
-                dp = mm(vn[kcols, pair : pair + 128], dopad[h])
-                ds = (p * (dp - drow[h : h + 1, :])).astype(BF)
-                dv[hs, kcols] += mm(dot[hs, cols], p.astype(BF), NT)
+            for h in heads:
+                half = (h % 2) * HD
+                hs = rows_of(h)
+                dp = mm(vn[kcols, pair_of(h)], dopad[h])
+                ds = (exps[h, step] * (dp - rowsc[h : h + 1, :])).astype(BF)
+                dv[hs, kcols] += mm(dopad[h, half : half + HD, :], low_exps[h, step], NT)
                 dk[hs, kcols] += mm(qt[hs, cols], ds, NT)
                 dqacc[hs, :] += mm(kt[hs, kcols], ds)
             return c
 
-        lax.fori_loop(0, i - low + 1, backward, 0)
+        lax.fori_loop(0, count, backward, 0)
         co = cos[:, cols]
         si = sin[:, cols]
-        for h in range(nh):
+        for h in heads:
             base = h * HD
             g = dqacc[base : base + HD, :] * (HD**-0.5)
             g1 = g[:HALF]
@@ -550,7 +587,7 @@
         cols = pl.ds(pl.multiple_of(i * blk, blk), blk)
         co = cos[:, cols]
         si = sin[:, cols]
-        for h in range(nh):
+        for h in heads:
             base = h * HD
             g = dk[base : base + HD, cols]
             g1 = g[:HALF]
@@ -577,13 +614,13 @@
         out_specs=(vm, vm),
         scratch_shapes=[
             pltpu.VMEM((nh, wb, blk, blk), F32),
-            pltpu.VMEM((wb, 8, blk), F32),
+            pltpu.VMEM((nh, wb, blk, blk), BF),
             pltpu.VMEM((width, tok), F32),
             pltpu.VMEM((width, tok), F32),
             pltpu.VMEM((nh, HD, blk), F32),
             pltpu.VMEM((width, blk), F32),
-            pltpu.VMEM((8, blk), F32),
-            pltpu.VMEM((8, blk), F32),
+            pltpu.VMEM((nh, 8, blk), F32),
+            pltpu.VMEM((nh, 8, blk), F32),
             pltpu.VMEM((8, blk), F32),
             pltpu.VMEM((nh, 128, blk), BF),
             pltpu.VMEM((nh, 128, blk), BF),
@@ -671,10 +708,10 @@
 
 
 def tail_kernel(gt_h, na_h, gm_h, ctx_h, dya_h, wqkv_h, wo_h, upk_h, upo_h, dn0_h, dn1_h, dn2_h, dn3_h, x_h, pown_h, py_h,
-                vec, small, smallf,
+                gain, shift_ref, bo, bd, small, smallf,
                 out_ref, g_ref, wup_ref, wdn_ref, wq_ref, wout_ref, sums_ref,
                 gt, na, gm, ctx, dya, wqkv, wo, upk, upo, dn, xo, pown, py,
-                ctx_in, up4, up_in, dn_in, up2, dn2, up_in2,
+                ctx_in, up4, up_in, dn_in, dn2,
                 dwq, qa_in, qb_in, qa4, qb4, qa_in2, qb_in2, qa2, qb2, qa_in3, qb_in3, qfin, q_own,
                 dwo, wo_in, wo4, wo_in2, wo2, wo_in3, piece, owner_in,
                 far_in, near_in, far_sum, y_in, sm, sm_in, load, send, recv):
@@ -717,15 +754,15 @@
         remote(ctx_h.at[:, pl.ds(3 * own + half, half)], ctx_in.at[2, :, hi], diag),
         remote(ctx_h.at[:, pl.ds(own, own)], ctx_in.at[0], core),
     ]
-    c_up0 = remote(up4.at[:, 1 - b0], up_in, p0)
+    z = i // 2
+    c_up = [remote(up4.at[z ^ k], up_in.at[k - 1], {"dp": i ^ (2 * k)}) for k in (1, 2, 3)]
     c_dnx = remote(dn2.at[1 - bx], dn_in, px)
-    c_up1 = remote(up2.at[1 - b1], up_in2, p1)
     rows = dwq.shape[3] // 2
     ra, rb = pl.ds(0, rows), pl.ds(rows, rows)
     c_qa = remote(dwq.at[:, :, 1 - bx, ra], qa_in, px)
-    c_qb = remote(dwq.at[:, 1 - b0, :, rb], qb_in, p0)
+    c_qb = remote(dwq.at[:, :, 1 - bx, rb], qb_in, px)
     c_qa0 = remote(qa4.at[:, 1 - b0], qa_in2, p0)
-    c_qbx = remote(qb4.at[:, 1 - bx], qb_in2, px)
+    c_qb0 = remote(qb4.at[:, 1 - b0], qb_in2, p0)
     c_qa1 = remote(qa2.at[1 - b1], qa_in3, p1)
     c_qb1 = remote(qb2.at[1 - b1], qb_in3, p1)
     c_wox = remote(dwo.at[:, :, 1 - bx], wo_in, px)
@@ -752,7 +789,7 @@
         c_q.append(remote(qfin.at[(3 * dst + t) // 4], q_own.at[t], {"head": dst}))
 
     barrier = pltpu.get_barrier_semaphore()
-    for to in (core, across, diag, px, p0, p1):
+    for to in (core, across, diag, px, p0, p1, {"dp": i ^ 6}):
         pl.semaphore_signal(barrier, inc=1, device_id=to, device_id_type=mesh_id)
     for c in loads:
         c.start()
@@ -764,7 +801,7 @@
             pl.semaphore_signal(barrier, inc=1, device_id={"dp": si, "head": sj}, device_id_type=mesh_id)
 
     to_self = jnp.where(2 * j + i // 4 == i, 1, 0)
-    pl.semaphore_wait(barrier, 10 - to_self)
+    pl.semaphore_wait(barrier, 11 - to_self)
 
     for c in c_ctx:
         c.start()
@@ -774,8 +811,9 @@
 
     for k in range(4):
         loads[k].wait()
-    up4[:, 1 - b0] = added(upk[:, 1 - b0], upo[:, 1 - b0]).astype(BF)
-    c_up0.start()
+    up4[...] = added(upk[...], upo[...]).astype(BF)
+    for c in c_up:
+        c.start()
     loads[16].wait()
     loads[17].wait()
     dn2[...] = (added(dn[0], dn[1]) + added(dn[2], dn[3])).astype(BF)
@@ -783,12 +821,13 @@
 
     loads[4].wait()
     loads[5].wait()
-    for k in range(4):
-        t = mm(gt[...], na[:, 256 * k : 256 * (k + 1)]).astype(BF)
-        dwq[k // 2, k % 2, 0] = t[:, :128]
-        dwq[k // 2, k % 2, 1] = t[:, 128:]
-    c_qa.start()
-    c_qb.start()
+    for part, c in ((ra, c_qa), (rb, c_qb)):
+        left = gt[part, :]
+        for k in range(4):
+            t = mm(left, na[:, 256 * k : 256 * (k + 1)]).astype(BF)
+            dwq[k // 2, k % 2, 0, part] = t[:, :128]
+            dwq[k // 2, k % 2, 1, part] = t[:, 128:]
+        c.start()
     loads[6].wait()
     loads[7].wait()
     t = mm(ctx[...], dya[...]).astype(BF)
@@ -798,7 +837,7 @@
 
     for k in range(8, 12):
         loads[k].wait()
-    scale = vec[0:1, :]
+    scale = flat(gain[...])
     ones = jnp.zeros((1, d), F32)
     s_gain, s_shift, s_bias = ones, ones, jnp.zeros((1, 3 * w), F32)
 
@@ -818,22 +857,18 @@
     c_g[0].start()
     sums = tile(3 * own, own, sums)
     c_g[1].start()
-    c_up0.wait_recv()
-    mine = added(upk[:, b0], upo[:, b0]) + up_in[...].astype(F32)
-    up2[...] = mine.astype(BF)
-    c_up1.start()
     c_g[0].wait_recv()
     far_sum[lo] = added(gm[2 * own : 2 * own + half], far_in[lo]).astype(BF)
     c_y[0].start()
+    sums = tile(own, own, sums)
+    c_g[2].start()
     c_g[1].wait_recv()
     far_sum[hi] = added(gm[3 * own : 3 * own + half], far_in[hi]).astype(BF)
     c_y[1].start()
-    sums = tile(own, own, sums)
-    c_g[2].start()
     sums = tile(0, own, sums)
 
     sm[0] = jnp.zeros((16, d), F32)
-    shift = vec[1:2, :]
+    shift = flat(shift_ref[...])
     sm[0, 0:1, :] = (sums[0] - shift * sums[1]) / scale
     sm[0, 1:2, :] = sums[1]
     for k in range(3):
@@ -843,23 +878,12 @@
     sm[0, pl.ds(8 + j, 1), :] = smallf[0:1, :]
     c_sm[0].start()
 
-    c_qa.wait_recv()
-    qa4[...] = added(dwq[:, :, bx, ra], qa_in[...]).astype(BF)
-    c_qa0.start()
-    c_qb.wait_recv()
-    qb4[...] = added(dwq[:, b0, :, rb], qb_in[...]).astype(BF)
-    c_qbx.start()
-    c_wox.wait_recv()
-    wo4[...] = added(dwo[:, :, bx], wo_in[...]).astype(BF)
-    c_wo0.start()
-
     def small_step(s):
         c_sm[s].wait_recv()
         sm[s + 1] = sm[s] + sm_in[s]
         if s < 4:
             c_sm[s + 1].start()
 
-    small_step(0)
     for k in range(12, 16):
         loads[k].wait()
     attn = mm(ctx[:, :own], wo[pl.ds(pl.multiple_of(j * w, 128), w), :], TN)
@@ -870,25 +894,37 @@
     attn += mm(ctx_in[1], wo[pl.ds(pl.multiple_of((j ^ 2) * w, 128), w), :], TN)
     attn += mm(ctx_in[2], wo[pl.ds(pl.multiple_of((j ^ 3) * w, 128), w), :], TN)
     out_ref[...] = (
-        xo[...].astype(F32) + attn + added(pown[...], py[...]) + (vec[11:12, :] + vec[12:13, :])
+        xo[...].astype(F32) + attn + added(pown[...], py[...]) + (flat(bo[...]) + flat(bd[...]))
     ).astype(BF)
+    small_step(0)
+
+    c_qa.wait_recv()
+    qa4[...] = added(dwq[:, :, bx, ra], qa_in[...]).astype(BF)
+    c_qa0.start()
     small_step(1)
-
     c_qa0.wait_recv()
     qa2[...] = added(qa4[:, b0], qa_in2[...]).astype(BF)
     c_qa1.start()
-    c_qbx.wait_recv()
-    qb2[...] = added(qb4[:, bx], qb_in2[...]).astype(BF)
+    c_qb.wait_recv()
+    qb4[...] = added(dwq[:, :, bx, rb], qb_in[...]).astype(BF)
+    c_qb0.start()
+    small_step(2)
+    for c in c_up:
+        c.wait_recv()
+    wup_ref[...] = (up4[z].astype(F32) + up_in[0].astype(F32) + added(up_in[1], up_in[2])).astype(BF)
+    c_dnx.wait_recv()
+    nd = dn2.shape[1]
+    piece[:nd, :] = added(dn2[bx], dn_in[...]).astype(BF)
+    c_wox.wait_recv()
+    wo4[...] = added(dwo[:, :, bx], wo_in[...]).astype(BF)
+    c_wo0.start()
+    c_qb0.wait_recv()
+    qb2[...] = added(qb4[:, b0], qb_in2[...]).astype(BF)
     c_qb1.start()
+    small_step(3)
     c_wo0.wait_recv()
     wo2[...] = added(wo4[:, b0], wo_in2[...]).astype(BF)
     c_wo1.start()
-    small_step(2)
-    c_up1.wait_recv()
-    wup_ref[...] = added(up2[b1], up_in2[...]).astype(BF)
-    c_dnx.wait_recv()
-    piece[: dn2.shape[1], :] = added(dn2[bx], dn_in[...]).astype(BF)
-    small_step(3)
     c_qa1.wait_recv()
     c_qb1.wait_recv()
     done = jnp.concatenate([added(qa2[b1], qa_in3[...]), added(qb2[b1], qb_in3[...])], axis=0).astype(BF)
@@ -905,7 +941,7 @@
             q_own[t] = qfin[(3 * j + t) // 4]
 
     c_wo1.wait_recv()
-    piece[dn2.shape[1] :, :] = added(wo2[b1], wo_in3[...]).astype(BF)
+    piece[nd:, :] = added(wo2[b1], wo_in3[...]).astype(BF)
     for r in range(4):
         di, dj = dests[r]
 
@@ -940,13 +976,12 @@
         def _():
             c_own[r].wait_recv()
 
-    nd = dn2.shape[1]
     no = wo2.shape[1]
     for a in range(4):
         wdn_ref[a * nd : (a + 1) * nd, :] = owner_in[a, :nd]
         wout_ref[a * no : (a + 1) * no, :] = owner_in[a, nd:]
 
-    for c in c_ctx + [c_up0, c_dnx, c_up1, c_qa, c_qb, c_qa0, c_qbx, c_qa1, c_qb1, c_wox, c_wo0, c_wo1] + c_g + c_y + c_sm:
+    for c in c_ctx + c_up + [c_dnx, c_qa, c_qb, c_qa0, c_qb0, c_qa1, c_qb1, c_wox, c_wo0, c_wo1] + c_g + c_y + c_sm:
         c.wait_send()
     for t in range(3):
 
@@ -962,7 +997,7 @@
             c_own[r].wait_send()
 
 
-def tail_stage(gt, na, gm, ctx, dya, w_qkv, w_out, upk, upo, dn, x, pown, py, vec, small, smallf, cid):
+def tail_stage(gt, na, gm, ctx, dya, w_qkv, w_out, upk, upo, dn, x, pown, py, ga, sa, bo, bd, small, smallf, cid):
     own, d = x.shape
     tok = na.shape[0]
     w = d // 4
@@ -975,7 +1010,7 @@
     r2 = 3 * w // 2
     return pl.pallas_call(
         tail_kernel,
-        in_specs=[hbm] * 16 + [vm] * 3,
+        in_specs=[hbm] * 16 + [vm] * 6,
         out_specs=[vm] * 7,
         out_shape=(
             sds((own, d), BF), sds((own, d), F32), sds((nb, d), BF), sds((4 * nb, w), BF),
@@ -983,10 +1018,9 @@
         ),
         scratch_shapes=[
             big(3 * w, tok), big(tok, d), big(tok, d), big(w, tok), big(tok, d), big(d, 3 * w), big(d, d),
-            big(2, 2, nb, d), big(2, 2, nb, d), big(4, 2, nb, d),
+            big(4, nb, d), big(4, nb, d), big(4, 2, nb, d),
             big(own, d), big(own, d), big(own, d),
-            big(3, w, own), big(2, 2, nb, d), big(2, nb, d), big(nb, d),
-            big(2, nb, d), big(2, nb, d), big(nb, d),
+            big(3, w, own), big(4, nb, d), big(3, nb, d), big(nb, d), big(2, nb, d),
             big(2, 2, 2, 3 * w, 128), big(2, 2, r2, 128), big(2, 2, r2, 128), big(2, 2, r2, 128), big(2, 2, r2, 128),
             big(2, r2, 128), big(2, r2, 128), big(2, r2, 128), big(2, r2, 128), big(r2, 128), big(r2, 128),
             big(3, w, 128), big(3, w, 128),
@@ -1001,7 +1035,7 @@
             flops=14 * tok * d * w, bytes_accessed=10 * tok * d, transcendentals=0
         ),
         name="tail_stage",
-    )(gt, na, gm, ctx, dya, w_qkv, w_out, upk, upo, *dn, x, pown, py, vec, small, smallf)
+    )(gt, na, gm, ctx, dya, w_qkv, w_out, upk, upo, *dn, x, pown, py, ga, sa, bo, bd, small, smallf)
 
 
 def final_kernel(out_t, g_ref, x_ref, dy_ref, wup, wdn, wq, wout, sums,
@@ -1071,18 +1105,17 @@
     w = d // n
     pos = lax.axis_index("head").astype(jnp.int32).reshape(1)
     lens = lengths[0]
-    vec = jnp.concatenate(
-        [attn_gain, attn_shift, mlp_gain, mlp_shift, b_up, b_qkv, b_out, b_down, jnp.zeros((3 * d,), BF)]
-    ).astype(F32).reshape(16, d)
     (g_mlp, na, dy_all, qt, kt, vt, dot, kn, vn, cos, sin, p_own, p_far, up_keep, up_send, *dn, small,
-     smallf) = head_stage(inputs, cotangent, w_up, w_down, w_qkv, w_out, vec, lens, n, 0)
+     smallf) = head_stage(
+        inputs, cotangent, w_up, w_down, w_qkv, w_out, attn_gain, attn_shift, mlp_gain, mlp_shift, b_up, b_qkv, lens, n, 0
+    )
     up_other = dp_perm(up_send, 1)
     dn = [dn[0]] + [dp_perm(dn[k], 2 * k) for k in (1, 2, 3)]
     p_y = head_perm(p_far, 2)
     gt, ctx = attention(lens, pos, cos, sin, qt, kt, vt, dot, kn, vn, own, tok // 2, halved=True)
-    quad = lambda v: v.reshape(2, 2, v.shape[1], v.shape[2])
     out_t, g, wup, wdn, wq, wout, sums = tail_stage(
-        gt, na, g_mlp, ctx, dy_all, w_qkv, w_out, quad(up_keep), quad(up_other), dn, inputs, p_own, p_y, vec, small, smallf, 1
+        gt, na, g_mlp, ctx, dy_all, w_qkv, w_out, up_keep, up_other, dn, inputs, p_own, p_y,
+        attn_gain, attn_shift, b_out, b_down, small, smallf, 1
     )
     return tuple(final_stage(out_t, g, inputs, cotangent, wup, wdn, wq, wout, sums))
 

time: 216 us -> 208 us (0.963)
  local copies, waits for them, and re-layouts: 7.26 us -> 1.09 us
    pallas_call x1, Pallas kernels: 50.1 us -> 35.8 us  [attention(): pl.pallas_call(functools.partial(attn_kernel, nh, tok, blk, chunk // blk,...]
    pallas_call x1, Pallas kernels: 81.9 us -> 94.3 us  [tail_stage(): pl.pallas_call(tail_kernel, in_specs=[hbm] * 16 + [vm] * 6, out_specs=[vm...]
    unnamed x12 -> x4, local copies, waits for them, and re-layouts: 6.61 us -> 1.09 us
  transfers between devices with their start and end apart: 5 -> 5, of which waited for: 0 -> 0; matrix products, arithmetic and copies ran while one was open for 0% -> 0% of each run, Pallas kernels for 23% -> 17%
where the time goes in v5:
time: 208 us
  Pallas kernels  201 us (97%)
  starting transfers between devices  4.6 us (2%)
    pallas_call x1, Pallas kernels, tail_stage(): pl.pallas_call(tail_kernel, in_specs=[hbm] * 16 + [vm] * 6, out_specs=[vm...  94.3 us
    pallas_call x1, Pallas kernels, head_stage(): pl.pallas_call(functools.partial(head_kernel, w // HD), grid=(n,), in_spe...  64.9 us
    pallas_call x1, Pallas kernels, attention(): pl.pallas_call(functools.partial(attn_kernel, nh, tok, blk, chunk // blk,...  35.8 us
    pallas_call x1, Pallas kernels, final_stage(): pl.pallas_call(final_kernel, grid=(steps,), in_specs=[row, row, row, row]...  6.43 us
  transfers between devices with their start and end apart: 5, of which 0 were waited for; matrix products, arithmetic and copies ran while one was open for 0% of the time, Pallas kernels for 17%

profile of v5, /device:TPU:7, one launch (start us, length us, event | category | flops | bytes accessed | tf_op | source)
XLA Modules:
  0.0 208.0 jit_solution(6718550988690144331)
XLA Ops:
  0.6 64.9 %head_stage.1 = (bf16[2048,1024]{1,0:T(8,128)(2,1)}, bf16[2048,1024]{1,0:T(8,128)(2,1)}, bf16[2048,1024]{1,0:T(8,128)(2,1)}, bf16[256,2048]{1,0:T(8,128)(2,1)}, ...) custom-call(bf16[512,1024]{1,0:T(8,128)(2,1)} %x_ref.1, ...), custom_call_target="tpu_custom_call" | custom-call | flops 31138512896 | bytes 33554432 | tf_op jit(solution)/shard_map/head_stage/pallas_call | solution.py:399
  65.6 0.3 collective-permute-start
  65.9 0.7 collective-permute-start.4
  66.6 1.3 collective-permute-start.1
  67.9 2.3 %collective-permute-start.2 = (bf16[2,128,1024]{2,1,0:T(8,128)(2,1)}, bf16[2,128,1024]{2,1,0:T(8,128)(2,1)}, u32[]{:S(2)}, u32[]{:S(2)}) collective-permute-start(bf16[2,128,1024]{2,1,0:T(8,128)(2,1)} %get-tuple-element.61), channel_id=1, source_target_pairs={{0,16},{4,20},{8,24},{12,28},{16,0},{20,4},{24,8},{28,12},{1,17},{... | collective-permute-start | bytes 1572872 | tf_op jit(solution)/shard_map/ppermute | solution.py:1097
  70.2 0.0 collective-permute-start.3
  70.2 35.8 %attention.1 = (bf16[768,2048]{1,0:T(8,128)(2,1)}, bf16[256,2048]{1,0:T(8,128)(2,1)}) custom-call(s32[4]{0:T(128)} %bitcast.3, s32[1]{0:T(128)} %bitcast.1.rel, f32[8,2048]{1,0:T(8,128)} %get-tuple-element.44.cos, f32[8,2048]{1,0:T(8,128)} %get-tuple-element.45.sin, bf16[256,2048]{1,0:T(8,128)(2,1)} %get-tuple-element.46.qt, ...), custom_call_target="tpu_custom_call" | custom-call | flops 10737418240 | bytes 10485760 | tf_op jit(solution)/shard_map/attention/pallas_call | solution.py:610
  106.0 0.0 collective-permute-done.1.dn1_h
  106.0 0.0 copy-start.1
  106.0 0.0 collective-permute-done.2.dn2_h
  106.0 0.0 collective-permute-done.3.dn3_h
  106.0 0.0 collective-permute-done.upo_h
  106.0 0.0 copy-start
  106.0 0.0 collective-permute-done.4.py_h
  106.0 0.7 copy-done.1
  106.8 0.3 copy-done
  107.1 94.3 %tail_stage.1 = (bf16[512,1024]{1,0:T(8,128)(2,1)}, f32[512,1024]{1,0:T(8,128)}, bf16[128,1024]{1,0:T(8,128)(2,1)}, bf16[512,256]{1,0:T(8,128)(2,1)}, bf16[128,7...) custom-call(bf16[768,2048]{1,0:T(8,128)(2,1)} %get-tuple-element.52.gt_h, ...), custom_call_target="tpu_custom_call" | custom-call | flops 7516192768 | bytes 20971520 | tf_op jit(solution)/shard_map/tail_stage/pallas_call | solution.py:1011
  201.4 6.4 %final_stage.1 = (bf16[512,1024]{1,0:T(8,128)(2,1)}, f32[512,1024]{1,0:T(8,128)}, f32[1024]{0:T(1024)}, f32[1024]{0:T(1024)}, f32[1024]{0:T(1024)}, /*index=5*/f...) custom-call(bf16[512,1024]{1,0:T(8,128)(2,1)} %get-tuple-element.67., ...), custom_call_target="tpu_custom_call" | custom-call | tf_op jit(solution)/shard_map/final_stage/pallas_call | solution.py:1072
Async XLA Ops:
  65.6 40.4 %collective-permute-start = (bf16[4,128,1024]{2,1,0:T(8,128)(2,1)}, bf16[4,128,1024]{2,1,0:T(8,128)(2,1)S(1)}, u32[]{:S(2)}, u32[]{:S(2)}) collective-permute-start(bf16[4,128,1024]{2,1,0:T(8,128)(2,1)} %get-tuple-element.58), channel_id=1, source_target_pairs={{0,4},{4,0},{8,12},{12,8},{16,20},{20,16},{24,28},{28,24},{1,5},{5... | collective-permute-start | bytes 3145736 | tf_op jit(solution)/shard_map/ppermute | solution.py:1097
  65.9 40.1 %collective-permute-start.4 = (bf16[512,1024]{1,0:T(8,128)(2,1)}, bf16[512,1024]{1,0:T(8,128)(2,1)}, u32[]{:S(2)}, u32[]{:S(2)}) collective-permute-start(bf16[512,1024]{1,0:T(8,128)(2,1)} %get-tuple-element.64), channel_id=1, source_target_pairs={{0,2},{1,3},{2,0},{3,1},{4,6},{5,7},{6,4},{7,5},{8,10},{9,11},{10,... | collective-permute-start | bytes 3145736 | tf_op jit(solution)/shard_map/ppermute | solution.py:1093
  66.6 39.4 %collective-permute-start.1 = (bf16[2,128,1024]{2,1,0:T(8,128)(2,1)}, bf16[2,128,1024]{2,1,0:T(8,128)(2,1)S(1)}, u32[]{:S(2)}, u32[]{:S(2)}) collective-permute-start(bf16[2,128,1024]{2,1,0:T(8,128)(2,1)} %get-tuple-element.60), channel_id=1, source_target_pairs={{0,8},{4,12},{8,0},{12,4},{16,24},{20,28},{24,16},{28,20},{1,9},{5... | collective-permute-start | bytes 1572872 | tf_op jit(solution)/shard_map/ppermute | solution.py:1097
  67.9 38.1 %collective-permute-start.2 = (bf16[2,128,1024]{2,1,0:T(8,128)(2,1)}, bf16[2,128,1024]{2,1,0:T(8,128)(2,1)}, u32[]{:S(2)}, u32[]{:S(2)}) collective-permute-start(bf16[2,128,1024]{2,1,0:T(8,128)(2,1)} %get-tuple-element.61), channel_id=1, source_target_pairs={{0,16},{4,20},{8,24},{12,28},{16,0},{20,4},{24,8},{28,12},{1,17},{... | collective-permute-start | bytes 1572872 | tf_op jit(solution)/shard_map/ppermute | solution.py:1097
  70.2 35.8 %collective-permute-start.3 = (bf16[2,128,1024]{2,1,0:T(8,128)(2,1)}, bf16[2,128,1024]{2,1,0:T(8,128)(2,1)}, u32[]{:S(2)}, u32[]{:S(2)}) collective-permute-start(bf16[2,128,1024]{2,1,0:T(8,128)(2,1)} %get-tuple-element.62), channel_id=1, source_target_pairs={{0,24},{4,28},{8,16},{12,20},{16,8},{20,12},{24,0},{28,4},{1,25},{... | collective-permute-start | bytes 1572872 | tf_op jit(solution)/shard_map/ppermute | solution.py:1097
  106.0 0.8 copy-start.1
  106.0 1.1 copy-start

commit v6 on v5

--- a/solution.py
+++ b/solution.py
@@ -202,7 +202,7 @@
 
 def head_kernel(nh, x_hbm, dy_hbm, wu_hbm, wd_hbm, wqkv_hbm, wo_hbm, gain_a, shift_a, gain_m, shift_m, bu, bq, lens,
                 g_out, na_out, dy_out, qt, kt, vt, dot, kn, vn, cos, sin, p_own, p_far, up_keep, up_send, dn0, dn1, dn2, dn3,
-                small, smallf,
+                w_t, small, smallf,
                 xs, dys, wu, wd, wqkv, wt, wo, bias_t, parts, far_in, near_in, dwu, dwd, load, send, recv):
     step = pl.program_id(0)
     i = lax.axis_index("dp")
@@ -270,65 +270,25 @@
     @pl.when(step == 1)
     def _():
         copies[0].wait_recv()
-        copies[1].wait_recv()
 
     @pl.when(step == 2)
     def _():
         copies[6].wait_recv()
-        copies[7].wait_recv()
 
     @pl.when(step == 3)
     def _():
         copies[8].wait_recv()
-        copies[9].wait_recv()
 
     normed, _unused = norm_parts(xs[step])
     scale = flat(gain_m[...])
     nm = (normed * scale + flat(shift_m[...])).astype(BF)
     na = (normed * flat(gain_a[...]) + flat(shift_a[...])).astype(BF)
-    dy = dys[step]
     na_out[...] = na
-    dy_out[...] = dy
     pre = mm(nm, wu[...]) + flat(bu[pl.ds(pl.multiple_of(j * f, 1024), f)])
     cdf = 0.5 + 0.5 * lax.erf(pre * (0.5**0.5))
     hid = (pre * cdf).astype(BF)
     slope = cdf + pre * (jnp.exp(-0.5 * pre * pre) * 0.3989422804014327)
-    gp = (mm(dy, wd[...], NT) * slope).astype(BF)
     parts[step] = mm(hid, wd[...]).astype(BF)
-    r = mm(gp, wu[...], NT)
-    g_out[...] = (r * scale).astype(BF)
-    smallf[0:1, :] += jnp.sum(gp.astype(F32), axis=0, keepdims=True)
-    small[0:1, :] += jnp.sum(r * normed, axis=0, keepdims=True)
-    small[1:2, :] += jnp.sum(r, axis=0, keepdims=True)
-    small[2:3, :] += jnp.sum(dy.astype(F32), axis=0, keepdims=True)
-    dwd[...] += mm(hid, dy, TN)
-    dwu[...] += mm(nm, gp, TN)
-
-    @pl.when(step == 1)
-    def _():
-        for k in (2, 3):
-            copies[k].wait_recv()
-            copies[k + 4].start()
-        copies[10].start()
-
-    @pl.when(step == 2)
-    def _():
-        for k in (4, 5):
-            copies[k].wait_recv()
-            copies[k + 4].start()
-        copies[11].start()
-
-    @pl.when(step == 3)
-    def _():
-        copies[12].start()
-        rows = up_keep.shape[1]
-        for b in range(4):
-            for ref, at in ((up_keep, 2 * b + i % 2), (up_send, 2 * b + 1 - i % 2)):
-                ref[b] = dwu[pl.ds(pl.multiple_of(at * rows, rows), rows), :].astype(BF)
-            ref = (dn0, dn1, dn2, dn3)[b]
-            for x in range(2):
-                at = 2 * ((i // 2) ^ b) + x
-                ref[x] = dwd[pl.ds(pl.multiple_of(at * rows, rows), rows), :].astype(BF)
 
     lane = lax.broadcasted_iota(jnp.int32, (1, own), 1)
     far = jnp.where(lane < half, j ^ 2, j ^ 3) * own + (step - 2) * half + lane % half
@@ -370,10 +330,63 @@
     values = projected(2)
     vt[...] = values
     vn[...] = values.T
+
+    @pl.when(step == 1)
+    def _():
+        copies[1].wait_recv()
+        copies[10].start()
+        copies[2].wait_recv()
+        copies[6].start()
+
+    @pl.when(step == 2)
+    def _():
+        copies[7].wait_recv()
+        copies[11].start()
+
+    @pl.when(step == 3)
+    def _():
+        copies[12].start()
+        copies[5].wait_recv()
+        copies[9].start()
+        copies[9].wait_recv()
+
+    dy = dys[step]
+    dy_out[...] = dy
+    gp = (mm(dy, wd[...], NT) * slope).astype(BF)
+    r = mm(gp, wu[...], NT)
+    g_out[...] = (r * scale).astype(BF)
+    smallf[0:1, :] += jnp.sum(gp.astype(F32), axis=0, keepdims=True)
+    small[0:1, :] += jnp.sum(r * normed, axis=0, keepdims=True)
+    small[1:2, :] += jnp.sum(r, axis=0, keepdims=True)
+    small[2:3, :] += jnp.sum(dy.astype(F32), axis=0, keepdims=True)
+    dwd[...] += mm(hid, dy, TN)
+    dwu[...] += mm(nm, gp, TN)
     dot[...] = mm(wo[...], dy, NT).astype(BF)
 
+    @pl.when(step == 1)
+    def _():
+        copies[3].wait_recv()
+        copies[7].start()
+
+    @pl.when(step == 2)
+    def _():
+        copies[4].wait_recv()
+        copies[8].start()
+
     @pl.when(step == 3)
     def _():
+        rows = dwu.shape[0] // 8
+        keep = dn0.shape[1]
+        for b in range(4):
+            for ref, at in ((up_keep, 2 * b + i % 2), (up_send, 2 * b + 1 - i % 2)):
+                at = pl.multiple_of(at * rows, rows)
+                ref[b, :rows] = dwu[pl.ds(at, rows), :].astype(BF)
+                ref[b, rows:] = dwd[pl.ds(at + keep, rows - keep), :].astype(BF)
+            ref = (dn0, dn1, dn2, dn3)[b]
+            for x in range(2):
+                at = 2 * ((i // 2) ^ b) + x
+                ref[x] = dwd[pl.ds(pl.multiple_of(at * rows, rows), keep), :].astype(BF)
+        w_t[...] = wt[...]
         copies[10].wait_recv()
         p_own[...] = (parts[0].astype(F32) + near_in[...].astype(F32)).astype(BF)
         copies[11].wait_recv()
@@ -407,18 +420,18 @@
         + [nat(w)] * 2
         + [lane(HALF)] * 2
         + [const((own, d))] * 2
-        + [const((4, d // 8, f))] * 2
-        + [const((2, f // 8, d))] * 4
-        + [const((8, d)), const((8, f))],
+        + [const((4, d // 8 + d // 32, d))] * 2
+        + [const((2, 3 * d // 32, d))] * 4
+        + [const((3 * w, d)), const((8, d)), const((8, f))],
         out_shape=tuple(
             [sds((tok, d), BF)] * 3
             + [sds((w, tok), BF)] * 4
             + [sds((tok, w), BF)] * 2
             + [sds((HALF, tok), F32)] * 2
             + [sds((own, d), BF)] * 2
-            + [sds((4, d // 8, f), BF)] * 2
-            + [sds((2, f // 8, d), BF)] * 4
-            + [sds((8, d), F32), sds((8, f), F32)]
+            + [sds((4, d // 8 + d // 32, d), BF)] * 2
+            + [sds((2, 3 * d // 32, d), BF)] * 4
+            + [sds((3 * w, d), BF), sds((8, d), F32), sds((8, f), F32)]
         ),
         scratch_shapes=[
             pltpu.VMEM((4, own, d), BF),
@@ -707,27 +720,29 @@
     )(pos, gt, na, gm, w_qkv, w_qkv, w_qkv, gain, shift)
 
 
-def tail_kernel(gt_h, na_h, gm_h, ctx_h, dya_h, wqkv_h, wo_h, upk_h, upo_h, dn0_h, dn1_h, dn2_h, dn3_h, x_h, pown_h, py_h,
+def tail_kernel(gt_h, na_h, gm_h, ctx_h, dya_h, wt_h, wo_h, upk_h, upo_h, dn0_h, dn1_h, dn2_h, dn3_h, x_h, pown_h, py_h,
                 gain, shift_ref, bo, bd, small, smallf,
                 out_ref, g_ref, wup_ref, wdn_ref, wq_ref, wout_ref, sums_ref,
-                gt, na, gm, ctx, dya, wqkv, wo, upk, upo, dn, xo, pown, py,
+                gt, na, gm, ctx, dya, wt, wo, upk, upo, dn, xo, pown, py,
                 ctx_in, up4, up_in, dn_in, dn2,
                 dwq, qa_in, qb_in, qa4, qb4, qa_in2, qb_in2, qa2, qb2, qa_in3, qb_in3, qfin, q_own,
-                dwo, wo_in, wo4, wo_in2, wo2, wo_in3, piece, owner_in,
+                dwo, wo_in, wo4, wo_in2, wo2, wo_in3, piece, piece2, owner_in, owner_in2,
                 far_in, near_in, far_sum, y_in, sm, sm_in, load, send, recv):
     i = lax.axis_index("dp")
     j = lax.axis_index("head")
     own, d = x_h.shape
-    w = wqkv.shape[1] // 3
+    w = wt.shape[0] // 3
     half = own // 2
     bx = i % 2
     b0 = (i // 2) % 2
     b1 = i // 4
+    z = i // 2
     mesh_id = pl.DeviceIdType.MESH
     core, across, diag = {"head": j ^ 1}, {"head": j ^ 2}, {"head": j ^ 3}
     px, p0, p1 = {"dp": i ^ 1}, {"dp": i ^ 2}, {"dp": i ^ 4}
     lo, hi = pl.ds(0, half), pl.ds(half, half)
     count = [0]
+    started = []
 
     def remote(src, dst, to):
         k = count[0]
@@ -735,17 +750,19 @@
         return pltpu.make_async_remote_copy(
             src_ref=src, dst_ref=dst, send_sem=send.at[k], recv_sem=recv.at[k], device_id=to, device_id_type=mesh_id)
 
+    def go(*copies):
+        for c in copies:
+            c.start()
+            started.append(c)
+
     def local(src, dst, k):
         return pltpu.make_async_copy(src, dst, load.at[k])
 
     loads = [
-        local(upk_h, upk, 0), local(upo_h, upo, 1), local(dn0_h, dn.at[0], 2), local(dn1_h, dn.at[1], 3),
-        local(gt_h, gt, 4), local(na_h, na, 5), local(ctx_h, ctx, 6), local(dya_h, dya, 7), local(gm_h, gm, 8),
-        local(wqkv_h.at[:, pl.ds(j * w, w)], wqkv.at[:, pl.ds(0, w)], 9),
-        local(wqkv_h.at[:, pl.ds(d + j * w, w)], wqkv.at[:, pl.ds(w, w)], 10),
-        local(wqkv_h.at[:, pl.ds(2 * d + j * w, w)], wqkv.at[:, pl.ds(2 * w, w)], 11),
-        local(wo_h, wo, 12), local(x_h, xo, 13), local(pown_h, pown, 14), local(py_h, py, 15),
-        local(dn2_h, dn.at[2], 16), local(dn3_h, dn.at[3], 17),
+        local(upk_h, upk, 0), local(upo_h, upo, 1),
+        local(dn0_h, dn.at[0], 2), local(dn1_h, dn.at[1], 3), local(dn2_h, dn.at[2], 4), local(dn3_h, dn.at[3], 5),
+        local(gt_h, gt, 6), local(na_h, na, 7), local(wt_h, wt, 8), local(ctx_h, ctx, 9), local(dya_h, dya, 10),
+        local(gm_h, gm, 11), local(wo_h, wo, 12), local(x_h, xo, 13), local(pown_h, pown, 14), local(py_h, py, 15),
     ]
     c_ctx = [
         remote(ctx_h.at[:, pl.ds(2 * own, half)], ctx_in.at[1, :, lo], across),
@@ -754,7 +771,6 @@
         remote(ctx_h.at[:, pl.ds(3 * own + half, half)], ctx_in.at[2, :, hi], diag),
         remote(ctx_h.at[:, pl.ds(own, own)], ctx_in.at[0], core),
     ]
-    z = i // 2
     c_up = [remote(up4.at[z ^ k], up_in.at[k - 1], {"dp": i ^ (2 * k)}) for k in (1, 2, 3)]
     c_dnx = remote(dn2.at[1 - bx], dn_in, px)
     rows = dwq.shape[3] // 2
@@ -776,11 +792,13 @@
     c_y = [remote(far_sum.at[lo], y_in.at[lo], across), remote(far_sum.at[hi], y_in.at[hi], across)]
     c_sm = [remote(sm.at[s], sm_in.at[s], to) for s, to in enumerate((core, across, px, p0, p1))]
     dests = []
-    c_own = []
+    c_own, c_own2 = [], []
     for r in range(4):
         di, dj = 2 * j + i // 4, (i % 4) ^ r
         dests.append((di, dj))
-        c_own.append(remote(piece.at[:, pl.ds(pl.multiple_of(dj * w, 128), w)], owner_in.at[i % 4], {"dp": di, "head": dj}))
+        cut = pl.ds(pl.multiple_of(dj * w, 128), w)
+        c_own.append(remote(piece.at[:, cut], owner_in.at[i % 4], {"dp": di, "head": dj}))
+        c_own2.append(remote(piece2.at[:, cut], owner_in2.at[i % 4], {"dp": di, "head": dj}))
     c_q = []
     q_dst = []
     for t in range(3):
@@ -803,89 +821,92 @@
     to_self = jnp.where(2 * j + i // 4 == i, 1, 0)
     pl.semaphore_wait(barrier, 11 - to_self)
 
-    for c in c_ctx:
-        c.start()
+    go(*c_ctx)
 
     def added(a, b):
         return a.astype(F32) + b.astype(F32)
 
-    for k in range(4):
-        loads[k].wait()
+    def ready(first, last):
+        for k in range(first, last):
+            loads[k].wait()
+
+    ready(0, 2)
     up4[...] = added(upk[...], upo[...]).astype(BF)
-    for c in c_up:
-        c.start()
-    loads[16].wait()
-    loads[17].wait()
+    go(*c_up)
+    ready(2, 6)
     dn2[...] = (added(dn[0], dn[1]) + added(dn[2], dn[3])).astype(BF)
-    c_dnx.start()
-
-    loads[4].wait()
-    loads[5].wait()
+    go(c_dnx)
+
+    ready(6, 9)
+    gains = [jnp.zeros((1, 256), F32)] * 4
     for part, c in ((ra, c_qa), (rb, c_qb)):
         left = gt[part, :]
         for k in range(4):
-            t = mm(left, na[:, 256 * k : 256 * (k + 1)]).astype(BF)
+            t = mm(left, na[:, 256 * k : 256 * (k + 1)])
+            gains[k] += jnp.sum(t * wt[part, 256 * k : 256 * (k + 1)].astype(F32), axis=0, keepdims=True)
+            t = t.astype(BF)
             dwq[k // 2, k % 2, 0, part] = t[:, :128]
             dwq[k // 2, k % 2, 1, part] = t[:, 128:]
-        c.start()
-    loads[6].wait()
-    loads[7].wait()
-    t = mm(ctx[...], dya[...]).astype(BF)
-    for b in range(8):
-        dwo[b // 4, (b // 2) % 2, b % 2] = t[32 * b : 32 * (b + 1)]
-    c_wox.start()
-
-    for k in range(8, 12):
-        loads[k].wait()
+        if c is c_qa:
+            go(c)
+    s_bias = mm(jnp.ones((8, gt.shape[1]), BF), gt[...], NT)[0:1]
+    high = s_bias.astype(BF)
+    low = (s_bias - high.astype(F32)).astype(BF)
+    s_shift = mm(jnp.broadcast_to(high, (8, 3 * w)), wt[...])[0:1] + mm(jnp.broadcast_to(low, (8, 3 * w)), wt[...])[0:1]
+    s_gain = jnp.concatenate(gains, axis=1)
     scale = flat(gain[...])
-    ones = jnp.zeros((1, d), F32)
-    s_gain, s_shift, s_bias = ones, ones, jnp.zeros((1, 3 * w), F32)
-
-    def tile(at, size, sums):
-        ts = slice(at, at + size)
-        gn = gt[:, ts].T
-        r = mm(gn, wqkv[...], NT)
-        gm[ts, :] = (r * scale + gm[ts, :].astype(F32)).astype(BF)
-        return (
-            sums[0] + jnp.sum(r * na[ts, :].astype(F32), axis=0, keepdims=True),
-            sums[1] + jnp.sum(r, axis=0, keepdims=True),
-            sums[2] + jnp.sum(gn.astype(F32), axis=0, keepdims=True),
-        )
-
-    sums = (s_gain, s_shift, s_bias)
-    sums = tile(2 * own, own, sums)
-    c_g[0].start()
-    sums = tile(3 * own, own, sums)
-    c_g[1].start()
-    c_g[0].wait_recv()
-    far_sum[lo] = added(gm[2 * own : 2 * own + half], far_in[lo]).astype(BF)
-    c_y[0].start()
-    sums = tile(own, own, sums)
-    c_g[2].start()
-    c_g[1].wait_recv()
-    far_sum[hi] = added(gm[3 * own : 3 * own + half], far_in[hi]).astype(BF)
-    c_y[1].start()
-    sums = tile(0, own, sums)
 
     sm[0] = jnp.zeros((16, d), F32)
-    shift = flat(shift_ref[...])
-    sm[0, 0:1, :] = (sums[0] - shift * sums[1]) / scale
-    sm[0, 1:2, :] = sums[1]
+    sm[0, 0:1, :] = (s_gain - flat(shift_ref[...]) * s_shift) / scale
+    sm[0, 1:2, :] = s_shift
     for k in range(3):
-        sm[0, 2 + k : 3 + k, pl.ds(pl.multiple_of(j * w, 128), w)] = sums[2][:, k * w : (k + 1) * w]
+        sm[0, 2 + k : 3 + k, pl.ds(pl.multiple_of(j * w, 128), w)] = s_bias[:, k * w : (k + 1) * w]
     sm[0, 5:7, :] = small[0:2, :]
     sm[0, 7:8, :] = small[2:3, :] * 0.25
     sm[0, pl.ds(8 + j, 1), :] = smallf[0:1, :]
-    c_sm[0].start()
+    go(c_sm[0])
 
     def small_step(s):
         c_sm[s].wait_recv()
         sm[s + 1] = sm[s] + sm_in[s]
         if s < 4:
-            c_sm[s + 1].start()
-
-    for k in range(12, 16):
-        loads[k].wait()
+            go(c_sm[s + 1])
+
+    ready(9, 11)
+    t = mm(ctx[...], dya[...]).astype(BF)
+    for b in range(8):
+        dwo[b // 4, (b // 2) % 2, b % 2] = t[32 * b : 32 * (b + 1)]
+    small_step(0)
+
+    ready(11, 12)
+
+    def tile(at):
+        ts = slice(at, at + own)
+        r = mm(gt[:, ts].T, wt[...])
+        gm[ts, :] = (r * scale + gm[ts, :].astype(F32)).astype(BF)
+
+    tile(2 * own)
+    go(c_g[0])
+    tile(3 * own)
+    go(c_g[1])
+    c_g[0].wait_recv()
+    far_sum[lo] = added(gm[2 * own : 2 * own + half], far_in[lo]).astype(BF)
+    go(c_y[0])
+    small_step(1)
+    go(c_qb, c_wox)
+    c_g[1].wait_recv()
+    far_sum[hi] = added(gm[3 * own : 3 * own + half], far_in[hi]).astype(BF)
+    go(c_y[1])
+    tile(own)
+    go(c_g[2])
+    small_step(2)
+    c_qa.wait_recv()
+    qa4[...] = added(dwq[:, :, bx, ra], qa_in[...]).astype(BF)
+    go(c_qa0)
+    tile(0)
+    small_step(3)
+
+    ready(12, 16)
     attn = mm(ctx[:, :own], wo[pl.ds(pl.multiple_of(j * w, 128), w), :], TN)
     c_ctx[4].wait_recv()
     attn += mm(ctx_in[0], wo[pl.ds(pl.multiple_of((j ^ 1) * w, 128), w), :], TN)
@@ -896,35 +917,47 @@
     out_ref[...] = (
         xo[...].astype(F32) + attn + added(pown[...], py[...]) + (flat(bo[...]) + flat(bd[...]))
     ).astype(BF)
-    small_step(0)
-
-    c_qa.wait_recv()
-    qa4[...] = added(dwq[:, :, bx, ra], qa_in[...]).astype(BF)
-    c_qa0.start()
-    small_step(1)
+
     c_qa0.wait_recv()
     qa2[...] = added(qa4[:, b0], qa_in2[...]).astype(BF)
-    c_qa1.start()
+    go(c_qa1)
     c_qb.wait_recv()
     qb4[...] = added(dwq[:, :, bx, rb], qb_in[...]).astype(BF)
-    c_qb0.start()
-    small_step(2)
+    go(c_qb0)
     for c in c_up:
         c.wait_recv()
-    wup_ref[...] = (up4[z].astype(F32) + up_in[0].astype(F32) + added(up_in[1], up_in[2])).astype(BF)
     c_dnx.wait_recv()
+    mine = up4[z].astype(F32) + up_in[0].astype(F32) + added(up_in[1], up_in[2])
+    nu = wup_ref.shape[0]
     nd = dn2.shape[1]
+    wup_ref[...] = mine[:nu].astype(BF)
     piece[:nd, :] = added(dn2[bx], dn_in[...]).astype(BF)
+    piece[nd:, :] = mine[nu:].astype(BF)
+
+    def hand_over(source, copies, target):
+        for r in range(4):
+            di, dj = dests[r]
+
+            @pl.when((di != i) | (dj != j))
+            def _():
+                copies[r].start()
+
+            @pl.when((di == i) & (dj == j))
+            def _():
+                target[i % 4] = source[:, pl.ds(pl.multiple_of(dj * w, 128), w)]
+
+    hand_over(piece, c_own, owner_in)
+    small_step(4)
+    sums_ref[...] = sm[5]
     c_wox.wait_recv()
     wo4[...] = added(dwo[:, :, bx], wo_in[...]).astype(BF)
-    c_wo0.start()
+    go(c_wo0)
     c_qb0.wait_recv()
     qb2[...] = added(qb4[:, b0], qb_in2[...]).astype(BF)
-    c_qb1.start()
-    small_step(3)
+    go(c_qb1)
     c_wo0.wait_recv()
     wo2[...] = added(wo4[:, b0], wo_in2[...]).astype(BF)
-    c_wo1.start()
+    go(c_wo1)
     c_qa1.wait_recv()
     c_qb1.wait_recv()
     done = jnp.concatenate([added(qa2[b1], qa_in3[...]), added(qb2[b1], qb_in3[...])], axis=0).astype(BF)
@@ -941,26 +974,14 @@
             q_own[t] = qfin[(3 * j + t) // 4]
 
     c_wo1.wait_recv()
-    piece[nd:, :] = added(wo2[b1], wo_in3[...]).astype(BF)
-    for r in range(4):
-        di, dj = dests[r]
-
-        @pl.when((di != i) | (dj != j))
-        def _():
-            c_own[r].start()
-
-        @pl.when((di == i) & (dj == j))
-        def _():
-            owner_in[i % 4] = piece[:, pl.ds(pl.multiple_of(dj * w, 128), w)]
-
-    small_step(4)
-    sums_ref[...] = sm[5]
+    piece2[...] = added(wo2[b1], wo_in3[...]).astype(BF)
+    hand_over(piece2, c_own2, owner_in2)
 
     c_g[2].wait_recv()
-    near = added(gm[0:own], near_in[...])
     c_y[0].wait_recv()
+    g_ref[lo] = added(gm[lo], near_in[lo]) + y_in[lo].astype(F32)
     c_y[1].wait_recv()
-    g_ref[...] = near + y_in[...].astype(F32)
+    g_ref[hi] = added(gm[hi], near_in[hi]) + y_in[hi].astype(F32)
 
     for t in range(3):
 
@@ -975,13 +996,15 @@
         @pl.when((di != i) | (dj != j))
         def _():
             c_own[r].wait_recv()
-
-    no = wo2.shape[1]
+            c_own2[r].wait_recv()
+
+    nd = piece.shape[0]
+    no = piece2.shape[0]
     for a in range(4):
-        wdn_ref[a * nd : (a + 1) * nd, :] = owner_in[a, :nd]
-        wout_ref[a * no : (a + 1) * no, :] = owner_in[a, nd:]
-
-    for c in c_ctx + c_up + [c_dnx, c_qa, c_qb, c_qa0, c_qb0, c_qa1, c_qb1, c_wox, c_wo0, c_wo1] + c_g + c_y + c_sm:
+        wdn_ref[a * nd : (a + 1) * nd, :] = owner_in[a]
+        wout_ref[a * no : (a + 1) * no, :] = owner_in2[a]
+
+    for c in started:
         c.wait_send()
     for t in range(3):
 
@@ -995,9 +1018,10 @@
         @pl.when((di != i) | (dj != j))
         def _():
             c_own[r].wait_send()
-
-
-def tail_stage(gt, na, gm, ctx, dya, w_qkv, w_out, upk, upo, dn, x, pown, py, ga, sa, bo, bd, small, smallf, cid):
+            c_own2[r].wait_send()
+
+
+def tail_stage(gt, na, gm, ctx, dya, wt, w_out, upk, upo, dn, x, pown, py, ga, sa, bo, bd, small, smallf, cid):
     own, d = x.shape
     tok = na.shape[0]
     w = d // 4
@@ -1006,6 +1030,8 @@
     sds = jax.ShapeDtypeStruct
     big = lambda *s: pltpu.VMEM(s, BF)
     nb = d // 8
+    nu = upk.shape[1]
+    nd = dn[0].shape[1]
     no = w // 8
     r2 = 3 * w // 2
     return pl.pallas_call(
@@ -1017,25 +1043,25 @@
             sds((nb, 3 * w), BF), sds((4 * no, w), BF), sds((16, d), F32),
         ),
         scratch_shapes=[
-            big(3 * w, tok), big(tok, d), big(tok, d), big(w, tok), big(tok, d), big(d, 3 * w), big(d, d),
-            big(4, nb, d), big(4, nb, d), big(4, 2, nb, d),
+            big(3 * w, tok), big(tok, d), big(tok, d), big(w, tok), big(tok, d), big(3 * w, d), big(d, d),
+            big(4, nu, d), big(4, nu, d), big(4, 2, nd, d),
             big(own, d), big(own, d), big(own, d),
-            big(3, w, own), big(4, nb, d), big(3, nb, d), big(nb, d), big(2, nb, d),
+            big(3, w, own), big(4, nu, d), big(3, nu, d), big(nd, d), big(2, nd, d),
             big(2, 2, 2, 3 * w, 128), big(2, 2, r2, 128), big(2, 2, r2, 128), big(2, 2, r2, 128), big(2, 2, r2, 128),
             big(2, r2, 128), big(2, r2, 128), big(2, r2, 128), big(2, r2, 128), big(r2, 128), big(r2, 128),
             big(3, w, 128), big(3, w, 128),
             big(2, 2, 2, no, d), big(2, 2, no, d), big(2, 2, no, d), big(2, no, d), big(2, no, d), big(no, d),
-            big(nb + no, d), big(4, nb + no, w),
+            big(nb, d), big(no, d), big(4, nb, w), big(4, no, w),
             big(own, d), big(own, d), big(own, d), big(own, d),
             pltpu.VMEM((6, 16, d), F32), pltpu.VMEM((5, 16, d), F32),
-            pltpu.SemaphoreType.DMA((18,)), pltpu.SemaphoreType.DMA((40,)), pltpu.SemaphoreType.DMA((40,)),
+            pltpu.SemaphoreType.DMA((16,)), pltpu.SemaphoreType.DMA((40,)), pltpu.SemaphoreType.DMA((40,)),
         ],
         compiler_params=pltpu.CompilerParams(vmem_limit_bytes=VMEM_LIMIT, collective_id=cid, has_side_effects=True),
         cost_estimate=pl.CostEstimate(
             flops=14 * tok * d * w, bytes_accessed=10 * tok * d, transcendentals=0
         ),
         name="tail_stage",
-    )(gt, na, gm, ctx, dya, w_qkv, w_out, upk, upo, *dn, x, pown, py, ga, sa, bo, bd, small, smallf)
+    )(gt, na, gm, ctx, dya, wt, w_out, upk, upo, *dn, x, pown, py, ga, sa, bo, bd, small, smallf)
 
 
 def final_kernel(out_t, g_ref, x_ref, dy_ref, wup, wdn, wq, wout, sums,
@@ -1105,7 +1131,7 @@
     w = d // n
     pos = lax.axis_index("head").astype(jnp.int32).reshape(1)
     lens = lengths[0]
-    (g_mlp, na, dy_all, qt, kt, vt, dot, kn, vn, cos, sin, p_own, p_far, up_keep, up_send, *dn, small,
+    (g_mlp, na, dy_all, qt, kt, vt, dot, kn, vn, cos, sin, p_own, p_far, up_keep, up_send, *dn, wt, small,
      smallf) = head_stage(
         inputs, cotangent, w_up, w_down, w_qkv, w_out, attn_gain, attn_shift, mlp_gain, mlp_shift, b_up, b_qkv, lens, n, 0
     )
@@ -1114,7 +1140,7 @@
     p_y = head_perm(p_far, 2)
     gt, ctx = attention(lens, pos, cos, sin, qt, kt, vt, dot, kn, vn, own, tok // 2, halved=True)
     out_t, g, wup, wdn, wq, wout, sums = tail_stage(
-        gt, na, g_mlp, ctx, dy_all, w_qkv, w_out, up_keep, up_other, dn, inputs, p_own, p_y,
+        gt, na, g_mlp, ctx, dy_all, wt, w_out, up_keep, up_other, dn, inputs, p_own, p_y,
         attn_gain, attn_shift, b_out, b_down, small, smallf, 1
     )
     return tuple(final_stage(out_t, g, inputs, cotangent, wup, wdn, wq, wout, sums))

time: 208 us -> 187 us (0.90); the launches traced: 208 us -> 185 us
  Pallas kernels: 201 us -> 178 us
    pallas_call x1, Pallas kernels: 94.3 us -> 74.7 us  [tail_stage(): pl.pallas_call(tail_kernel, in_specs=[hbm] * 16 + [vm] * 6, out_specs=[vm...]
    pallas_call x1, Pallas kernels: 64.9 us -> 61.5 us  [head_stage(): pl.pallas_call(functools.partial(head_kernel, w // HD), grid=(n,), in_spe...]
  transfers between devices with their start and end apart: 5 -> 5, of which waited for: 0 -> 0; matrix products, arithmetic and copies ran while one was open for 0% -> 0% of each run, Pallas kernels for 17% -> 19%
where the time goes in v6:
time: 187 us; the launch traced here: 185 us
  Pallas kernels  178 us (95%)
  starting transfers between devices  4.59 us (2%)
    pallas_call x1, Pallas kernels, tail_stage(): pl.pallas_call(tail_kernel, in_specs=[hbm] * 16 + [vm] * 6, out_specs=[vm...  74.7 us
    pallas_call x1, Pallas kernels, head_stage(): pl.pallas_call(functools.partial(head_kernel, w // HD), grid=(n,), in_spe...  61.5 us
    pallas_call x1, Pallas kernels, attention(): pl.pallas_call(functools.partial(attn_kernel, nh, tok, blk, chunk // blk,...  35.6 us
    pallas_call x1, Pallas kernels, final_stage(): pl.pallas_call(final_kernel, grid=(steps,), in_specs=[row, row, row, row]...  6.43 us
    ppermute x4, starting transfers between devices, dp_perm(): return lax.ppermute(v, 'dp', [(k, k ^ bit) for k in range(8)])  3.92 us
  transfers between devices with their start and end apart: 5, of which 0 were waited for; matrix products, arithmetic and copies ran while one was open for 0% of the time, Pallas kernels for 19%

profile of v6, /device:TPU:7, one launch (start us, length us, event | category | flops | bytes accessed | tf_op | source)
XLA Modules:
  0.0 184.9 jit_solution(1855217178764954607)
XLA Ops:
  0.6 61.5 %head_stage.1 = (bf16[2048,1024]{1,0:T(8,128)(2,1)}, bf16[2048,1024]{1,0:T(8,128)(2,1)}, bf16[2048,1024]{1,0:T(8,128)(2,1)}, bf16[256,2048]{1,0:T(8,128)(2,1)}, ...) custom-call(bf16[512,1024]{1,0:T(8,128)(2,1)} %x_ref.1, ...), custom_call_target="tpu_custom_call" | custom-call | flops 31138512896 | bytes 33554432 | tf_op jit(solution)/shard_map/head_stage/pallas_call | solution.py:412
  62.2 0.3 collective-permute-start
  62.5 0.7 collective-permute-start.4
  63.1 1.3 collective-permute-start.1
  64.4 2.3 %collective-permute-start.2 = (bf16[2,96,1024]{2,1,0:T(8,128)(2,1)}, bf16[2,96,1024]{2,1,0:T(8,128)(2,1)}, u32[]{:S(2)}, u32[]{:S(2)}) collective-permute-start(bf16[2,96,1024]{2,1,0:T(8,128)(2,1)} %get-tuple-element.63), channel_id=1, source_target_pairs={{0,16},{4,20},{8,24},{12,28},{16,0},{20,4},{24,8},{28,12},{1,17},{... | collective-permute-start | bytes 1179656 | tf_op jit(solution)/shard_map/ppermute | solution.py:1123
  66.8 0.0 collective-permute-start.3
  66.8 35.6 %attention.1 = (bf16[768,2048]{1,0:T(8,128)(2,1)}, bf16[256,2048]{1,0:T(8,128)(2,1)}) custom-call(s32[4]{0:T(128)} %bitcast.3, s32[1]{0:T(128)} %bitcast.1.rel, f32[8,2048]{1,0:T(8,128)} %get-tuple-element.45.cos, f32[8,2048]{1,0:T(8,128)} %get-tuple-element.46.sin, bf16[256,2048]{1,0:T(8,128)(2,1)} %get-tuple-element.47.qt, ...), custom_call_target="tpu_custom_call" | custom-call | flops 10737418240 | bytes 10485760 | tf_op jit(solution)/shard_map/attention/pallas_call | solution.py:623
  102.3 0.0 collective-permute-done.1.dn1_h
  102.4 0.0 copy-start.1
  102.4 0.0 collective-permute-done.2.dn2_h
  102.4 0.0 collective-permute-done.3.dn3_h
  102.4 0.0 collective-permute-done.4.py_h
  102.4 0.0 collective-permute-done.upo_h
  102.4 0.0 copy-start
  102.4 0.7 copy-done.1
  103.1 0.4 copy-done
  103.5 74.7 %tail_stage.1 = (bf16[512,1024]{1,0:T(8,128)(2,1)}, f32[512,1024]{1,0:T(8,128)}, bf16[128,1024]{1,0:T(8,128)(2,1)}, bf16[512,256]{1,0:T(8,128)(2,1)}, bf16[128,7...) custom-call(bf16[768,2048]{1,0:T(8,128)(2,1)} %get-tuple-element.53.gt_h, ...), custom_call_target="tpu_custom_call" | custom-call | flops 7516192768 | bytes 20971520 | tf_op jit(solution)/shard_map/tail_stage/pallas_call | solution.py:1037
  178.3 6.4 %final_stage.1 = (bf16[512,1024]{1,0:T(8,128)(2,1)}, f32[512,1024]{1,0:T(8,128)}, f32[1024]{0:T(1024)}, f32[1024]{0:T(1024)}, f32[1024]{0:T(1024)}, /*index=5*/f...) custom-call(bf16[512,1024]{1,0:T(8,128)(2,1)} %get-tuple-element.69., ...), custom_call_target="tpu_custom_call" | custom-call | tf_op jit(solution)/shard_map/final_stage/pallas_call | solution.py:1098
Async XLA Ops:
  62.2 40.2 %collective-permute-start = (bf16[4,160,1024]{2,1,0:T(8,128)(2,1)}, bf16[4,160,1024]{2,1,0:T(8,128)(2,1)S(1)}, u32[]{:S(2)}, u32[]{:S(2)}) collective-permute-start(bf16[4,160,1024]{2,1,0:T(8,128)(2,1)} %get-tuple-element.60), channel_id=1, source_target_pairs={{0,4},{4,0},{8,12},{12,8},{16,20},{20,16},{24,28},{28,24},{1,5},{5... | collective-permute-start | bytes 3932168 | tf_op jit(solution)/shard_map/ppermute | solution.py:1123
  62.5 39.9 %collective-permute-start.4 = (bf16[512,1024]{1,0:T(8,128)(2,1)}, bf16[512,1024]{1,0:T(8,128)(2,1)}, u32[]{:S(2)}, u32[]{:S(2)}) collective-permute-start(bf16[512,1024]{1,0:T(8,128)(2,1)} %get-tuple-element.66), channel_id=1, source_target_pairs={{0,2},{1,3},{2,0},{3,1},{4,6},{5,7},{6,4},{7,5},{8,10},{9,11},{10,... | collective-permute-start | bytes 3145736 | tf_op jit(solution)/shard_map/ppermute | solution.py:1119
  63.1 39.2 %collective-permute-start.1 = (bf16[2,96,1024]{2,1,0:T(8,128)(2,1)}, bf16[2,96,1024]{2,1,0:T(8,128)(2,1)S(1)}, u32[]{:S(2)}, u32[]{:S(2)}) collective-permute-start(bf16[2,96,1024]{2,1,0:T(8,128)(2,1)} %get-tuple-element.62), channel_id=1, source_target_pairs={{0,8},{4,12},{8,0},{12,4},{16,24},{20,28},{24,16},{28,20},{1,9},{5... | collective-permute-start | bytes 1179656 | tf_op jit(solution)/shard_map/ppermute | solution.py:1123
  64.4 37.9 %collective-permute-start.2 = (bf16[2,96,1024]{2,1,0:T(8,128)(2,1)}, bf16[2,96,1024]{2,1,0:T(8,128)(2,1)}, u32[]{:S(2)}, u32[]{:S(2)}) collective-permute-start(bf16[2,96,1024]{2,1,0:T(8,128)(2,1)} %get-tuple-element.63), channel_id=1, source_target_pairs={{0,16},{4,20},{8,24},{12,28},{16,0},{20,4},{24,8},{28,12},{1,17},{... | collective-permute-start | bytes 1179656 | tf_op jit(solution)/shard_map/ppermute | solution.py:1123
  66.8 35.6 %collective-permute-start.3 = (bf16[2,96,1024]{2,1,0:T(8,128)(2,1)}, bf16[2,96,1024]{2,1,0:T(8,128)(2,1)}, u32[]{:S(2)}, u32[]{:S(2)}) collective-permute-start(bf16[2,96,1024]{2,1,0:T(8,128)(2,1)} %get-tuple-element.64), channel_id=1, source_target_pairs={{0,24},{4,28},{8,16},{12,20},{16,8},{20,12},{24,0},{28,4},{1,25},{... | collective-permute-start | bytes 1179656 | tf_op jit(solution)/shard_map/ppermute | solution.py:1123
  102.4 0.7 copy-start.1
  102.4 1.1 copy-start

commit v7 on v6

--- a/solution.py
+++ b/solution.py
@@ -203,7 +203,7 @@
 def head_kernel(nh, x_hbm, dy_hbm, wu_hbm, wd_hbm, wqkv_hbm, wo_hbm, gain_a, shift_a, gain_m, shift_m, bu, bq, lens,
                 g_out, na_out, dy_out, qt, kt, vt, dot, kn, vn, cos, sin, p_own, p_far, up_keep, up_send, dn0, dn1, dn2, dn3,
                 w_t, small, smallf,
-                xs, dys, wu, wd, wqkv, wt, wo, bias_t, parts, far_in, near_in, dwu, dwd, load, send, recv):
+                xs, dys, wu, wd, wqkv, wt, wo, bias_t, bias_all, bias_u, parts, far_in, near_in, dwu, dwd, load, send, recv):
     step = pl.program_id(0)
     i = lax.axis_index("dp")
     j = lax.axis_index("head")
@@ -238,13 +238,16 @@
     locals_ = [
         pltpu.make_async_copy(x_hbm, xs.at[0], load.at[0]),
         pltpu.make_async_copy(dy_hbm, dys.at[0], load.at[1]),
-        pltpu.make_async_copy(wu_hbm.at[:, pl.ds(j * f, f)], wu, load.at[2]),
-        pltpu.make_async_copy(wd_hbm.at[pl.ds(j * f, f)], wd, load.at[3]),
-        pltpu.make_async_copy(wo_hbm.at[pl.ds(j * w, w)], wo, load.at[4]),
+        pltpu.make_async_copy(wo_hbm.at[pl.ds(j * w, w)], wo, load.at[2]),
     ] + [
-        pltpu.make_async_copy(wqkv_hbm.at[:, pl.ds(k * d + j * w, w)], wqkv.at[:, pl.ds(k * w, w)], load.at[5 + k])
+        pltpu.make_async_copy(wqkv_hbm.at[:, pl.ds(k * d + j * w, w)], wqkv.at[:, pl.ds(k * w, w)], load.at[3 + k])
         for k in range(3)
     ]
+    part = f // 8
+    for k in range(8):
+        there, here = pl.ds(4 * k * part + j * part, part), pl.ds(k * part, part)
+        locals_.append(pltpu.make_async_copy(wu_hbm.at[:, there], wu.at[:, here], load.at[6 + k]))
+        locals_.append(pltpu.make_async_copy(wd_hbm.at[there], wd.at[here], load.at[14 + k]))
 
     @pl.when(step == 0)
     def _():
@@ -266,6 +269,9 @@
             wt[k * w : (k + 1) * w, :] = wqkv[:, k * w : (k + 1) * w].T
             row = flat(bq[pl.ds(pl.multiple_of(k * d + j * w, 256), w)])
             bias_t[k * w : (k + 1) * w, :] = jnp.broadcast_to(row, (128, w)).T
+        bias_all[0:1, :] = flat(bu[...])
+        for k in range(8):
+            bias_u[0:1, k * part : (k + 1) * part] = bias_all[0:1, pl.ds(pl.multiple_of(4 * k * part + j * part, 128), part)]
 
     @pl.when(step == 1)
     def _():
@@ -284,7 +290,7 @@
     nm = (normed * scale + flat(shift_m[...])).astype(BF)
     na = (normed * flat(gain_a[...]) + flat(shift_a[...])).astype(BF)
     na_out[...] = na
-    pre = mm(nm, wu[...]) + flat(bu[pl.ds(pl.multiple_of(j * f, 1024), f)])
+    pre = mm(nm, wu[...]) + bias_u[0:1, :]
     cdf = 0.5 + 0.5 * lax.erf(pre * (0.5**0.5))
     hid = (pre * cdf).astype(BF)
     slope = cdf + pre * (jnp.exp(-0.5 * pre * pre) * 0.3989422804014327)
@@ -442,12 +448,14 @@
             pltpu.VMEM((3 * w, d), BF),
             pltpu.VMEM((w, d), BF),
             pltpu.VMEM((3 * w, 128), F32),
+            pltpu.VMEM((8, 4 * f), F32),
+            pltpu.VMEM((8, f), F32),
             pltpu.VMEM((4, own, d), BF),
             pltpu.VMEM((own, d), BF),
             pltpu.VMEM((own, d), BF),
             pltpu.VMEM((d, f), F32),
             pltpu.VMEM((f, d), F32),
-            pltpu.SemaphoreType.DMA((8,)),
+            pltpu.SemaphoreType.DMA((22,)),
             pltpu.SemaphoreType.DMA((13,)),
             pltpu.SemaphoreType.DMA((13,)),
         ],
@@ -726,7 +734,7 @@
                 gt, na, gm, ctx, dya, wt, wo, upk, upo, dn, xo, pown, py,
                 ctx_in, up4, up_in, dn_in, dn2,
                 dwq, qa_in, qb_in, qa4, qb4, qa_in2, qb_in2, qa2, qb2, qa_in3, qb_in3, qfin, q_own,
-                dwo, wo_in, wo4, wo_in2, wo2, wo_in3, piece, piece2, owner_in, owner_in2,
+                dwo, wo_in, wo4, wo_in2, wo2, wo_in3, fin, piece2, own_in, owner_in2,
                 far_in, near_in, far_sum, y_in, sm, sm_in, load, send, recv):
     i = lax.axis_index("dp")
     j = lax.axis_index("head")
@@ -791,13 +799,13 @@
     ]
     c_y = [remote(far_sum.at[lo], y_in.at[lo], across), remote(far_sum.at[hi], y_in.at[hi], across)]
     c_sm = [remote(sm.at[s], sm_in.at[s], to) for s, to in enumerate((core, across, px, p0, p1))]
+    c_own = [remote(fin.at[j ^ r], own_in.at[j], {"head": j ^ r}) for r in (1, 2, 3)]
     dests = []
-    c_own, c_own2 = [], []
+    c_own2 = []
     for r in range(4):
         di, dj = 2 * j + i // 4, (i % 4) ^ r
         dests.append((di, dj))
         cut = pl.ds(pl.multiple_of(dj * w, 128), w)
-        c_own.append(remote(piece.at[:, cut], owner_in.at[i % 4], {"dp": di, "head": dj}))
         c_own2.append(remote(piece2.at[:, cut], owner_in2.at[i % 4], {"dp": di, "head": dj}))
     c_q = []
     q_dst = []
@@ -863,7 +871,10 @@
         sm[0, 2 + k : 3 + k, pl.ds(pl.multiple_of(j * w, 128), w)] = s_bias[:, k * w : (k + 1) * w]
     sm[0, 5:7, :] = small[0:2, :]
     sm[0, 7:8, :] = small[2:3, :] * 0.25
-    sm[0, pl.ds(8 + j, 1), :] = smallf[0:1, :]
+    part_u = d // 8
+    for b in range(8):
+        at = pl.multiple_of((b % 2) * 4 * part_u + j * part_u, 128)
+        sm[0, 8 + b // 2 : 9 + b // 2, pl.ds(at, part_u)] = smallf[0:1, b * part_u : (b + 1) * part_u]
     go(c_sm[0])
 
     def small_step(s):
@@ -930,23 +941,14 @@
     mine = up4[z].astype(F32) + up_in[0].astype(F32) + added(up_in[1], up_in[2])
     nu = wup_ref.shape[0]
     nd = dn2.shape[1]
-    wup_ref[...] = mine[:nu].astype(BF)
-    piece[:nd, :] = added(dn2[bx], dn_in[...]).astype(BF)
-    piece[nd:, :] = mine[nu:].astype(BF)
-
-    def hand_over(source, copies, target):
-        for r in range(4):
-            di, dj = dests[r]
-
-            @pl.when((di != i) | (dj != j))
-            def _():
-                copies[r].start()
-
-            @pl.when((di == i) & (dj == j))
-            def _():
-                target[i % 4] = source[:, pl.ds(pl.multiple_of(dj * w, 128), w)]
-
-    hand_over(piece, c_own, owner_in)
+    down = added(dn2[bx], dn_in[...])
+    for a in range(4):
+        cut = slice(a * w, (a + 1) * w)
+        fin[a, :nu] = mine[:nu, cut].astype(BF)
+        fin[a, nu : nu + nd] = down[:, cut].astype(BF)
+        fin[a, nu + nd :] = mine[nu:, cut].astype(BF)
+    go(*c_own)
+    own_in[j] = fin[j]
     small_step(4)
     sums_ref[...] = sm[5]
     c_wox.wait_recv()
@@ -975,7 +977,17 @@
 
     c_wo1.wait_recv()
     piece2[...] = added(wo2[b1], wo_in3[...]).astype(BF)
-    hand_over(piece2, c_own2, owner_in2)
+    for r in range(4):
+        di, dj = dests[r]
+
+        @pl.when((di != i) | (dj != j))
+        def _():
+            c_own2[r].start()
+
+        @pl.when((di == i) & (dj == j))
+        def _():
+            owner_in2[i % 4] = piece2[:, pl.ds(pl.multiple_of(dj * w, 128), w)]
+
 
     c_g[2].wait_recv()
     c_y[0].wait_recv()
@@ -995,13 +1007,15 @@
 
         @pl.when((di != i) | (dj != j))
         def _():
-            c_own[r].wait_recv()
             c_own2[r].wait_recv()
 
-    nd = piece.shape[0]
+    for c in c_own:
+        c.wait_recv()
     no = piece2.shape[0]
     for a in range(4):
-        wdn_ref[a * nd : (a + 1) * nd, :] = owner_in[a]
+        wup_ref[:, a * part_u : (a + 1) * part_u] = own_in[a, :nu, :part_u]
+        wup_ref[:, (4 + a) * part_u : (5 + a) * part_u] = own_in[a, :nu, part_u:]
+        wdn_ref[a * nu : (a + 1) * nu, :] = own_in[a, nu:]
         wout_ref[a * no : (a + 1) * no, :] = owner_in2[a]
 
     for c in started:
@@ -1017,7 +1031,6 @@
 
         @pl.when((di != i) | (dj != j))
         def _():
-            c_own[r].wait_send()
             c_own2[r].wait_send()
 
 
@@ -1051,7 +1064,7 @@
             big(2, r2, 128), big(2, r2, 128), big(2, r2, 128), big(2, r2, 128), big(r2, 128), big(r2, 128),
             big(3, w, 128), big(3, w, 128),
             big(2, 2, 2, no, d), big(2, 2, no, d), big(2, 2, no, d), big(2, no, d), big(2, no, d), big(no, d),
-            big(nb, d), big(no, d), big(4, nb, w), big(4, no, w),
+            big(4, 2 * nb, w), big(no, d), big(4, 2 * nb, w), big(4, no, w),
             big(own, d), big(own, d), big(own, d), big(own, d),
             pltpu.VMEM((6, 16, d), F32), pltpu.VMEM((5, 16, d), F32),
             pltpu.SemaphoreType.DMA((16,)), pltpu.SemaphoreType.DMA((40,)), pltpu.SemaphoreType.DMA((40,)),

time: 187 us -> 179 us (0.957)
  Pallas kernels: 178 us -> 171 us
    pallas_call x1, Pallas kernels: 74.7 us -> 67.2 us  [tail_stage(): pl.pallas_call(tail_kernel, in_specs=[hbm] * 16 + [vm] * 6, out_specs=[vm...]
  transfers between devices with their start and end apart: 5 -> 5, of which waited for: 0 -> 0; matrix products, arithmetic and copies ran while one was open for 0% -> 0% of each run, Pallas kernels for 19% -> 20%
where the time goes in v7:
time: 179 us; the launch traced here: 177 us
  Pallas kernels  171 us (96%)
  starting transfers between devices  4.58 us (3%)
    pallas_call x1, Pallas kernels, tail_stage(): pl.pallas_call(tail_kernel, in_specs=[hbm] * 16 + [vm] * 6, out_specs=[vm...  67.2 us
    pallas_call x1, Pallas kernels, head_stage(): pl.pallas_call(functools.partial(head_kernel, w // HD), grid=(n,), in_spe...  61.6 us
    pallas_call x1, Pallas kernels, attention(): pl.pallas_call(functools.partial(attn_kernel, nh, tok, blk, chunk // blk,...  35.6 us
    pallas_call x1, Pallas kernels, final_stage(): pl.pallas_call(final_kernel, grid=(steps,), in_specs=[row, row, row, row]...  6.43 us
    ppermute x4, starting transfers between devices, dp_perm(): return lax.ppermute(v, 'dp', [(k, k ^ bit) for k in range(8)])  3.9 us
  transfers between devices with their start and end apart: 5, of which 0 were waited for; matrix products, arithmetic and copies ran while one was open for 0% of the time, Pallas kernels for 20%

profile of v7, /device:TPU:7, one launch (start us, length us, event | category | flops | bytes accessed | tf_op | source)
XLA Modules:
  0.0 177.4 jit_solution(8720083524514202475)
XLA Ops:
  0.6 61.6 %head_stage.1 = (bf16[2048,1024]{1,0:T(8,128)(2,1)}, bf16[2048,1024]{1,0:T(8,128)(2,1)}, bf16[2048,1024]{1,0:T(8,128)(2,1)}, bf16[256,2048]{1,0:T(8,128)(2,1)}, ...) custom-call(bf16[512,1024]{1,0:T(8,128)(2,1)} %x_ref.1, ...), custom_call_target="tpu_custom_call" | custom-call | flops 31138512896 | bytes 33554432 | tf_op jit(solution)/shard_map/head_stage/pallas_call | solution.py:418
  62.3 0.3 collective-permute-start
  62.6 0.7 collective-permute-start.4
  63.3 1.3 collective-permute-start.1
  64.6 2.3 %collective-permute-start.2 = (bf16[2,96,1024]{2,1,0:T(8,128)(2,1)}, bf16[2,96,1024]{2,1,0:T(8,128)(2,1)}, u32[]{:S(2)}, u32[]{:S(2)}) collective-permute-start(bf16[2,96,1024]{2,1,0:T(8,128)(2,1)} %get-tuple-element.63), channel_id=1, source_target_pairs={{0,16},{4,20},{8,24},{12,28},{16,0},{20,4},{24,8},{28,12},{1,17},{... | collective-permute-start | bytes 1179656 | tf_op jit(solution)/shard_map/ppermute | solution.py:1136
  66.9 0.0 collective-permute-start.3
  66.9 35.6 %attention.1 = (bf16[768,2048]{1,0:T(8,128)(2,1)}, bf16[256,2048]{1,0:T(8,128)(2,1)}) custom-call(s32[4]{0:T(128)} %bitcast.3, s32[1]{0:T(128)} %bitcast.1.rel, f32[8,2048]{1,0:T(8,128)} %get-tuple-element.45.cos, f32[8,2048]{1,0:T(8,128)} %get-tuple-element.46.sin, bf16[256,2048]{1,0:T(8,128)(2,1)} %get-tuple-element.47.qt, ...), custom_call_target="tpu_custom_call" | custom-call | flops 10737418240 | bytes 10485760 | tf_op jit(solution)/shard_map/attention/pallas_call | solution.py:631
  102.5 0.0 collective-permute-done.1.dn1_h
  102.5 0.0 copy-start.1
  102.5 0.0 collective-permute-done.2.dn2_h
  102.5 0.0 collective-permute-done.3.dn3_h
  102.5 0.0 collective-permute-done.4.py_h
  102.5 0.0 collective-permute-done.upo_h
  102.5 0.0 copy-start
  102.6 0.7 copy-done.1
  103.2 0.4 copy-done
  103.7 67.2 %tail_stage.1 = (bf16[512,1024]{1,0:T(8,128)(2,1)}, f32[512,1024]{1,0:T(8,128)}, bf16[128,1024]{1,0:T(8,128)(2,1)}, bf16[512,256]{1,0:T(8,128)(2,1)}, bf16[128,7...) custom-call(bf16[768,2048]{1,0:T(8,128)(2,1)} %get-tuple-element.53.gt_h, ...), custom_call_target="tpu_custom_call" | custom-call | flops 7516192768 | bytes 20971520 | tf_op jit(solution)/shard_map/tail_stage/pallas_call | solution.py:1050
  170.8 6.4 %final_stage.1 = (bf16[512,1024]{1,0:T(8,128)(2,1)}, f32[512,1024]{1,0:T(8,128)}, f32[1024]{0:T(1024)}, f32[1024]{0:T(1024)}, f32[1024]{0:T(1024)}, /*index=5*/f...) custom-call(bf16[512,1024]{1,0:T(8,128)(2,1)} %get-tuple-element.69., ...), custom_call_target="tpu_custom_call" | custom-call | tf_op jit(solution)/shard_map/final_stage/pallas_call | solution.py:1111
Async XLA Ops:
  62.3 40.2 %collective-permute-start = (bf16[4,160,1024]{2,1,0:T(8,128)(2,1)}, bf16[4,160,1024]{2,1,0:T(8,128)(2,1)S(1)}, u32[]{:S(2)}, u32[]{:S(2)}) collective-permute-start(bf16[4,160,1024]{2,1,0:T(8,128)(2,1)} %get-tuple-element.60), channel_id=1, source_target_pairs={{0,4},{4,0},{8,12},{12,8},{16,20},{20,16},{24,28},{28,24},{1,5},{5... | collective-permute-start | bytes 3932168 | tf_op jit(solution)/shard_map/ppermute | solution.py:1136
  62.6 39.9 %collective-permute-start.4 = (bf16[512,1024]{1,0:T(8,128)(2,1)}, bf16[512,1024]{1,0:T(8,128)(2,1)}, u32[]{:S(2)}, u32[]{:S(2)}) collective-permute-start(bf16[512,1024]{1,0:T(8,128)(2,1)} %get-tuple-element.66), channel_id=1, source_target_pairs={{0,2},{1,3},{2,0},{3,1},{4,6},{5,7},{6,4},{7,5},{8,10},{9,11},{10,... | collective-permute-start | bytes 3145736 | tf_op jit(solution)/shard_map/ppermute | solution.py:1132
  63.3 39.2 %collective-permute-start.1 = (bf16[2,96,1024]{2,1,0:T(8,128)(2,1)}, bf16[2,96,1024]{2,1,0:T(8,128)(2,1)S(1)}, u32[]{:S(2)}, u32[]{:S(2)}) collective-permute-start(bf16[2,96,1024]{2,1,0:T(8,128)(2,1)} %get-tuple-element.62), channel_id=1, source_target_pairs={{0,8},{4,12},{8,0},{12,4},{16,24},{20,28},{24,16},{28,20},{1,9},{5... | collective-permute-start | bytes 1179656 | tf_op jit(solution)/shard_map/ppermute | solution.py:1136
  64.6 37.9 %collective-permute-start.2 = (bf16[2,96,1024]{2,1,0:T(8,128)(2,1)}, bf16[2,96,1024]{2,1,0:T(8,128)(2,1)}, u32[]{:S(2)}, u32[]{:S(2)}) collective-permute-start(bf16[2,96,1024]{2,1,0:T(8,128)(2,1)} %get-tuple-element.63), channel_id=1, source_target_pairs={{0,16},{4,20},{8,24},{12,28},{16,0},{20,4},{24,8},{28,12},{1,17},{... | collective-permute-start | bytes 1179656 | tf_op jit(solution)/shard_map/ppermute | solution.py:1136
  66.9 35.6 %collective-permute-start.3 = (bf16[2,96,1024]{2,1,0:T(8,128)(2,1)}, bf16[2,96,1024]{2,1,0:T(8,128)(2,1)}, u32[]{:S(2)}, u32[]{:S(2)}) collective-permute-start(bf16[2,96,1024]{2,1,0:T(8,128)(2,1)} %get-tuple-element.64), channel_id=1, source_target_pairs={{0,24},{4,28},{8,16},{12,20},{16,8},{20,12},{24,0},{28,4},{1,25},{... | collective-permute-start | bytes 1179656 | tf_op jit(solution)/shard_map/ppermute | solution.py:1136
  102.5 0.7 copy-start.1
  102.5 1.1 copy-start
